TPU v7x, 16 devices: a whole 2x2x2 slice. The times are simulated.
16 devices in a mesh: col: 4 (over z, y), row: 4 (over x, core).
Axes of the slice: x: 2, y: 2, z: 2, core: 2. Of those that a mesh axis runs over, the one named last changes fastest.
Arguments:
- vel_u: float32 [41, 384, 2048], P(None, 'row', 'col')
- vel_v: float32 [41, 384, 2048], P(None, 'row', 'col')
- temperature: float32 [41, 384, 2048], P(None, 'row', 'col')
- salinity: float32 [41, 384, 2048], P(None, 'row', 'col')
- sea_level: float32 [384, 2048], P('row', 'col')
- trans_u: float32 [384, 2048], P('row', 'col')
- trans_v: float32 [384, 2048], P('row', 'col')
- bathymetry: float32 [384, 2048], P('row', 'col')
- kmt_levels: int32 [384, 2048], P('row', 'col')
- tide_force: float32 [36, 2], replicated
Outputs:
- output 1: float32 [384, 2048], P('row', 'col')
- output 2: float32 [384, 2048], P('row', 'col')
- output 3: float32 [384, 2048], P('row', 'col')
- output 4: float32 [41, 384, 2048], P(None, 'row', 'col')
- output 5: float32 [41, 384, 2048], P(None, 'row', 'col')
- output 6: float32 [41, 384, 2048], P(None, 'row', 'col')
- output 7: float32 [41, 384, 2048], P(None, 'row', 'col')
All inputs are finite; a program needn't handle non-finite values.
Results may differ from a plain program's by a relative error of at most 0.001.
Values sent between devices are 32-bit elements.
A program may use at most 1 GiB of HBM per device.

v0:
```python
import jax
import jax.numpy as jnp
from jax import lax
from jax.sharding import PartitionSpec as P

GRAVITY = 1.0
GRID_DX = 1.0
TIME_STEP = 4.0
ALPHA_T = 0.02
BETA_S = 0.015
T_REF = 1.0
S_REF = 1.0
VISC_KV = 0.001
DIFF_KT = 0.0005


def level_mask(count, n_levels):
    levels = jnp.arange(n_levels, dtype=jnp.int32)[:, None, None]
    return (levels < count[None]).astype(jnp.float32)


def interface_coef(count, thick, kappa, n_levels):
    levels = jnp.arange(n_levels - 1, dtype=jnp.int32)[:, None, None]
    active = (levels + 1 < count[None]).astype(jnp.float32)
    safe = jnp.where(count > 0, thick, 1.0)
    return active * (TIME_STEP * kappa / (safe * safe))[None]


def column_solve(source, couple):
    edge = jnp.zeros_like(source[:1])
    upper = jnp.concatenate([couple, edge], axis=0)
    lower = jnp.concatenate([edge, couple], axis=0)
    diag = 1.0 + upper + lower

    def forward(carry, slab):
        gain_prev, part_prev = carry
        lower_k, diag_k, upper_k, source_k = slab
        pivot = diag_k - lower_k * gain_prev
        gain = upper_k / pivot
        part = (source_k + lower_k * part_prev) / pivot
        return (gain, part), (gain, part)

    start = (jnp.zeros_like(source[0]), jnp.zeros_like(source[0]))
    _, (gains, parts) = lax.scan(forward, start, (lower, diag, upper, source))

    def backward(below, slab):
        gain, part = slab
        here = part + gain * below
        return here, here

    _, profile = lax.scan(backward, jnp.zeros_like(source[0]), (gains, parts), reverse=True)
    return profile


def geometry(kmt_ext, depth_ext):
    kmt_cell = kmt_ext[1:-1, 1:-1]
    thick_ext = depth_ext / jnp.maximum(kmt_ext, 1).astype(jnp.float32)
    thick_cell = thick_ext[1:-1, 1:-1]
    return {"k_cell": kmt_cell, "k_u": jnp.minimum(kmt_cell, kmt_ext[1:-1, 2:]), "k_v": jnp.minimum(kmt_cell, kmt_ext[2:, 1:-1]), "dz_cell": thick_cell, "dz_u": 0.5 * (thick_cell + thick_ext[1:-1, 2:]), "dz_v": 0.5 * (thick_cell + thick_ext[2:, 1:-1])}


def surface_fields(layout):
    k_faces = jnp.stack([layout["k_u"], layout["k_v"]])
    face_depth = k_faces.astype(jnp.float32) * jnp.stack([layout["dz_u"], layout["dz_v"]])
    face_wet = (k_faces > 0).astype(jnp.float32)
    wet_cell = (layout["k_cell"] > 0).astype(jnp.float32)
    return face_depth, face_wet, wet_cell


def momentum_tend(u_ext, v_ext, p_ext):
    cen_u = 0.5 * (u_ext[:, 1:-1, :-1] + u_ext[:, 1:-1, 1:])
    corner_v = 0.5 * (v_ext[:, :-1, 1:-1] + v_ext[:, :-1, 2:])
    corner_u = 0.5 * (u_ext[:, :-1, 1:-1] + u_ext[:, 1:, 1:-1])
    flux_uu = cen_u * cen_u
    flux_vu = corner_v * corner_u
    tend_u = -(flux_uu[:, :, 1:] - flux_uu[:, :, :-1] + flux_vu[:, 1:, :] - flux_vu[:, :-1, :] + p_ext[:, 1:-1, 2:] - p_ext[:, 1:-1, 1:-1]) / GRID_DX
    cen_v = 0.5 * (v_ext[:, :-1, 1:-1] + v_ext[:, 1:, 1:-1])
    side_u = 0.5 * (u_ext[:, 1:-1, :-1] + u_ext[:, 2:, :-1])
    side_v = 0.5 * (v_ext[:, 1:-1, :-1] + v_ext[:, 1:-1, 1:])
    flux_vv = cen_v * cen_v
    flux_uv = side_u * side_v
    tend_v = -(flux_vv[:, 1:, :] - flux_vv[:, :-1, :] + flux_uv[:, :, 1:] - flux_uv[:, :, :-1] + p_ext[:, 2:, 1:-1] - p_ext[:, 1:-1, 1:-1]) / GRID_DX
    return tend_u, tend_v


def baroclinic_predict(vel_u, vel_v, value_a11, salinity, layout, halo_fn):
    n_levels = vel_u.shape[0]
    mask_c = level_mask(layout["k_cell"], n_levels)
    mask_u = level_mask(layout["k_u"], n_levels)
    mask_v = level_mask(layout["k_v"], n_levels)
    vel_um = vel_u * mask_u
    vel_vm = vel_v * mask_v
    density = mask_c * (BETA_S * (salinity - S_REF) - ALPHA_T * (value_a11 - T_REF))
    pressure = GRAVITY * layout["dz_cell"] * (jnp.cumsum(density, axis=0) - 0.5 * density)
    cell_coef = interface_coef(layout["k_cell"], layout["dz_cell"], DIFF_KT, n_levels)
    temp_mix = column_solve(value_a11 * mask_c, cell_coef)
    salt_mix = column_solve(salinity * mask_c, cell_coef)
    edges = halo_fn(jnp.stack([vel_um, vel_vm, pressure, temp_mix, salt_mix]))
    tend_u, tend_v = momentum_tend(edges[0], edges[1], edges[2])
    u_star = column_solve(mask_u * (vel_um + TIME_STEP * tend_u), interface_coef(layout["k_u"], layout["dz_u"], VISC_KV, n_levels))
    v_star = column_solve(mask_v * (vel_vm + TIME_STEP * tend_v), interface_coef(layout["k_v"], layout["dz_v"], VISC_KV, n_levels))
    forcing = jnp.stack([jnp.sum(layout["dz_u"] * (u_star - vel_um), axis=0), jnp.sum(layout["dz_v"] * (v_star - vel_vm), axis=0)]) / TIME_STEP
    return u_star, v_star, forcing, edges[3:], (mask_c, mask_u, mask_v)


def barotropic(eta_start, trans_start, face_depth, face_wet, wet_cell, forcing, tide_force, halo_fn):
    n_sub = tide_force.shape[0]
    dt_sub = TIME_STEP / n_sub
    weight_norm = 6.0 / (n_sub * (n_sub + 1) * (n_sub + 2))

    def substep(step, carry):
        eta_now, trans_now, trans_avg = carry
        trans_ext = halo_fn(trans_now)
        divergence = (trans_now[0] - trans_ext[0, 1:-1, :-2] + trans_now[1] - trans_ext[1, :-2, 1:-1]) / GRID_DX
        eta_next = wet_cell * (eta_now - dt_sub * divergence)
        eta_ext = halo_fn(eta_next)
        slope = jnp.stack([eta_ext[1:-1, 2:] - eta_next, eta_ext[2:, 1:-1] - eta_next]) / GRID_DX
        tide_now = lax.dynamic_index_in_dim(tide_force, step, 0, keepdims=False)
        trans_next = face_wet * (trans_now + dt_sub * (face_depth * (tide_now[:, None, None] - GRAVITY * slope) + forcing))
        weight = weight_norm * ((step + 1) * (n_sub - step)).astype(jnp.float32)
        return eta_next, trans_next, trans_avg + weight * trans_next

    return lax.fori_loop(0, n_sub, substep, (eta_start, trans_start, jnp.zeros_like(trans_start)))


def correct_velocity(star, dz_face, depth_face, mean_trans, mask):
    safe = jnp.where(depth_face > 0, depth_face, 1.0)
    return mask * (star + ((mean_trans - jnp.sum(dz_face * star, axis=0)) / safe)[None])


def advect_tracers(tracer_ext, flow_ext, mask_c):
    flux_x = flow_ext[0, :, 1:-1, :-1] * (0.5 * (tracer_ext[..., 1:-1, :-1] + tracer_ext[..., 1:-1, 1:]))
    flux_y = flow_ext[1, :, :-1, 1:-1] * (0.5 * (tracer_ext[..., :-1, 1:-1] + tracer_ext[..., 1:, 1:-1]))
    divergence = (flux_x[..., 1:] - flux_x[..., :-1] + flux_y[..., 1:, :] - flux_y[..., :-1, :]) / GRID_DX
    return mask_c * (tracer_ext[..., 1:-1, 1:-1] - TIME_STEP * divergence)


def baroclinic_finish(u_star, v_star, trans_avg, face_depth, layout, tracer_ext, masks, halo_fn):
    mask_c, mask_u, mask_v = masks
    vel_uc = correct_velocity(u_star, layout["dz_u"], face_depth[0], trans_avg[0], mask_u)
    vel_vc = correct_velocity(v_star, layout["dz_v"], face_depth[1], trans_avg[1], mask_v)
    flows = halo_fn(jnp.stack([vel_uc, vel_vc]))
    tracers = advect_tracers(tracer_ext, flows, mask_c)
    return vel_uc, vel_vc, tracers[0], tracers[1]


def ocean_step(vel_u, vel_v, value_a11, salinity, sea_level, trans_u, trans_v, bathymetry, kmt_levels, tide_force, halo_fn):
    layout = geometry(halo_fn(kmt_levels), halo_fn(bathymetry))
    u_star, v_star, forcing, tracer_ext, masks = baroclinic_predict(vel_u, vel_v, value_a11, salinity, layout, halo_fn)
    face_depth, face_wet, wet_cell = surface_fields(layout)
    eta_new, trans_new, trans_avg = barotropic(wet_cell * sea_level, face_wet * jnp.stack([trans_u, trans_v]), face_depth, face_wet, wet_cell, forcing, tide_force, halo_fn)
    vel_uc, vel_vc, temp_new, salt_new = baroclinic_finish(u_star, v_star, trans_avg, face_depth, layout, tracer_ext, masks, halo_fn)
    return eta_new, trans_new[0], trans_new[1], vel_uc, vel_vc, temp_new, salt_new


def solution(mesh):
    n_cols = mesh.shape["col"]
    n_rows = mesh.shape["row"]
    east_perm = [(member, (member - 1) % n_cols) for member in range(n_cols)]
    west_perm = [(member, (member + 1) % n_cols) for member in range(n_cols)]
    north_perm = [(member, member - 1) for member in range(1, n_rows)]
    south_perm = [(member, member + 1) for member in range(n_rows - 1)]

    def halo_swap(field):
        from_east = lax.ppermute(field[..., :1], "col", east_perm)
        from_west = lax.ppermute(field[..., -1:], "col", west_perm)
        wide = jnp.concatenate([from_west, field, from_east], axis=-1)
        from_north = lax.ppermute(wide[..., :1, :], "row", north_perm)
        from_south = lax.ppermute(wide[..., -1:, :], "row", south_perm)
        return jnp.concatenate([from_south, wide, from_north], axis=-2)

    def local_step(vel_u, vel_v, value_a11, salinity, sea_level, trans_u, trans_v, bathymetry, kmt_levels, tide_force):
        return ocean_step(vel_u, vel_v, value_a11, salinity, sea_level, trans_u, trans_v, bathymetry, kmt_levels, tide_force, halo_swap)

    spec_cube = P(None, "row", "col")
    spec_plane = P("row", "col")
    return jax.shard_map(local_step, mesh=mesh, in_specs=(spec_cube, spec_cube, spec_cube, spec_cube, spec_plane, spec_plane, spec_plane, spec_plane, spec_plane, P(None, None)), out_specs=(spec_plane, spec_plane, spec_plane, spec_cube, spec_cube, spec_cube, spec_cube), check_vma=False)
```

profile of v0, /device:TPU:0, one launch (start us, length us, event | category | flops | bytes accessed | tf_op | source)
XLA Modules:
  0.0 1999.7 jit_solution(3946511926419470064)
XLA Ops:
  9.7 11.2 fusion.61
  37.1 6.9 compare_select_fusion.2
  44.0 9.9 fusion.99
  62.5 87.9 %while.156 = (s32[]{:T(128)}, f32[96,512]{1,0:T(8,128)S(1)}, f32[96,512]{1,0:T(8,128)S(1)}, f32[41,96,512]{2,1,0:T(8,128)}, f32[41,96,512]{2,1,0:T(8,128)}, /*in...) while((s32[]{:T(128)}, f32[96,512]{1,0:T(8,128)S(1)}, ...), condition=%wide.region_6.7_spmd.clone, body=%wide.region_5.6_spmd.clone.sunk | while | flops 393219 | bytes 1966711 | solution.py:44
  154.7 76.6 %while.157 = (s32[]{:T(128)}, f32[96,512]{1,0:T(8,128)S(1)}, f32[41,96,512]{2,1,0:T(8,128)}, f32[41,96,512]{2,1,0:T(8,128)}, f32[41,96,512]{2,1,0:T(8,128)}, /*index=5*/s32[]{:T(128)}, s32[]{:T(128)}, s32[]{:T(128)}) while((s32[]{:T(128)}, f32[96,512]{1,0:T(8,128)S(1)}, f32[41,96,512]{2,1,0:T(8,128)}, f32[41,96,512]{2,1,0:T(8,128)}, ...), condition=%wide.region_8.9_spmd.clone, body=%wide.region_7.8_spmd.clone.sunk | while | flops 147460 | bytes 983151 | solution.py:51
  239.9 87.9 %while.154 = (s32[]{:T(128)}, f32[96,512]{1,0:T(8,128)S(1)}, f32[96,512]{1,0:T(8,128)S(1)}, f32[41,96,512]{2,1,0:T(8,128)}, f32[41,96,512]{2,1,0:T(8,128)}, /*in...) while((s32[]{:T(128)}, f32[96,512]{1,0:T(8,128)S(1)}, ...), condition=%wide.region_2.3_spmd.clone, body=%wide.region_1.2_spmd.clone.sunk | while | flops 393219 | bytes 1966711 | solution.py:44
  332.0 76.5 %while.155 = (s32[]{:T(128)}, f32[96,512]{1,0:T(8,128)S(1)}, f32[41,96,512]{2,1,0:T(8,128)}, f32[41,96,512]{2,1,0:T(8,128)}, f32[41,96,512]{2,1,0:T(8,128)}, /*index=5*/s32[]{:T(128)}, s32[]{:T(128)}, s32[]{:T(128)}) while((s32[]{:T(128)}, f32[96,512]{1,0:T(8,128)S(1)}, f32[41,96,512]{2,1,0:T(8,128)}, f32[41,96,512]{2,1,0:T(8,128)}, ...), condition=%wide.region_4.5_spmd.clone, body=%wide.region_3.4_spmd.clone.sunk | while | flops 147460 | bytes 983151 | solution.py:51
  408.5 8.5 bitcast_dynamic-update-slice_fusion.14
  417.0 8.5 bitcast_dynamic-update-slice_fusion.13
  425.5 7.5 bitcast_dynamic-update-slice_fusion.12
  433.0 8.1 constant_dynamic-update-slice_fusion.1
  445.2 16.3 fusion.97
  461.5 6.0 copy.18
  469.4 6.0 copy.19
  476.6 13.8 fusion.98
  490.3 14.0 fusion.100
  506.7 5.4 copy.20
  512.1 5.4 copy.21
  517.5 6.4 pad_maximum_fusion.34
  531.7 31.9 %maximum_bitcast_fusion.1 = (f32[41,98,514]{2,1,0:T(8,128)}, f32[41,98,514]{2,1,0:T(8,128)}, f32[41,98,514]{2,1,0:T(8,128)}) fusion(f32[5,41,1,514]{3,2,1,0:T(1,128)S(1)} %collective-permute-done.17, f32[5,41,1,514]{3,2,1,0:T(1,128)S(1)} %collective-permute-done.16, f32[5,41,96,1]{3,2,1,0:T(8,128)} %copy.21, ...), kind=kLoop, calls=%fused_computation.99 | loop fusion | flops 24783024 | bytes 66088064 | tf_op jit(solution)/shard_map/squeeze | solution.py:99
  563.7 30.8 %fusion.42 = (f32[41,96,513]{2,1,0:T(8,128)}, f32[41,96,513]{2,1,0:T(8,128)}) fusion(f32[41,98,514]{2,1,0:T(8,128)} %get-tuple-element.1206, f32[41,98,514]{2,1,0:T(8,128)} %get-tuple-element.1207), kind=kLoop, calls=%fused_computation.111 | loop fusion | flops 16153344 | bytes 56536704 | tf_op jit(solution)/shard_map/mul | solution.py:74
  594.5 33.1 %fusion.48 = (f32[41,97,512]{2,1,0:T(8,128)}, f32[41,97,512]{2,1,0:T(8,128)}) fusion(f32[41,98,514]{2,1,0:T(8,128)} %get-tuple-element.1206, f32[41,98,514]{2,1,0:T(8,128)} %get-tuple-element.1207), kind=kLoop, calls=%fused_computation.123 | loop fusion | flops 16289792 | bytes 57014272 | tf_op jit(solution)/shard_map/mul | solution.py:75
  627.6 45.2 %fusion.59 = (f32[41,96,512]{2,1,0:T(8,128)}, f32[41,96,512]{2,1,0:T(8,128)}) fusion(f32[41,98,514]{2,1,0:T(8,128)} %get-tuple-element.1208, f32[41,97,512]{2,1,0:T(8,128)} %get-tuple-element.1221, f32[41,96,513]{2,1,0:T(8,128)} %get-tuple-element.1219, f32[41,96,512]{2,1,0:T(8,128)} %param.28, s32[96,512]{1,0:T(8,128)S(1)} %copy-done.8, ...), kind=kLoop, calls=%fused_computation.142 | loop fusion | flops 44335104 | bytes 121307136 | tf_op jit(solution)/shard_map/mul | solution.py:100
  681.3 87.9 %while.158 = (s32[]{:T(128)}, f32[96,512]{1,0:T(8,128)S(1)}, f32[96,512]{1,0:T(8,128)S(1)}, f32[41,96,512]{2,1,0:T(8,128)}, f32[41,96,512]{2,1,0:T(8,128)}, /*in...) while((s32[]{:T(128)}, f32[96,512]{1,0:T(8,128)S(1)}, ...), condition=%wide.region_10.11_spmd.clone, body=%wide.region_9.10_spmd.clone.sunk | while | flops 393219 | bytes 1966711 | solution.py:44
  773.4 76.8 %while.159 = (s32[]{:T(128)}, f32[96,512]{1,0:T(8,128)S(1)}, f32[41,96,512]{2,1,0:T(8,128)}, f32[41,96,512]{2,1,0:T(8,128)}, f32[41,96,512]{2,1,0:T(8,128)}, /*index=5*/s32[]{:T(128)}, s32[]{:T(128)}, s32[]{:T(128)}) while((s32[]{:T(128)}, f32[96,512]{1,0:T(8,128)S(1)}, f32[41,96,512]{2,1,0:T(8,128)}, ...), condition=%wide.region_12.13_spmd.clone, body=%wide.region_11.12_spmd.clone.sunk | while | flops 147460 | bytes 983151 | solution.py:51
  850.2 7.4 multiply_reduce_fusion.1
  866.2 87.9 %while.160 = (s32[]{:T(128)}, f32[96,512]{1,0:T(8,128)S(1)}, f32[96,512]{1,0:T(8,128)S(1)}, f32[41,96,512]{2,1,0:T(8,128)}, f32[41,96,512]{2,1,0:T(8,128)}, /*in...) while((s32[]{:T(128)}, f32[96,512]{1,0:T(8,128)S(1)}, ...), condition=%wide.region_15.16_spmd.clone, body=%wide.region_14.15_spmd.clone.sunk | while | flops 393219 | bytes 1966711 | solution.py:44
  958.5 76.6 %while.161 = (s32[]{:T(128)}, f32[96,512]{1,0:T(8,128)S(1)}, f32[41,96,512]{2,1,0:T(8,128)}, f32[41,96,512]{2,1,0:T(8,128)}, f32[41,96,512]{2,1,0:T(8,128)}, /*index=5*/s32[]{:T(128)}, s32[]{:T(128)}, s32[]{:T(128)}) while((s32[]{:T(128)}, f32[96,512]{1,0:T(8,128)S(1)}, f32[41,96,512]{2,1,0:T(8,128)}, ...), condition=%wide.region_17.18_spmd.clone, body=%wide.region_16.17_spmd.clone.sunk | while | flops 147460 | bytes 983151 | solution.py:51
  1035.2 7.5 multiply_reduce_fusion
  1042.8 805.9 %while.162 = (s32[]{:T(128)}, f32[96,512]{1,0:T(8,128)S(1)}, f32[2,96,512]{2,1,0:T(8,128)S(1)}, f32[2,96,512]{2,1,0:T(8,128)S(1)}, f32[96,512]{1,0:T(8,128)S(1)}...) while((s32[]{:T(128)}, f32[96,512]{1,0:T(8,128)S(1)}, ...), condition=%wide.region_20.21_spmd.clone, body=%wide.region_19.20_spmd.clone.sunk | while | flops 1772563 | bytes 5953611 | solution.py:123
  1050.3 7.7 collective-permute-start.2
  1163.2 5.3 collective-permute-start.2
  1252.5 5.2 collective-permute-start.2
  1341.7 5.2 collective-permute-start.2
  1430.9 5.2 collective-permute-start.2
  1520.2 5.2 collective-permute-start.2
  1609.4 5.2 collective-permute-start.2
  1698.6 5.2 collective-permute-start.2
  1787.9 5.2 collective-permute-start.2
  1849.8 6.8 add_select_fusion
  1856.6 5.3 pad_maximum_fusion.31
  1877.5 10.1 fusion.37
  1892.6 5.6 collective-permute-start.20
  1898.2 24.6 %fusion.29 = f32[2,41,96,513]{3,2,1,0:T(8,128)} fusion(f32[5,41,96,1]{3,2,1,0:T(8,128)} %copy.21, f32[5,41,96,512]{3,2,1,0:T(8,128)} %constant_dynamic-update-slice_fusion, f32[5,41,96,1]{3,2,1,0:T(8,128)} %copy.20, f32[41,96,513]{2,1,0:T(8,128)} %fusion.37), kind=kLoop, calls=%fused_computation.77 | loop fusion | flops 16153344 | bytes 64692096 | tf_op jit(solution)/shard_map/mul | solution.py:132
  1922.9 5.8 fusion.44
  1928.8 20.9 %fusion.31 = f32[2,41,97,512]{3,2,1,0:T(8,128)} fusion(f32[5,41,1,514]{3,2,1,0:T(1,128)} %copy-done.20, f32[5,41,96,1]{3,2,1,0:T(8,128)S(1)} %bitcast.259, f32[5,41,96,512]{3,2,1,0:T(8,128)} %constant_dynamic-update-slice_fusion, f32[5,41,96,1]{3,2,1,0:T(8,128)S(1)} %bitcast.257, f32[5,41,1,514]{3,2,1,0:T(1,128)S(1)} %copy-done.19, f32[41,97,512]{2,1,0:T(8,128)} %fusion.44), kind=kLoop, calls=%fused_computation.81 | loop fusion | flops 32579584 | bytes 65739728 | tf_op jit(solution)/shard_map/mul | solution.py:133
  1949.7 38.8 %fusion.34 = f32[2,41,96,512]{3,2,1,0:T(8,128)} fusion(f32[2,41,97,512]{3,2,1,0:T(8,128)} %fusion.31, f32[2,41,96,513]{3,2,1,0:T(8,128)} %fusion.29, f32[1,41,96,512]{3,2,1,0:T(8,128)} %bitcast.274, f32[1,41,96,512]{3,2,1,0:T(8,128)} %bitcast.277, f32[41,96,512]{2,1,0:T(8,128)} %fusion.60), kind=kLoop, calls=%fused_computation.90 | loop fusion | flops 28213248 | bytes 104792064 | tf_op jit(solution)/shard_map/mul | solution.py:135
  1988.5 11.0 slice_bitcast_fusion
  (1210 shorter events, 1527.3 us)
Async XLA Ops:
  1.5 23.6 %collective-permute-start.6 = (s32[96,1]{1,0:T(8,128)S(1)}, s32[96,1]{1,0:T(8,128)S(1)}, u32[]{:S(2)}, u32[]{:S(2)}) collective-permute-start(s32[96,1]{1,0:T(8,128)S(1)} %get-tuple-element.1249), channel_id=1, source_target_pairs={{0,12},{4,0},{8,4},{12,8},{1,13},{5,1},{9,5},{13,9},{2,14},{6,2},{... | collective-permute-start | bytes 1160 | tf_op jit(solution)/shard_map/ppermute | solution.py:165
  5.8 19.3 collective-permute-start.7
  6.7 22.8 %collective-permute-start.10 = (f32[96,1]{1,0:T(8,128)S(1)}, f32[96,1]{1,0:T(8,128)S(1)}, u32[]{:S(2)}, u32[]{:S(2)}) collective-permute-start(f32[96,1]{1,0:T(8,128)S(1)} %get-tuple-element.1251), channel_id=1, source_target_pairs={{0,12},{4,0},{8,4},{12,8},{1,13},{5,1},{9,5},{13,9},{2,14},{6,2},{... | collective-permute-start | bytes 1160 | tf_op jit(solution)/shard_map/ppermute | solution.py:165
  9.7 19.9 collective-permute-start.9
  25.2 9.6 collective-permute-start.8
  26.5 8.3 collective-permute-start.13
  467.5 39.2 %collective-permute-start.14 = (f32[5,41,96,1]{2,3,1,0:T(1,128)S(1)}, f32[5,41,96,1]{2,3,1,0:T(1,128)S(1)}, u32[]{:S(2)}, u32[]{:S(2)}) collective-permute-start(f32[5,41,96,1]{2,3,1,0:T(1,128)S(1)} %copy.18), channel_id=1, source_target_pairs={{0,4},{4,8},{8,12},{12,0},{1,5},{5,9},{9,13},{13,1},{2,6},{6,10},{... | collective-permute-start | bytes 236168 | tf_op jit(solution)/shard_map/ppermute | solution.py:166
  475.5 36.6 %collective-permute-start.15 = (f32[5,41,96,1]{2,3,1,0:T(1,128)S(1)}, f32[5,41,96,1]{2,3,1,0:T(1,128)S(1)}, u32[]{:S(2)}, u32[]{:S(2)}) collective-permute-start(f32[5,41,96,1]{2,3,1,0:T(1,128)S(1)} %copy.19), channel_id=1, source_target_pairs={{0,12},{4,0},{8,4},{12,8},{1,13},{5,1},{9,5},{13,9},{2,14},{6,2},{... | collective-permute-start | bytes 236168 | tf_op jit(solution)/shard_map/ppermute | solution.py:165
  1044.7 5.5 collective-permute-start.1
  1050.3 8.5 collective-permute-start.2
  1059.4 5.5 collective-permute-start.4
  1069.8 5.9 collective-permute-start.1
  1090.9 5.5 collective-permute-start.1
  1118.9 5.6 collective-permute-start.2
  1141.4 5.7 collective-permute-start.2
  1163.2 6.1 collective-permute-start.2
  1208.1 5.7 collective-permute-start.2
  1230.7 5.7 collective-permute-start.2
  1252.5 6.1 collective-permute-start.2
  1269.4 5.5 collective-permute-start.1
  1297.4 5.8 collective-permute-start.2
  1319.9 5.7 collective-permute-start.2
  1341.7 6.1 collective-permute-start.2
  1358.6 5.5 collective-permute-start.1
  1386.6 5.8 collective-permute-start.2
  1409.1 5.7 collective-permute-start.2
  1430.9 6.1 collective-permute-start.2
  1447.8 5.5 collective-permute-start.1
  1475.9 5.8 collective-permute-start.2
  1498.4 5.7 collective-permute-start.2
  1520.2 6.1 collective-permute-start.2
  1537.1 5.5 collective-permute-start.1
  1565.1 5.8 collective-permute-start.2
  1587.6 5.7 collective-permute-start.2
  1609.4 6.1 collective-permute-start.2
  1626.3 5.5 collective-permute-start.1
  1654.3 5.8 collective-permute-start.2
  1676.8 5.7 collective-permute-start.2
  1698.6 6.1 collective-permute-start.2
  1715.5 5.5 collective-permute-start.1
  1743.6 5.8 collective-permute-start.2
  1766.1 5.7 collective-permute-start.2
  1787.9 6.1 collective-permute-start.2
  1804.8 5.5 collective-permute-start.1
  1832.8 5.8 collective-permute-start.2
  1867.9 6.8 collective-permute-start.18
  1871.1 16.4 collective-permute-start.19
  1892.6 30.3 %collective-permute-start.20 = (f32[2,41,1,514]{3,2,1,0:T(1,128)S(1)}, f32[2,41,1,514]{3,2,1,0:T(1,128)S(1)}, u32[]{:S(2)}, u32[]{:S(2)}) collective-permute-start(f32[2,41,1,514]{3,2,1,0:T(1,128)S(1)} %pad_maximum_fusion.35), channel_id=1, source_target_pairs={{0,1},{1,2},{2,3},{4,5},{5,6},{6,7},{8,9},{9,10},{10,11},{12,13},{... | collective-permute-start | bytes 505784 | tf_op jit(solution)/shard_map/ppermute | solution.py:169
  (227 other events, 2447.8 us)
where the time goes:
time: 2010 us; the launch traced here: 2000 us
  other arithmetic  1050 us (52%)
  starting transfers between devices  405 us (20%)
  waiting for transfers between devices  374 us (19%)
  local copies, waits for them, and re-layouts  162 us (8%)
    dynamic_update_slice x328, other arithmetic, column_solve(): _, (gains, parts) = lax.scan(forward, start, (lower, diag, upper, source))  658 us
    ppermute x40, starting transfers between devices, halo_swap(): from_south = lax.ppermute(wide[..., -1:, :], 'row', south_perm)  194 us
    ppermute x76, waiting for transfers between devices, halo_swap(): from_east = lax.ppermute(field[..., :1], 'col', east_perm)  168 us
    ppermute x76, waiting for transfers between devices, halo_swap(): from_west = lax.ppermute(field[..., -1:], 'col', west_perm)  134 us
    ppermute x76, starting transfers between devices, halo_swap(): from_west = lax.ppermute(field[..., -1:], 'col', west_perm)  91.5 us
    ppermute x76, starting transfers between devices, halo_swap(): from_east = lax.ppermute(field[..., :1], 'col', east_perm)  69.4 us
    another operation x12, local copies, waits for them, and re-layouts  51.3 us
    ppermute x39, starting transfers between devices, halo_swap(): from_north = lax.ppermute(wide[..., :1, :], 'row', north_perm)  50 us
  transfers between devices with their start and end apart: 231, of which 219 were waited for; matrix products, arithmetic and copies ran while one was open for 6% of the time, Pallas kernels for 0%

commit v1 on v0

v1 whole, which is shorter than its diff:
```python
import functools

import jax
import jax.numpy as jnp
from jax import lax
from jax.experimental import pallas as pl
from jax.experimental.pallas import tpu as pltpu
from jax.sharding import PartitionSpec as P

NL = 41
NR = 96
NC = 512
LN = 128
LP = 48
HR = 40
ER = NR + 2 * HR
EC = NC + 128
NB = NR // 8
SUB = 36
DT = 4.0
DTB = DT / SUB
KV = 0.001
KT = 0.0005
F32 = jnp.float32
HT = HR // 8
ET = ER // 8
SLAB, ROW, WIDE, TILE = (NL, 8, NC), (8, NC), (8, EC), (8, LN)
VM = pltpu.VMEM


def only(mask, x):
    return jnp.where(mask, x, jnp.zeros_like(x))


def iota(shape, dim):
    return lax.broadcasted_iota(jnp.int32, shape, dim)


def tile_rows(i):
    return slice(8 * i, 8 * (i + 1))


def from_west(x):
    return pltpu.roll(x, 1, axis=1)


def from_east(x):
    return pltpu.roll(x, x.shape[1] - 1, axis=1)


def lane_to(x, src, dst):
    shift = (dst - src) % LN
    return x if shift == 0 else pltpu.roll(x, shift, axis=1)


def up_row(x, nxt, row):
    return pltpu.roll(jnp.where(row == 0, nxt, x), 7, axis=0)


def down_row(x, prev, row):
    return pltpu.roll(jnp.where(row == 7, prev, x), 1, axis=0)


def couple(count, thick, kappa):
    safe = jnp.where(count > 0, thick, 1.0)
    return DT * kappa / (safe * safe)


def pressure_step(t, s, wet, cum, thick):
    half = only(wet, 0.5 * (0.015 * (s - 1.0) - 0.02 * (t - 1.0)))
    mid = cum + half
    return thick * mid, mid + half


def edge_kernel(u0, u3, v0, v3, t0, s0, kc, hc, uf, vf, ul, vl, tf, sf, kr, hr, pke, pkw, rn, rs):
    b = pl.program_id(0)
    lane = iota(TILE, 1)
    cnt = kc[:]
    thick = hc[:] / jnp.maximum(cnt, 1).astype(F32)
    ae = jnp.zeros(TILE, F32)
    aw = jnp.zeros(TILE, F32)
    cum = jnp.zeros(TILE, F32)
    for k in range(NL):
        p, cum = pressure_step(t0[k], s0[k], k < cnt, cum, thick)
        ae = jnp.where(lane == k, lane_to(u3[k], LN - 1, k), ae)
        ae = jnp.where(lane == NL + k, lane_to(v3[k], LN - 1, NL + k), ae)
        aw = jnp.where(lane == k, lane_to(u0[k], 0, k), aw)
        aw = jnp.where(lane == NL + k, lane_to(v0[k], 0, NL + k), aw)
        aw = jnp.where(lane == 2 * NL + k, lane_to(p, 0, 2 * NL + k), aw)
    pke[:] = ae
    pkw[:] = aw

    @pl.when(b == 0)
    def _():
        count = kr[:]
        dz = hr[:] / jnp.maximum(count, 1).astype(F32)
        acc = jnp.zeros(ROW, F32)
        for k in range(NL):
            p, acc = pressure_step(tf[k], sf[k], k < count, acc, dz)
            rn[0, k : k + 1, :] = ul[k, 7:8, :]
            rn[1, k : k + 1, :] = vl[k, 7:8, :]
            rs[0, k : k + 1, :] = uf[k, 0:1, :]
            rs[1, k : k + 1, :] = vf[k, 0:1, :]
            rs[2, k : k + 1, :] = p[0:1, :]
        for i in range(3):
            rs[i, NL:LP, :] = jnp.zeros((LP - NL, NC), F32)
            if i < 2:
                rn[i, NL:LP, :] = jnp.zeros((LP - NL, NC), F32)


def edges(u, v, t, s, kmt, depth):
    def strip(j):
        return pl.BlockSpec((NL, 8, 128), lambda b: (0, b, j))

    def slab(i):
        return pl.BlockSpec(SLAB, lambda b: (0, i, 0))

    col = pl.BlockSpec(TILE, lambda b: (b, 0))
    row0 = pl.BlockSpec(ROW, lambda b: (0, 0))
    return pl.pallas_call(
        edge_kernel,
        grid=(NB,),
        in_specs=[strip(0), strip(3), strip(0), strip(3), strip(0), strip(0), col, col, slab(0), slab(0), slab(NB - 1), slab(NB - 1), slab(0), slab(0), row0, row0],
        out_specs=[col, col, pl.BlockSpec((2, LP, NC), lambda b: (0, 0, 0)), pl.BlockSpec((3, LP, NC), lambda b: (0, 0, 0))],
        out_shape=[
            jax.ShapeDtypeStruct((NR, LN), F32),
            jax.ShapeDtypeStruct((NR, LN), F32),
            jax.ShapeDtypeStruct((2, LP, NC), F32),
            jax.ShapeDtypeStruct((3, LP, NC), F32),
        ],
        compiler_params=pltpu.CompilerParams(dimension_semantics=("arbitrary",)),
        cost_estimate=pl.CostEstimate(flops=10**7, bytes_accessed=16 * 10**6, transcendentals=0),
        name="edges",
    )(u, u, v, v, t, s, kmt, depth, u, v, u, v, t, s, kmt, depth)


def tracer_kernel(t, s, kc, hc, tm, sm, pr, pke, pkw, rn, rs, gains):
    b = pl.program_id(0)
    lane = iota(TILE, 1)
    cnt = kc[:]
    thick = hc[:] / jnp.maximum(cnt, 1).astype(F32)
    c = couple(cnt, thick, KT)
    zero = jnp.zeros(ROW, F32)
    cum = lower = pt = ps = zero
    keep = zero
    for k in range(NL):
        wet = k < cnt
        tk, sk = t[k], s[k]
        p, cum = pressure_step(tk, sk, wet, cum, thick)
        pr[k] = p
        upper = jnp.where(k + 1 < cnt, c, 0.0) if k + 1 < NL else zero
        top = 1.0 + lower * keep if k else jnp.ones_like(zero)
        inv = 1.0 / (top + upper)
        keep = top * inv
        gains[k] = upper * inv
        pt = (jnp.where(wet, tk, 0.0) + lower * pt) * inv
        ps = (jnp.where(wet, sk, 0.0) + lower * ps) * inv
        tm[k] = pt
        sm[k] = ps
        lower = upper
    ae = jnp.zeros(TILE, F32)
    aw = jnp.zeros(TILE, F32)
    bt = bs = zero
    for k in reversed(range(NL)):
        gain = gains[k]
        bt = tm[k] + gain * bt
        bs = sm[k] + gain * bs
        tm[k] = bt
        sm[k] = bs
        for x, base in ((bt, NL), (bs, 2 * NL)):
            ae = jnp.where(lane == base + k, lane_to(x[:, NC - LN :], LN - 1, base + k), ae)
            aw = jnp.where(lane == base + k, lane_to(x[:, :LN], 0, base + k), aw)
    pke[:] = ae
    pkw[:] = aw

    @pl.when(b == 0)
    def _():
        for k in range(NL):
            rs[0, k : k + 1, :] = tm[k, 0:1, :]
            rs[1, k : k + 1, :] = sm[k, 0:1, :]
        for i in range(2):
            rs[i, NL:LP, :] = jnp.zeros((LP - NL, NC), F32)

    @pl.when(b == NB - 1)
    def _():
        for k in range(NL):
            rn[0, k : k + 1, :] = tm[k, 7:8, :]
            rn[1, k : k + 1, :] = sm[k, 7:8, :]
        for i in range(2):
            rn[i, NL:LP, :] = jnp.zeros((LP - NL, NC), F32)


def tracers(t, s, kmt, depth):
    cube = pl.BlockSpec(SLAB, lambda b: (0, b, 0))
    plane = pl.BlockSpec(ROW, lambda b: (b, 0))
    col = pl.BlockSpec(TILE, lambda b: (b, 0))
    rows = pl.BlockSpec((2, LP, NC), lambda b: (0, 0, 0))
    big = jax.ShapeDtypeStruct((NL, NR, NC), F32)
    return pl.pallas_call(
        tracer_kernel,
        grid=(NB,),
        in_specs=[cube, cube, plane, plane],
        out_specs=[cube, cube, cube, col, col, rows, rows],
        out_shape=[big, big, big] + [jax.ShapeDtypeStruct((NR, LN), F32)] * 2 + [jax.ShapeDtypeStruct((2, LP, NC), F32)] * 2,
        scratch_shapes=[VM(SLAB, F32)],
        compiler_params=pltpu.CompilerParams(dimension_semantics=("arbitrary",)),
        cost_estimate=pl.CostEstimate(flops=10**8, bytes_accessed=40 * 10**6, transcendentals=0),
        name="tracers",
    )(t, s, kmt, depth)


def geometry_kernel(pl5, ku, kv, du, dv):
    row = iota(WIDE, 0)
    for i in range(ET):
        lo = tile_rows(i)
        hi = slice(8 * (i + 1), 8 * i + 16) if i + 1 < ET else lo
        k, h = pl5[0, lo, :], pl5[1, lo, :]
        dz = h / jnp.maximum(k, 1.0)
        kn, hn = pl5[0, hi, :], pl5[1, hi, :]
        dzn = hn / jnp.maximum(kn, 1.0)
        ku[lo, :] = jnp.minimum(k, from_east(k))
        kv[lo, :] = jnp.minimum(k, up_row(k, kn, row))
        du[lo, :] = 0.5 * (dz + from_east(dz))
        dv[lo, :] = 0.5 * (dz + up_row(dz, dzn, row))


def geometry(planes):
    return pl.pallas_call(geometry_kernel, out_shape=[jax.ShapeDtypeStruct((ER, EC), F32)] * 4, name="geometry")(planes)


def solve_pair(src_a, src_b, ca, cb, na, nb, out_a, out_b, gain_a, gain_b):
    zero = jnp.zeros(ROW, F32)
    la = lb = pa = pb = wa = wb = zero
    for k in range(NL):
        ua = jnp.where(k + 1 < na, ca, 0.0) if k + 1 < NL else zero
        ub = jnp.where(k + 1 < nb, cb, 0.0) if k + 1 < NL else zero
        ta = 1.0 + la * wa if k else jnp.ones_like(zero)
        tb = 1.0 + lb * wb if k else jnp.ones_like(zero)
        ia = 1.0 / (ta + ua)
        ib = 1.0 / (tb + ub)
        wa, wb = ta * ia, tb * ib
        gain_a[k] = ua * ia
        gain_b[k] = ub * ib
        pa = (src_a[k] + la * pa) * ia
        pb = (src_b[k] + lb * pb) * ib
        src_a[k] = pa
        src_b[k] = pb
        la, lb = ua, ub
    xa = xb = sa = sb = zero
    for k in reversed(range(NL)):
        xa = src_a[k] + gain_a[k] * xa
        xb = src_b[k] + gain_b[k] * xb
        out_a[k] = xa
        out_b[k] = xb
        sa += xa
        sb += xb
    return sa, sb


def momentum_kernel(
    u, un, v, vn, p, pn, ku, kun, kv, kvn, du, dv, kus, kvs, rw, rwn, re, rnorth, rsouth, rown, corner,
    us, vs, fx, fy, su, sv, pke, vrow,
    cc, hh, srcu, srcv, gu, gv,
):
    b = pl.program_id(0)
    last = b == NB - 1
    row = iota(ROW, 0)
    rowx = iota(WIDE, 0)
    lane = iota(TILE, 1)

    @pl.when(b == 0)
    def _():
        lev = iota((LP, NC), 0).astype(F32)
        lev1 = iota((LP, LN), 0)
        ks, kw = kus[7:8, :NC], kvs[7:8, :NC]
        s_u = only(lev < ks, rsouth[0])
        s_v = only(lev < kw, rsouth[1])
        pick = only(iota((LP, LN), 1) == lev1 + NL, corner[7:8, :])
        edge = jnp.sum(pick, axis=1, keepdims=True)
        edge = only(lev[:, :1] < kvs[7:8, NC : NC + 1], edge)
        s_ve = jnp.where(iota((LP, NC), 1) == NC - 1, edge, from_east(s_v))
        u_0 = only(lev < ku[0:1, :NC], rown[0])
        v_0 = only(lev < kv[0:1, :NC], rown[1])
        c_s = 0.25 * ((s_v + s_ve) * (s_u + u_0))
        h_s = s_v + v_0
        h_s = 0.25 * (h_s * h_s) + rown[2]
        for k in range(NL):
            cc[k, 7:8, :] = c_s[k : k + 1, :]
            hh[k, 7:8, :] = h_s[k : k + 1, :]

    kx, ky = ku[:], kv[:]
    kxn, kyn = kun[:], kvn[:, :NC]
    rwv, rwnv, rev = rw[:], rwn[:], re[:]
    zx = jnp.zeros(ROW, F32)
    ax, ay = zx, zx
    for k in range(NL):
        hu = jnp.where(lane == 0, lane_to(rev, k, 0), lane_to(rwv, k, LN - 1))
        hv = jnp.where(lane == 0, lane_to(rev, NL + k, 0), lane_to(rwv, NL + k, LN - 1))
        hp = lane_to(rev, 2 * NL + k, 0)
        hn = lane_to(rwnv, k, LN - 1)
        um = only(k < kx, jnp.concatenate([u[k], hu], axis=1))
        vm = only(k < ky, jnp.concatenate([v[k], hv], axis=1))
        pe = jnp.concatenate([p[k], hp], axis=1)
        nu = jnp.where(last, rnorth[0, k : k + 1, :], un[k])
        nv = jnp.where(last, rnorth[1, k : k + 1, :], vn[k])
        np_ = jnp.where(last, rnorth[2, k : k + 1, :], pn[k])
        nu = only(k < kxn, jnp.concatenate([nu, hn], axis=1))
        nv = only(k < kyn, nv)
        u_n = up_row(um, nu, rowx)
        c = 0.25 * ((vm + from_east(vm)) * (um + u_n))
        g = from_west(um) + um
        g = 0.25 * (g * g) + pe
        ge = from_east(g)[:, :NC]
        v5 = vm[:, :NC]
        h = v5 + up_row(v5, nv, row)
        h = 0.25 * (h * h) + up_row(pe[:, :NC], np_, row)
        cw = from_west(c)[:, :NC]
        c5 = c[:, :NC]
        tu = (ge - g[:, :NC]) + (c5 - down_row(c5, cc[k], row))
        tv = (h - down_row(h, hh[k], row)) + (c5 - cw)
        tu = only(k < kx[:, :NC], tu)
        tv = only(k < ky[:, :NC], tv)
        ax += tu
        ay += tv
        srcu[k] = um[:, :NC] - DT * tu
        srcv[k] = v5 - DT * tv
        cc[k] = c5
        hh[k] = h
    dzu, dzv = du[:, :NC], dv[:, :NC]
    kx, ky = kx[:, :NC], ky[:, :NC]
    fx[:] = -dzu * ax
    fy[:] = -dzv * ay
    sa, sb = solve_pair(srcu, srcv, couple(kx, dzu, KV), couple(ky, dzv, KV), kx, ky, us, vs, gu, gv)
    sa, sb = dzu * sa, dzv * sb
    su[:] = sa
    sv[:] = sb
    ae = jnp.zeros(TILE, F32)
    for k in range(NL):
        ae = jnp.where(lane == k, lane_to(us[k, :, NC - LN :], LN - 1, k), ae)
    pke[:] = jnp.where(lane == 3 * NL, lane_to(sa[:, NC - LN :], LN - 1, 3 * NL), ae)

    @pl.when(last)
    def _():
        for k in range(NL):
            vrow[k : k + 1, :] = vs[k, 7:8, :]
        vrow[NL : NL + 1, :] = sb[7:8, :]
        vrow[NL + 1 : LP, :] = jnp.zeros((LP - NL - 1, NC), F32)


def momentum(u, v, p, geo, rw, re, rnorth, rsouth, rown, corner):
    ku, kv, du, dv = geo
    cube = pl.BlockSpec(SLAB, lambda b: (0, b, 0))
    cubn = pl.BlockSpec(SLAB, lambda b: (0, jnp.minimum(b + 1, NB - 1), 0))
    wide = pl.BlockSpec(WIDE, lambda b: (HT + b, 0))
    widn = pl.BlockSpec(WIDE, lambda b: (HT + 1 + b, 0))
    wids = pl.BlockSpec(WIDE, lambda b: (HT - 1, 0))
    plane = pl.BlockSpec(ROW, lambda b: (b, 0))
    col = pl.BlockSpec(TILE, lambda b: (b, 0))
    coln = pl.BlockSpec(TILE, lambda b: (b + 1, 0))
    big = jax.ShapeDtypeStruct((NL, NR, NC), F32)
    flat = jax.ShapeDtypeStruct((NR, NC), F32)

    def rows(n):
        return pl.BlockSpec((n, LP, NC), lambda b: (0, 0, 0))

    return pl.pallas_call(
        momentum_kernel,
        grid=(NB,),
        in_specs=[cube, cubn, cube, cubn, cube, cubn, wide, widn, wide, widn, wide, wide, wids, wids, col, coln, col, rows(3), rows(2), rows(3), pl.BlockSpec(TILE, lambda b: (0, 0))],
        out_specs=[cube, cube, plane, plane, plane, plane, col, pl.BlockSpec((LP, NC), lambda b: (0, 0))],
        out_shape=[big, big, flat, flat, flat, flat, jax.ShapeDtypeStruct((NR, LN), F32), jax.ShapeDtypeStruct((LP, NC), F32)],
        scratch_shapes=[VM(SLAB, F32)] * 6,
        compiler_params=pltpu.CompilerParams(dimension_semantics=("arbitrary",)),
        cost_estimate=pl.CostEstimate(flops=2 * 10**8, bytes_accessed=64 * 10**6, transcendentals=0),
        name="momentum",
    )(u, u, v, v, p, p, ku, ku, kv, kv, du, dv, ku, kv, rw, rw, re, rnorth, rsouth, rown, corner)


def subcycle_kernel(planes, ku, kv, du, dv, force, tide, eta_o, u_o, v_o, ub_o, vb_o, eta, tu, tv, cu, cv, fu, fv, ub, vb):
    nt = ET
    row = iota(WIDE, 0)
    zero = jnp.zeros(WIDE, F32)
    for i in range(nt):
        sl = tile_rows(i)
        kx, ky = ku[sl, :], kv[sl, :]
        eta[sl, :] = only(planes[0, sl, :] > 0, planes[2, sl, :])
        tu[sl, :] = only(kx > 0, planes[3, sl, :])
        tv[sl, :] = only(ky > 0, planes[4, sl, :])
        cu[sl, :] = DTB * (kx * du[sl, :])
        cv[sl, :] = DTB * (ky * dv[sl, :])
        fu[sl, :] = only(kx > 0, DTB * force[0, sl, :])
        fv[sl, :] = only(ky > 0, DTB * force[1, sl, :])
        ub[sl, :] = zero
        vb[sl, :] = zero
    norm = 6.0 / (SUB * (SUB + 1) * (SUB + 2))

    def stage(first, last, lo, hi):
        def step(n, _):
            tx, ty = tide[n, 0], tide[n, 1]
            w = norm * ((n + 1) * (SUB - n)).astype(F32)
            prev_eta = None
            vsouth = tv[8 * lo - 8 : 8 * lo, :] if lo else zero
            for i in range(lo, hi):
                sl = tile_rows(i)
                un, vn = tu[sl, :], tv[sl, :]
                e = eta[sl, :] - DTB * ((un - from_west(un)) + (vn - down_row(vn, vsouth, row)))
                eta[sl, :] = e
                un = un + (cu[sl, :] * (tx - (from_east(e) - e)) + fu[sl, :])
                tu[sl, :] = un
                if lo_bar <= i < hi_bar:
                    ub[sl, :] = ub[sl, :] + w * un
                if i > lo:
                    finish(i - 1, prev_eta, e, vsouth, ty, w)
                prev_eta, vsouth = e, vn
            finish(hi - 1, prev_eta, prev_eta, vsouth, ty, w)
            return 0

        lax.fori_loop(first, last, step, 0)

    lo_bar, hi_bar = HT - 1, HT + NB

    def finish(i, e, north, vold, ty, w):
        sl = tile_rows(i)
        x = vold + (cv[sl, :] * (ty - (up_row(e, north, row) - e)) + fv[sl, :])
        tv[sl, :] = x
        if lo_bar <= i < hi_bar:
            vb[sl, :] = vb[sl, :] + w * x

    for s in range(0, SUB, 8):
        stage(s, min(s + 8, SUB), s // 8, nt - s // 8)
    eta_o[:] = eta[HR : HR + NR, :NC]
    u_o[:] = tu[HR : HR + NR, :NC]
    v_o[:] = tv[HR : HR + NR, :NC]
    ub_o[:] = ub[HR - 8 : HR + NR, :]
    vb_o[:] = vb[HR - 8 : HR + NR, :]


def subcycles(planes, geo, force, tide):
    flat = jax.ShapeDtypeStruct((NR, NC), F32)
    bar = jax.ShapeDtypeStruct((NR + 8, EC), F32)
    vm = pl.BlockSpec(memory_space=VM)
    return pl.pallas_call(
        subcycle_kernel,
        in_specs=[vm] * 6 + [pl.BlockSpec(memory_space=pltpu.SMEM)],
        out_specs=[vm] * 5,
        out_shape=[flat, flat, flat, bar, bar],
        scratch_shapes=[VM((ER, EC), F32)] * 9,
        cost_estimate=pl.CostEstimate(flops=10**8, bytes_accessed=10**6, transcendentals=0),
        name="subcycles",
    )(planes, *geo, force, tide)


def finish_kernel(
    us, vs, t, tn, s, sn, kc, ku, kv, du, dv, ub, vb, su, sv, kvs, dvs, vbs, rw, re, rnorth, rsouth, rown,
    uo, vo, to, so, ct, cs,
):
    b = pl.program_id(0)
    last = b == NB - 1
    row = iota(ROW, 0)
    lane = iota(TILE, 1)

    def correction(mean, total, k, dz):
        deep = k * dz
        return (mean - total) / jnp.where(deep > 0, deep, 1.0)

    @pl.when(b == 0)
    def _():
        lev = iota((LP, NC), 0).astype(F32)
        kx = kvs[7:8, :NC]
        cor = correction(vbs[7:8, :NC], rsouth[0, NL : NL + 1, :], kx, dvs[7:8, :NC])
        vel = 0.5 * DT * only(lev < kx, rsouth[0] + cor)
        ft = vel * (rsouth[1] + rown[0])
        fs = vel * (rsouth[2] + rown[1])
        for k in range(NL):
            ct[k, 7:8, :] = ft[k : k + 1, :]
            cs[k, 7:8, :] = fs[k : k + 1, :]

    kx, ky, cnt = ku[:], kv[:, :NC], kc[:]
    rwv, rev = rw[:], re[:]
    tot = jnp.concatenate([su[:], lane_to(rwv, 3 * NL, LN - 1)], axis=1)
    cx = correction(ub[:], tot, kx, du[:])
    cy = correction(vb[:, :NC], sv[:], ky, dv[:, :NC])
    for k in range(NL):
        ue = jnp.concatenate([us[k], lane_to(rwv, k, LN - 1)], axis=1)
        ue = only(k < kx, ue + cx)
        uo[k] = ue[:, :NC]
        ve = only(k < ky, vs[k] + cy)
        vo[k] = ve
        hx, hy = (0.5 * DT) * ue, (0.5 * DT) * ve
        wet = k < cnt
        for i, (x, nxt, out, carry) in enumerate(((t, tn, to, ct), (s, sn, so, cs))):
            base = NL * (i + 1) + k
            halo = jnp.where(lane == 0, lane_to(rev, base, 0), lane_to(rwv, base, LN - 1))
            own = x[k]
            xe = jnp.concatenate([own, halo], axis=1)
            f = hx * (xe + from_east(xe))
            north = jnp.where(last, rnorth[i, k : k + 1, :], nxt[k])
            fy = hy * (own + up_row(own, north, row))
            div = (f - from_west(f))[:, :NC] + (fy - down_row(fy, carry[k], row))
            carry[k] = fy
            out[k] = only(wet, own - div)


def finish(us, vs, tm, sm, kmt, geo, ub, vb, su, sv, rw, re, rnorth, rsouth, rown):
    ku, kv, du, dv = geo
    cube = pl.BlockSpec(SLAB, lambda b: (0, b, 0))
    cubn = pl.BlockSpec(SLAB, lambda b: (0, jnp.minimum(b + 1, NB - 1), 0))
    wide = pl.BlockSpec(WIDE, lambda b: (HT + b, 0))
    wids = pl.BlockSpec(WIDE, lambda b: (HT - 1, 0))
    bar = pl.BlockSpec(WIDE, lambda b: (b + 1, 0))
    bars = pl.BlockSpec(WIDE, lambda b: (0, 0))
    plane = pl.BlockSpec(ROW, lambda b: (b, 0))
    col = pl.BlockSpec(TILE, lambda b: (b, 0))
    big = jax.ShapeDtypeStruct((NL, NR, NC), F32)

    def rows(n):
        return pl.BlockSpec((n, LP, NC), lambda b: (0, 0, 0))

    return pl.pallas_call(
        finish_kernel,
        grid=(NB,),
        in_specs=[cube, cube, cube, cubn, cube, cubn, plane, wide, wide, wide, wide, bar, bar, plane, plane, wids, wids, bars, col, col, rows(2), rows(3), rows(2)],
        out_specs=[cube] * 4,
        out_shape=[big] * 4,
        scratch_shapes=[VM(SLAB, F32)] * 2,
        compiler_params=pltpu.CompilerParams(dimension_semantics=("arbitrary",)),
        cost_estimate=pl.CostEstimate(flops=10**8, bytes_accessed=80 * 10**6, transcendentals=0),
        name="finish",
    )(us, vs, tm, tm, sm, sm, kmt, ku, kv, du, dv, ub, vb, su, sv, kv, dv, vb, rw, re, rnorth, rsouth, rown)


def solution(mesh):
    n_cols, n_rows = mesh.shape["col"], mesh.shape["row"]

    def send(x, drow, dcol):
        pairs = []
        for c in range(n_cols):
            for r in range(n_rows):
                if 0 <= r + drow < n_rows:
                    pairs.append((c * n_rows + r, ((c + dcol) % n_cols) * n_rows + r + drow))
        return lax.ppermute(x, ("col", "row"), pairs)

    def widen(x):
        lane = lax.broadcasted_iota(jnp.int32, (1, 1, 128), 2)
        east, west = send(x[..., :LN], 0, -1), send(x[..., NC - LN :], 0, 1)
        wide = jnp.concatenate([x, jnp.where(lane < 64, east, west)], axis=-1)
        north, south = send(wide[:, :HR], -1, 0), send(wide[:, NR - HR :], 1, 0)
        return jnp.concatenate([south, wide, north], axis=1)

    def local_step(u, v, t, s, eta, tu, tv, depth, kmt, tide):
        pke, pkw, prn, prs = edges(u, v, t, s, kmt, depth)
        planes = widen(jnp.stack([kmt.astype(F32), depth, eta, tu, tv]))
        rw, re = send(pke, 0, 1), send(pkw, 0, -1)
        rsouth, rnorth = send(prn, 1, 0), send(prs, -1, 0)
        nw = send(pke[:8], -1, 1)
        se = send(pkw[NR - 8 :], 1, -1)
        geo = geometry(planes)
        tm, sm, pr, tke, tkw, trn, trs = tracers(t, s, kmt, depth)
        rw = jnp.concatenate([rw, nw], axis=0)
        us, vs, fx, fy, su, sv, uke, vrow = momentum(u, v, pr, geo, rw, re, rnorth, rsouth, prs, se)
        force = widen(jnp.stack([fx, fy]))
        fw, fe = send(tke + uke, 0, 1), send(tkw, 0, -1)
        fsouth, fnorth = send(jnp.concatenate([vrow[None], trn]), 1, 0), send(trs, -1, 0)
        eta_n, u_n, v_n, ub, vb = subcycles(planes, geo, force, tide)
        uo, vo, to, so = finish(us, vs, tm, sm, kmt, geo, ub, vb, su, sv, fw, fe, fnorth, fsouth, trs)
        return eta_n, u_n, v_n, uo, vo, to, so

    cube, plane = P(None, "row", "col"), P("row", "col")
    return jax.shard_map(
        local_step,
        mesh=mesh,
        in_specs=(cube,) * 4 + (plane,) * 5 + (P(None, None),),
        out_specs=(plane,) * 3 + (cube,) * 4,
        check_vma=False,
    )
```

time: 2010 us -> 328 us (0.16)
  other arithmetic: 1050 us -> 8.89 us
  starting transfers between devices: 405 us -> 35.1 us
  waiting for transfers between devices: 374 us -> 16.9 us
  Pallas kernels: 0 us -> 257 us
  local copies, waits for them, and re-layouts: 162 us -> 7.34 us
    dynamic_update_slice x328 -> x0, other arithmetic: 658 us -> none  [column_solve(): _, (gains, parts) = lax.scan(forward, start, (lower, diag, upper, source))]
    ppermute x231 -> x18, starting transfers between devices: 405 us -> 35.1 us  [send(): return lax.ppermute(x, ('col', 'row'), pairs)]
    ppermute x231 -> x18, waiting for transfers between devices: 374 us -> 16.9 us  [send(): return lax.ppermute(x, ('col', 'row'), pairs)]
    pallas_call x0 -> x6, Pallas kernels: none -> 257 us  [the longest x1 122 us: finish(): pl.pallas_call(finish_kernel, grid=(NB,), in_specs=[cube, cube, cube, cub...]
    mul x50 -> x0, other arithmetic: 242 us -> none  [the longest x1 45.2 us: baroclinic_predict(): mask_u * (vel_um + TIME_STEP * tend_u)]
    another operation x13 -> x1, local copies, waits for them, and re-layouts: 55.4 us -> 0.94 us  [local_step(): planes = widen(jnp.stack([kmt.astype(F32), depth, eta, tu, tv]))]
    slice x79 -> x3, local copies, waits for them, and re-layouts: 42.1 us -> 1.42 us  [the longest x1 0.69 us: local_step(): se = send(pkw[NR - 8:], 1, -1)]
    concatenate x77 -> x4, other arithmetic: 45.4 us -> 5.09 us  [the longest x2 3.56 us: widen(): return jnp.concatenate([south, wide, north], axis=1)]
  transfers between devices with their start and end apart: 231 -> 18, of which waited for: 219 -> 4; matrix products, arithmetic and copies ran while one was open for 6% -> 2% of each run, Pallas kernels for 0% -> 20%
where the time goes in v1:
time: 328 us; the launch traced here: 327 us
  Pallas kernels  257 us (78%)
  starting transfers between devices  35.1 us (11%)
  waiting for transfers between devices  16.9 us (5%)
  other arithmetic  8.89 us (3%)
  local copies, waits for them, and re-layouts  7.34 us (2%)
    pallas_call x1, Pallas kernels, finish(): pl.pallas_call(finish_kernel, grid=(NB,), in_specs=[cube, cube, cube, cub...  122 us
    pallas_call x1, Pallas kernels, momentum(): pl.pallas_call(momentum_kernel, grid=(NB,), in_specs=[cube, cubn, cube, c...  71.3 us
    ppermute x18, starting transfers between devices, send(): return lax.ppermute(x, ('col', 'row'), pairs)  35.1 us
    pallas_call x1, Pallas kernels, subcycles(): pl.pallas_call(subcycle_kernel, in_specs=[vm] * 6 + [pl.BlockSpec(memory_...  26.8 us
    pallas_call x1, Pallas kernels, tracers(): pl.pallas_call(tracer_kernel, grid=(NB,), in_specs=[cube, cube, plane, pl...  21.3 us
    ppermute x18, waiting for transfers between devices, send(): return lax.ppermute(x, ('col', 'row'), pairs)  16.9 us
    pallas_call x1, Pallas kernels, edges(): pl.pallas_call(edge_kernel, grid=(NB,), in_specs=[strip(0), strip(3), str...  12.7 us
  transfers between devices with their start and end apart: 18, of which 4 were waited for; matrix products, arithmetic and copies ran while one was open for 2% of the time, Pallas kernels for 20%

profile of v1, /device:TPU:0, one launch (start us, length us, event | category | flops | bytes accessed | tf_op | source)
XLA Modules:
  0.0 326.6 jit_solution(14449001290386871473)
XLA Ops:
  0.6 0.9 bitcast_dynamic-update-slice_fusion.4
  1.6 0.9 bitcast_dynamic-update-slice_fusion.3
  2.5 0.9 bitcast_dynamic-update-slice_fusion.2
  3.5 0.9 bitcast_dynamic-update-slice_fusion.1
  4.4 0.9 bitcast_dynamic-update-slice_fusion
  5.4 4.3 %collective-permute-start = (f32[5,96,128]{2,1,0:T(8,128)S(1)}, f32[5,96,128]{2,1,0:T(8,128)S(1)}, u32[]{:S(2)}, u32[]{:S(2)}) collective-permute-start(f32[5,96,128]{2,1,0:T(8,128)S(1)} %get-tuple-element.74), channel_id=1, source_target_pairs={{0,12},{1,13},{2,14},{3,15},{4,0},{5,1},{6,2},{7,3},{8,4},{9,5},{1... | collective-permute-start | bytes 737288 | tf_op jit(solution)/shard_map/ppermute | solution.py:541
  9.7 6.4 %collective-permute-done = f32[5,96,128]{2,1,0:T(8,128)S(1)} collective-permute-done((f32[5,96,128]{2,1,0:T(8,128)S(1)}, f32[5,96,128]{2,1,0:T(8,128)S(1)}, u32[]{:S(2)}, u32[]{:S(2)}) %collective-permute-start) | collective-permute-done | bytes 245792 | tf_op jit(solution)/shard_map/ppermute | solution.py:541
  16.2 5.2 %collective-permute-done.1 = f32[5,96,128]{2,1,0:T(8,128)S(1)} collective-permute-done((f32[5,96,128]{2,1,0:T(8,128)S(1)}, f32[5,96,128]{2,1,0:T(8,128)S(1)}, u32[]{:S(2)}, u32[]{:S(2)}) %collective-permute-start.1) | collective-permute-done | bytes 245792 | tf_op jit(solution)/shard_map/ppermute | solution.py:541
  21.4 0.1 pad_maximum_fusion.3
  21.5 1.3 collective-permute-start.3
  22.8 3.1 collective-permute-start.2
  25.9 12.7 %edges.1 = (f32[96,128]{1,0:T(8,128)}, f32[96,128]{1,0:T(8,128)}, f32[2,48,512]{2,1,0:T(8,128)}, f32[3,48,512]{2,1,0:T(8,128)}) custom-call(f32[41,96,512]{2,1,0:T(8,128)} %un.1, f32[41,96,512]{2,1,0:T(8,128)} %un.1, f32[41,96,512]{2,1,0:T(8,128)} %vn.1, f32[41,96,512]{2,1,0:T(8,128)} %vn.1, f32[41,96,512]{2,1,0:T(8,128)} %tf.1, f32[41,96,512]{2,1,0:T(8,128)} %sf.1, ...), custom_call_target="tpu_custom_call" | custom-call | flops 10000000 | bytes 16000000 | tf_op jit(solution)/shard_map/edges/pallas_call | solution.py:120
  38.6 1.3 collective-permute-start.4
  39.9 1.3 collective-permute-start.7
  41.2 0.7 slice.34
  41.9 1.3 collective-permute-start.5
  43.2 21.3 %tracers.1 = (f32[41,96,512]{2,1,0:T(8,128)}, f32[41,96,512]{2,1,0:T(8,128)}, f32[41,96,512]{2,1,0:T(8,128)}, f32[96,128]{1,0:T(8,128)}, f32[96,128]{1,0:T(8,128...) custom-call(f32[41,96,512]{2,1,0:T(8,128)} %tf.1, f32[41,96,512]{2,1,0:T(8,128)} %sf.1, s32[96,512]{1,0:T(8,128)} %kc.5, ...), custom_call_target="tpu_custom_call" | custom-call | flops 100000000 | bytes 40000000 | tf_op jit(solution)/shard_map/tracers/pallas_call | solution.py:199
  64.5 0.7 slice.35
  65.2 1.6 collective-permute-start.6
  66.8 3.7 %collective-permute-start.8 = (f32[2,48,512]{2,1,0:T(8,128)}, f32[2,48,512]{2,1,0:T(8,128)S(1)}, u32[]{:S(2)}, u32[]{:S(2)}) collective-permute-start(f32[2,48,512]{2,1,0:T(8,128)} %get-tuple-element.47), channel_id=1, source_target_pairs={{0,1},{1,2},{2,3},{4,5},{5,6},{6,7},{8,9},{9,10},{10,11},{12,13},{... | collective-permute-start | bytes 589832 | tf_op jit(solution)/shard_map/ppermute | solution.py:541
  70.5 0.6 pad_maximum_fusion.10.rw.rwn
  71.2 5.0 %collective-permute-start.9 = (f32[8,128]{1,0:T(8,128)S(1)}, f32[8,128]{1,0:T(8,128)S(1)}, u32[]{:S(2)}, u32[]{:S(2)}) collective-permute-start(f32[8,128]{1,0:T(8,128)S(1)} %slice.35), channel_id=1, source_target_pairs={{0,13},{1,14},{2,15},{4,1},{5,2},{6,3},{8,5},{9,6},{10,7},{12,9},{... | collective-permute-start | bytes 12296 | tf_op jit(solution)/shard_map/ppermute | solution.py:541
  76.1 1.6 pad_maximum_fusion.pl5.planes
  77.7 3.0 geometry.1
  80.8 0.5 copy-done.8
  81.3 0.1 copy-done.3
  81.5 71.3 %momentum.1 = (f32[41,96,512]{2,1,0:T(8,128)}, f32[41,96,512]{2,1,0:T(8,128)}, f32[96,512]{1,0:T(8,128)}, f32[96,512]{1,0:T(8,128)}, f32[96,512]{1,0:T(8,128)}, ...) custom-call(f32[41,96,512]{2,1,0:T(8,128)} %un.1, f32[41,96,512]{2,1,0:T(8,128)} %un.1, ...), custom_call_target="tpu_custom_call" | custom-call | flops 200000000 | bytes 64000000 | tf_op jit(solution)/shard_map/momentum/pallas_call | solution.py:366
  152.8 0.9 pad_maximum_fusion.8
  153.7 1.2 collective-permute-start.10
  154.9 0.8 collective-permute-start.11
  155.7 3.1 collective-permute-done.10
  158.8 2.1 collective-permute-done.11
  160.9 1.0 pad_maximum_fusion.7
  162.0 1.3 collective-permute-start.13
  163.3 3.0 collective-permute-start.12
  166.3 0.9 pad_maximum_fusion.4
  167.3 2.1 collective-permute-start.17
  169.4 1.5 collective-permute-start.16
  170.9 2.2 collective-permute-start.15
  173.1 0.7 copy.17.tide
  173.8 0.8 add.3
  174.6 0.1 collective-permute-start.14
  174.7 2.0 pad_maximum_fusion.1.force
  176.7 26.8 %subcycles.1 = (f32[96,512]{1,0:T(8,128)}, f32[96,512]{1,0:T(8,128)}, f32[96,512]{1,0:T(8,128)}, f32[104,640]{1,0:T(8,128)}, f32[104,640]{1,0:T(8,128)}) custom-call(f32[5,176,640]{2,1,0:T(8,128)} %pad_maximum_fusion.pl5.planes, f32[176,640]{1,0:T(8,128)} %get-tuple-element.39.ku.kun.kus, f32[176,640]{1,0:T(8,128)} %get-tuple-element.40.kv.kvn.kvs, ...), custom_call_target="tpu_custom_call" | custom-call | flops 100000000 | bytes 1000000 | tf_op jit(solution)/shard_map/subcycles/pallas_call | solution.py:442
  203.6 0.5 copy-done.6
  204.1 0.1 copy-done.2
  204.3 0.1 copy-done
  204.4 122.1 %finish.1 = (f32[41,96,512]{2,1,0:T(8,128)}, f32[41,96,512]{2,1,0:T(8,128)}, f32[41,96,512]{2,1,0:T(8,128)}, f32[41,96,512]{2,1,0:T(8,128)}) custom-call(f32[41,96,512]{2,1,0:T(8,128)} %get-tuple-element.53.us, f32[41,96,512]{2,1,0:T(8,128)} %get-tuple-element.54.vs, f32[41,96,512]{2,1,0:T(8,128)} %get-tuple-element.55.t.tn, ...), custom_call_target="tpu_custom_call" | custom-call | flops 100000000 | bytes 80000000 | tf_op jit(solution)/shard_map/finish/pallas_call | solution.py:519
  (36 shorter events, 0.2 us)
Async XLA Ops:
  5.4 10.8 %collective-permute-start = (f32[5,96,128]{2,1,0:T(8,128)S(1)}, f32[5,96,128]{2,1,0:T(8,128)S(1)}, u32[]{:S(2)}, u32[]{:S(2)}) collective-permute-start(f32[5,96,128]{2,1,0:T(8,128)S(1)} %get-tuple-element.74), channel_id=1, source_target_pairs={{0,12},{1,13},{2,14},{3,15},{4,0},{5,1},{6,2},{7,3},{8,4},{9,5},{1... | collective-permute-start | bytes 737288 | tf_op jit(solution)/shard_map/ppermute | solution.py:541
  9.7 11.7 %collective-permute-start.1 = (f32[5,96,128]{2,1,0:T(8,128)S(1)}, f32[5,96,128]{2,1,0:T(8,128)S(1)}, u32[]{:S(2)}, u32[]{:S(2)}) collective-permute-start(f32[5,96,128]{2,1,0:T(8,128)S(1)} %get-tuple-element.73), channel_id=1, source_target_pairs={{0,4},{1,5},{2,6},{3,7},{4,8},{5,9},{6,10},{7,11},{8,12},{9,13},{1... | collective-permute-start | bytes 737288 | tf_op jit(solution)/shard_map/ppermute | solution.py:541
  21.5 49.7 %collective-permute-start.3 = (f32[5,40,640]{2,1,0:T(8,128)S(1)}, f32[5,40,640]{2,1,0:T(8,128)S(1)}, u32[]{:S(2)}, u32[]{:S(2)}) collective-permute-start(f32[5,40,640]{2,1,0:T(8,128)S(1)} %get-tuple-element.72), channel_id=1, source_target_pairs={{1,0},{2,1},{3,2},{5,4},{6,5},{7,6},{9,8},{10,9},{11,10},{13,12},{... | collective-permute-start | bytes 1536008 | tf_op jit(solution)/shard_map/ppermute | solution.py:541
  22.8 53.3 %collective-permute-start.2 = (f32[5,40,640]{2,1,0:T(8,128)S(1)}, f32[5,40,640]{2,1,0:T(8,128)S(1)}, u32[]{:S(2)}, u32[]{:S(2)}) collective-permute-start(f32[5,40,640]{2,1,0:T(8,128)S(1)} %get-tuple-element.71), channel_id=1, source_target_pairs={{0,1},{1,2},{2,3},{4,5},{5,6},{6,7},{8,9},{9,10},{10,11},{12,13},{... | collective-permute-start | bytes 1536008 | tf_op jit(solution)/shard_map/ppermute | solution.py:541
  38.6 28.3 %collective-permute-start.4 = (f32[96,128]{1,0:T(8,128)}, f32[96,128]{1,0:T(8,128)S(1)}, u32[]{:S(2)}, u32[]{:S(2)}) collective-permute-start(f32[96,128]{1,0:T(8,128)} %get-tuple-element.44), channel_id=1, source_target_pairs={{0,4},{1,5},{2,6},{3,7},{4,8},{5,9},{6,10},{7,11},{8,12},{9,13},{1... | collective-permute-start | bytes 147464 | tf_op jit(solution)/shard_map/ppermute | solution.py:541
  39.9 40.9 %collective-permute-start.7 = (f32[3,48,512]{2,1,0:T(8,128)}, f32[3,48,512]{2,1,0:T(8,128)}, u32[]{:S(2)}, u32[]{:S(2)}) collective-permute-start(f32[3,48,512]{2,1,0:T(8,128)} %get-tuple-element.46.rown), channel_id=1, source_target_pairs={{1,0},{2,1},{3,2},{5,4},{6,5},{7,6},{9,8},{10,9},{11,10},{13,12},{... | collective-permute-start | bytes 884744 | tf_op jit(solution)/shard_map/ppermute | solution.py:541
  41.9 23.3 %collective-permute-start.5 = (f32[8,128]{1,0:T(8,128)S(1)}, f32[8,128]{1,0:T(8,128)S(1)}, u32[]{:S(2)}, u32[]{:S(2)}) collective-permute-start(f32[8,128]{1,0:T(8,128)S(1)} %slice.34), channel_id=1, source_target_pairs={{1,4},{2,5},{3,6},{5,8},{6,9},{7,10},{9,12},{10,13},{11,14},{13,0}... | collective-permute-start | bytes 12296 | tf_op jit(solution)/shard_map/ppermute | solution.py:541
  65.2 15.5 %collective-permute-start.6 = (f32[96,128]{1,0:T(8,128)}, f32[96,128]{1,0:T(8,128)}, u32[]{:S(2)}, u32[]{:S(2)}) collective-permute-start(f32[96,128]{1,0:T(8,128)} %get-tuple-element.45), channel_id=1, source_target_pairs={{0,12},{1,13},{2,14},{3,15},{4,0},{5,1},{6,2},{7,3},{8,4},{9,5},{1... | collective-permute-start | bytes 147464 | tf_op jit(solution)/shard_map/ppermute | solution.py:541
  66.8 13.9 %collective-permute-start.8 = (f32[2,48,512]{2,1,0:T(8,128)}, f32[2,48,512]{2,1,0:T(8,128)S(1)}, u32[]{:S(2)}, u32[]{:S(2)}) collective-permute-start(f32[2,48,512]{2,1,0:T(8,128)} %get-tuple-element.47), channel_id=1, source_target_pairs={{0,1},{1,2},{2,3},{4,5},{5,6},{6,7},{8,9},{9,10},{10,11},{12,13},{... | collective-permute-start | bytes 589832 | tf_op jit(solution)/shard_map/ppermute | solution.py:541
  71.2 9.6 %collective-permute-start.9 = (f32[8,128]{1,0:T(8,128)S(1)}, f32[8,128]{1,0:T(8,128)S(1)}, u32[]{:S(2)}, u32[]{:S(2)}) collective-permute-start(f32[8,128]{1,0:T(8,128)S(1)} %slice.35), channel_id=1, source_target_pairs={{0,13},{1,14},{2,15},{4,1},{5,2},{6,3},{8,5},{9,6},{10,7},{12,9},{... | collective-permute-start | bytes 12296 | tf_op jit(solution)/shard_map/ppermute | solution.py:541
  80.7 0.6 copy-start.8
  80.8 0.7 copy-start.3
  81.5 84.9 %copy-start.4 = (f32[2,48,512]{2,1,0:T(8,128)S(1)}, f32[2,48,512]{2,1,0:T(8,128)}, u32[]{:S(2)}) copy-start(f32[2,48,512]{2,1,0:T(8,128)} %get-tuple-element.66) | copy-start | bytes 589828
  81.5 87.9 %copy-start.1 = (f32[2,48,512]{2,1,0:T(8,128)S(1)}, f32[2,48,512]{2,1,0:T(8,128)}, u32[]{:S(2)}) copy-start(f32[2,48,512]{2,1,0:T(8,128)} %get-tuple-element.64.rown) | copy-start | bytes 589828
  81.5 89.4 %copy-start.10 = (f32[96,128]{1,0:T(8,128)S(1)}, f32[96,128]{1,0:T(8,128)}, u32[]{:S(2)}) copy-start(f32[96,128]{1,0:T(8,128)} %get-tuple-element.63) | copy-start | bytes 147460
  81.5 91.6 %copy-start.9 = (f32[36,2]{0,1:T(2,128)S(1)}, f32[36,2]{0,1:T(2,128)}, u32[]{:S(2)}) copy-start(f32[36,2]{0,1:T(2,128)} %param.19) | copy-start | bytes 868
  81.5 92.3 %copy-start.5 = (f32[96,128]{1,0:T(8,128)S(1)}, f32[96,128]{1,0:T(8,128)}, u32[]{:S(2)}) copy-start(f32[96,128]{1,0:T(8,128)} %get-tuple-element.61) | copy-start | bytes 147460
  153.7 5.2 %collective-permute-start.10 = (f32[2,96,128]{2,1,0:T(8,128)S(1)}, f32[2,96,128]{2,1,0:T(8,128)S(1)}, u32[]{:S(2)}, u32[]{:S(2)}) collective-permute-start(f32[2,96,128]{2,1,0:T(8,128)S(1)} %get-tuple-element.78), channel_id=1, source_target_pairs={{0,12},{1,13},{2,14},{3,15},{4,0},{5,1},{6,2},{7,3},{8,4},{9,5},{1... | collective-permute-start | bytes 294920 | tf_op jit(solution)/shard_map/ppermute | solution.py:541
  154.9 6.0 %collective-permute-start.11 = (f32[2,96,128]{2,1,0:T(8,128)S(1)}, f32[2,96,128]{2,1,0:T(8,128)S(1)}, u32[]{:S(2)}, u32[]{:S(2)}) collective-permute-start(f32[2,96,128]{2,1,0:T(8,128)S(1)} %get-tuple-element.77), channel_id=1, source_target_pairs={{0,4},{1,5},{2,6},{3,7},{4,8},{5,9},{6,10},{7,11},{8,12},{9,13},{1... | collective-permute-start | bytes 294920 | tf_op jit(solution)/shard_map/ppermute | solution.py:541
  162.0 12.6 %collective-permute-start.13 = (f32[2,40,640]{2,1,0:T(8,128)S(1)}, f32[2,40,640]{2,1,0:T(8,128)S(1)}, u32[]{:S(2)}, u32[]{:S(2)}) collective-permute-start(f32[2,40,640]{2,1,0:T(8,128)S(1)} %get-tuple-element.76), channel_id=1, source_target_pairs={{1,0},{2,1},{3,2},{5,4},{6,5},{7,6},{9,8},{10,9},{11,10},{13,12},{... | collective-permute-start | bytes 614408 | tf_op jit(solution)/shard_map/ppermute | solution.py:541
  163.3 11.4 %collective-permute-start.12 = (f32[2,40,640]{2,1,0:T(8,128)S(1)}, f32[2,40,640]{2,1,0:T(8,128)S(1)}, u32[]{:S(2)}, u32[]{:S(2)}) collective-permute-start(f32[2,40,640]{2,1,0:T(8,128)S(1)} %get-tuple-element.75), channel_id=1, source_target_pairs={{0,1},{1,2},{2,3},{4,5},{5,6},{6,7},{8,9},{9,10},{10,11},{12,13},{... | collective-permute-start | bytes 614408 | tf_op jit(solution)/shard_map/ppermute | solution.py:541
  167.3 36.3 %collective-permute-start.17 = (f32[3,48,512]{2,1,0:T(8,128)S(1)}, f32[3,48,512]{2,1,0:T(8,128)S(1)}, u32[]{:S(2)}, u32[]{:S(2)}) collective-permute-start(f32[3,48,512]{2,1,0:T(8,128)S(1)} %pad_maximum_fusion.4), channel_id=1, source_target_pairs={{0,1},{1,2},{2,3},{4,5},{5,6},{6,7},{8,9},{9,10},{10,11},{12,13},{... | collective-permute-start | bytes 884744 | tf_op jit(solution)/shard_map/ppermute | solution.py:541
  169.4 34.1 %collective-permute-start.16 = (f32[2,48,512]{2,1,0:T(8,128)S(1)}, f32[2,48,512]{2,1,0:T(8,128)S(1)}, u32[]{:S(2)}, u32[]{:S(2)}) collective-permute-start(f32[2,48,512]{2,1,0:T(8,128)S(1)} %copy-done.1), channel_id=1, source_target_pairs={{1,0},{2,1},{3,2},{5,4},{6,5},{7,6},{9,8},{10,9},{11,10},{13,12},{... | collective-permute-start | bytes 589832 | tf_op jit(solution)/shard_map/ppermute | solution.py:541
  170.9 32.6 %collective-permute-start.15 = (f32[96,128]{1,0:T(8,128)S(1)}, f32[96,128]{1,0:T(8,128)S(1)}, u32[]{:S(2)}, u32[]{:S(2)}) collective-permute-start(f32[96,128]{1,0:T(8,128)S(1)} %copy-done.10), channel_id=1, source_target_pairs={{0,12},{1,13},{2,14},{3,15},{4,0},{5,1},{6,2},{7,3},{8,4},{9,5},{1... | collective-permute-start | bytes 147464 | tf_op jit(solution)/shard_map/ppermute | solution.py:541
  174.6 29.0 %collective-permute-start.14 = (f32[96,128]{1,0:T(8,128)S(1)}, f32[96,128]{1,0:T(8,128)S(1)}, u32[]{:S(2)}, u32[]{:S(2)}) collective-permute-start(f32[96,128]{1,0:T(8,128)S(1)} %add.3), channel_id=1, source_target_pairs={{0,4},{1,5},{2,6},{3,7},{4,8},{5,9},{6,10},{7,11},{8,12},{9,13},{1... | collective-permute-start | bytes 147464 | tf_op jit(solution)/shard_map/ppermute | solution.py:541
  203.5 0.6 copy-start.6
  203.5 0.7 copy-start.2
  203.6 0.7 copy-start.7
  203.6 0.8 copy-start

commit v2 on v1

--- a/solution.py
+++ b/solution.py
@@ -134,7 +134,8 @@
     )(u, u, v, v, t, s, kmt, depth, u, v, u, v, t, s, kmt, depth)
 
 
-def tracer_kernel(t, s, kc, hc, tm, sm, pr, pke, pkw, rn, rs, gains):
+def tracer_kernel(t, s, kc, hc, tm_b, sm_b, pr_b, pke, pkw, rn, rs_b, gains):
+    tm, sm, pr, rs = tm_b.at[0], sm_b.at[0], pr_b.at[0], rs_b.at[0]
     b = pl.program_id(0)
     lane = iota(TILE, 1)
     cnt = kc[:]
@@ -148,6 +149,7 @@
         tk, sk = t[k], s[k]
         p, cum = pressure_step(tk, sk, wet, cum, thick)
         pr[k] = p
+        rs[2, k : k + 1, :] = p[0:1, :]
         upper = jnp.where(k + 1 < cnt, c, 0.0) if k + 1 < NL else zero
         top = 1.0 + lower * keep if k else jnp.ones_like(zero)
         inv = 1.0 / (top + upper)
@@ -167,20 +169,14 @@
         bs = sm[k] + gain * bs
         tm[k] = bt
         sm[k] = bs
+        rs[0, k : k + 1, :] = bt[0:1, :]
+        rs[1, k : k + 1, :] = bs[0:1, :]
         for x, base in ((bt, NL), (bs, 2 * NL)):
             ae = jnp.where(lane == base + k, lane_to(x[:, NC - LN :], LN - 1, base + k), ae)
             aw = jnp.where(lane == base + k, lane_to(x[:, :LN], 0, base + k), aw)
     pke[:] = ae
     pkw[:] = aw
 
-    @pl.when(b == 0)
-    def _():
-        for k in range(NL):
-            rs[0, k : k + 1, :] = tm[k, 0:1, :]
-            rs[1, k : k + 1, :] = sm[k, 0:1, :]
-        for i in range(2):
-            rs[i, NL:LP, :] = jnp.zeros((LP - NL, NC), F32)
-
     @pl.when(b == NB - 1)
     def _():
         for k in range(NL):
@@ -190,18 +186,29 @@
             rn[i, NL:LP, :] = jnp.zeros((LP - NL, NC), F32)
 
 
+PACK = jax.ShapeDtypeStruct((NB,) + SLAB, F32)
+
+
+def block_major(f):
+    return pl.BlockSpec((1,) + SLAB, lambda b: (f(b), 0, 0, 0))
+
+
+def first_rows(f):
+    return pl.BlockSpec((1, 3, LP, NC), lambda b: (f(b), 0, 0, 0))
+
+
 def tracers(t, s, kmt, depth):
     cube = pl.BlockSpec(SLAB, lambda b: (0, b, 0))
+    pack = block_major(lambda b: b)
     plane = pl.BlockSpec(ROW, lambda b: (b, 0))
     col = pl.BlockSpec(TILE, lambda b: (b, 0))
     rows = pl.BlockSpec((2, LP, NC), lambda b: (0, 0, 0))
-    big = jax.ShapeDtypeStruct((NL, NR, NC), F32)
     return pl.pallas_call(
         tracer_kernel,
         grid=(NB,),
         in_specs=[cube, cube, plane, plane],
-        out_specs=[cube, cube, cube, col, col, rows, rows],
-        out_shape=[big, big, big] + [jax.ShapeDtypeStruct((NR, LN), F32)] * 2 + [jax.ShapeDtypeStruct((2, LP, NC), F32)] * 2,
+        out_specs=[pack, pack, pack, col, col, rows, first_rows(lambda b: b)],
+        out_shape=[PACK, PACK, PACK] + [jax.ShapeDtypeStruct((NR, LN), F32)] * 2 + [jax.ShapeDtypeStruct((2, LP, NC), F32), jax.ShapeDtypeStruct((NB, 3, LP, NC), F32)],
         scratch_shapes=[VM(SLAB, F32)],
         compiler_params=pltpu.CompilerParams(dimension_semantics=("arbitrary",)),
         cost_estimate=pl.CostEstimate(flops=10**8, bytes_accessed=40 * 10**6, transcendentals=0),
@@ -258,18 +265,29 @@
 
 
 def momentum_kernel(
-    u, un, v, vn, p, pn, ku, kun, kv, kvn, du, dv, kus, kvs, rw, rwn, re, rnorth, rsouth, rown, corner,
-    us, vs, fx, fy, su, sv, pke, vrow,
-    cc, hh, srcu, srcv, gu, gv,
+    u, v, p_b, pfirst, kun, kvn, kux, kvx, du, dv, kus, kvs, rwn, ren, re, rnorth, rsouth, rown, corner,
+    us_b, vs_b, fx, fy, su, sv, pke, vrow,
+    cc, hh, srcu, srcv, gu, gv, ums, vms,
 ):
-    b = pl.program_id(0)
-    last = b == NB - 1
+    step = pl.program_id(0)
+    last = step == NB
+    us, vs, p = us_b.at[0], vs_b.at[0], p_b.at[0]
     row = iota(ROW, 0)
     rowx = iota(WIDE, 0)
     lane = iota(TILE, 1)
-
-    @pl.when(b == 0)
+    kxn, kyn = kun[:], kvn[:]
+    rwv, rev = rwn[:], ren[:]
+
+    def masked(k, uk, vk):
+        hu = jnp.where(lane == 0, lane_to(rev, k, 0), lane_to(rwv, k, LN - 1))
+        hv = jnp.where(lane == 0, lane_to(rev, NL + k, 0), lane_to(rwv, NL + k, LN - 1))
+        um = only(k < kxn, jnp.concatenate([uk, hu], axis=1))
+        return um, only(k < kyn, jnp.concatenate([vk, hv], axis=1))
+
+    @pl.when(step == 0)
     def _():
+        for k in range(NL):
+            ums[k], vms[k] = masked(k, u[k], v[k])
         lev = iota((LP, NC), 0).astype(F32)
         lev1 = iota((LP, LN), 0)
         ks, kw = kus[7:8, :NC], kvs[7:8, :NC]
@@ -279,8 +297,8 @@
         edge = jnp.sum(pick, axis=1, keepdims=True)
         edge = only(lev[:, :1] < kvs[7:8, NC : NC + 1], edge)
         s_ve = jnp.where(iota((LP, NC), 1) == NC - 1, edge, from_east(s_v))
-        u_0 = only(lev < ku[0:1, :NC], rown[0])
-        v_0 = only(lev < kv[0:1, :NC], rown[1])
+        u_0 = only(lev < kxn[0:1, :NC], rown[0])
+        v_0 = only(lev < kyn[0:1, :NC], rown[1])
         c_s = 0.25 * ((s_v + s_ve) * (s_u + u_0))
         h_s = s_v + v_0
         h_s = 0.25 * (h_s * h_s) + rown[2]
@@ -288,76 +306,78 @@
             cc[k, 7:8, :] = c_s[k : k + 1, :]
             hh[k, 7:8, :] = h_s[k : k + 1, :]
 
-    kx, ky = ku[:], kv[:]
-    kxn, kyn = kun[:], kvn[:, :NC]
-    rwv, rwnv, rev = rw[:], rwn[:], re[:]
-    zx = jnp.zeros(ROW, F32)
-    ax, ay = zx, zx
-    for k in range(NL):
-        hu = jnp.where(lane == 0, lane_to(rev, k, 0), lane_to(rwv, k, LN - 1))
-        hv = jnp.where(lane == 0, lane_to(rev, NL + k, 0), lane_to(rwv, NL + k, LN - 1))
-        hp = lane_to(rev, 2 * NL + k, 0)
-        hn = lane_to(rwnv, k, LN - 1)
-        um = only(k < kx, jnp.concatenate([u[k], hu], axis=1))
-        vm = only(k < ky, jnp.concatenate([v[k], hv], axis=1))
-        pe = jnp.concatenate([p[k], hp], axis=1)
-        nu = jnp.where(last, rnorth[0, k : k + 1, :], un[k])
-        nv = jnp.where(last, rnorth[1, k : k + 1, :], vn[k])
-        np_ = jnp.where(last, rnorth[2, k : k + 1, :], pn[k])
-        nu = only(k < kxn, jnp.concatenate([nu, hn], axis=1))
-        nv = only(k < kyn, nv)
-        u_n = up_row(um, nu, rowx)
-        c = 0.25 * ((vm + from_east(vm)) * (um + u_n))
-        g = from_west(um) + um
-        g = 0.25 * (g * g) + pe
-        ge = from_east(g)[:, :NC]
-        v5 = vm[:, :NC]
-        h = v5 + up_row(v5, nv, row)
-        h = 0.25 * (h * h) + up_row(pe[:, :NC], np_, row)
-        cw = from_west(c)[:, :NC]
-        c5 = c[:, :NC]
-        tu = (ge - g[:, :NC]) + (c5 - down_row(c5, cc[k], row))
-        tv = (h - down_row(h, hh[k], row)) + (c5 - cw)
-        tu = only(k < kx[:, :NC], tu)
-        tv = only(k < ky[:, :NC], tv)
-        ax += tu
-        ay += tv
-        srcu[k] = um[:, :NC] - DT * tu
-        srcv[k] = v5 - DT * tv
-        cc[k] = c5
-        hh[k] = h
-    dzu, dzv = du[:, :NC], dv[:, :NC]
-    kx, ky = kx[:, :NC], ky[:, :NC]
-    fx[:] = -dzu * ax
-    fy[:] = -dzv * ay
-    sa, sb = solve_pair(srcu, srcv, couple(kx, dzu, KV), couple(ky, dzv, KV), kx, ky, us, vs, gu, gv)
-    sa, sb = dzu * sa, dzv * sb
-    su[:] = sa
-    sv[:] = sb
-    ae = jnp.zeros(TILE, F32)
-    for k in range(NL):
-        ae = jnp.where(lane == k, lane_to(us[k, :, NC - LN :], LN - 1, k), ae)
-    pke[:] = jnp.where(lane == 3 * NL, lane_to(sa[:, NC - LN :], LN - 1, 3 * NL), ae)
-
-    @pl.when(last)
+    @pl.when(step > 0)
     def _():
-        for k in range(NL):
-            vrow[k : k + 1, :] = vs[k, 7:8, :]
-        vrow[NL : NL + 1, :] = sb[7:8, :]
-        vrow[NL + 1 : LP, :] = jnp.zeros((LP - NL - 1, NC), F32)
-
-
-def momentum(u, v, p, geo, rw, re, rnorth, rsouth, rown, corner):
+        kx, ky = kux[:], kvx[:]
+        pev = re[:]
+        zx = jnp.zeros(ROW, F32)
+        ax, ay = zx, zx
+        for k in range(NL):
+            um, vm = ums[k], vms[k]
+            pe = jnp.concatenate([p[k], lane_to(pev, 2 * NL + k, 0)], axis=1)
+            uk = jnp.where(last, rnorth[0, k : k + 1, :], u[k])
+            vk = jnp.where(last, rnorth[1, k : k + 1, :], v[k])
+            np_ = jnp.where(last, rnorth[2, k : k + 1, :], pfirst[0, 2, k : k + 1, :])
+            nu, nv = masked(k, uk, vk)
+            ums[k], vms[k] = nu, nv
+            u_n = up_row(um, nu, rowx)
+            c = 0.25 * ((vm + from_east(vm)) * (um + u_n))
+            g = from_west(um) + um
+            g = 0.25 * (g * g) + pe
+            ge = from_east(g)[:, :NC]
+            v5 = vm[:, :NC]
+            h = v5 + up_row(v5, nv[:, :NC], row)
+            h = 0.25 * (h * h) + up_row(pe[:, :NC], np_, row)
+            cw = from_west(c)[:, :NC]
+            c5 = c[:, :NC]
+            tu = (ge - g[:, :NC]) + (c5 - down_row(c5, cc[k], row))
+            tv = (h - down_row(h, hh[k], row)) + (c5 - cw)
+            tu = only(k < kx, tu)
+            tv = only(k < ky, tv)
+            ax += tu
+            ay += tv
+            srcu[k] = um[:, :NC] - DT * tu
+            srcv[k] = v5 - DT * tv
+            cc[k] = c5
+            hh[k] = h
+        dzu, dzv = du[:], dv[:]
+        fx[:] = -dzu * ax
+        fy[:] = -dzv * ay
+        sa, sb = solve_pair(srcu, srcv, couple(kx, dzu, KV), couple(ky, dzv, KV), kx, ky, us, vs, gu, gv)
+        sa, sb = dzu * sa, dzv * sb
+        su[:] = sa
+        sv[:] = sb
+        ae = jnp.zeros(TILE, F32)
+        for k in range(NL):
+            ae = jnp.where(lane == k, lane_to(us[k, :, NC - LN :], LN - 1, k), ae)
+        pke[:] = jnp.where(lane == 3 * NL, lane_to(sa[:, NC - LN :], LN - 1, 3 * NL), ae)
+
+        @pl.when(last)
+        def _():
+            for k in range(NL):
+                vrow[k : k + 1, :] = vs[k, 7:8, :]
+            vrow[NL : NL + 1, :] = sb[7:8, :]
+            vrow[NL + 1 : LP, :] = jnp.zeros((LP - NL - 1, NC), F32)
+
+
+def momentum(u, v, p, first, geo, rw, re, rnorth, rsouth, rown, corner):
     ku, kv, du, dv = geo
-    cube = pl.BlockSpec(SLAB, lambda b: (0, b, 0))
-    cubn = pl.BlockSpec(SLAB, lambda b: (0, jnp.minimum(b + 1, NB - 1), 0))
-    wide = pl.BlockSpec(WIDE, lambda b: (HT + b, 0))
-    widn = pl.BlockSpec(WIDE, lambda b: (HT + 1 + b, 0))
+
+    def this(b):
+        return jnp.maximum(b, 1) - 1
+
+    def ahead(b):
+        return jnp.minimum(b, NB - 1)
+
+    cube = pl.BlockSpec(SLAB, lambda b: (0, ahead(b), 0))
+    pack = block_major(this)
+    near = pl.BlockSpec(ROW, lambda b: (HT + this(b), 0))
+    widn = pl.BlockSpec(WIDE, lambda b: (HT + b, 0))
     wids = pl.BlockSpec(WIDE, lambda b: (HT - 1, 0))
-    plane = pl.BlockSpec(ROW, lambda b: (b, 0))
-    col = pl.BlockSpec(TILE, lambda b: (b, 0))
-    coln = pl.BlockSpec(TILE, lambda b: (b + 1, 0))
-    big = jax.ShapeDtypeStruct((NL, NR, NC), F32)
+    plane = pl.BlockSpec(ROW, lambda b: (this(b), 0))
+    col = pl.BlockSpec(TILE, lambda b: (this(b), 0))
+    colw = pl.BlockSpec(TILE, lambda b: (b, 0))
+    cole = pl.BlockSpec(TILE, lambda b: (ahead(b), 0))
     flat = jax.ShapeDtypeStruct((NR, NC), F32)
 
     def rows(n):
@@ -365,15 +385,15 @@
 
     return pl.pallas_call(
         momentum_kernel,
-        grid=(NB,),
-        in_specs=[cube, cubn, cube, cubn, cube, cubn, wide, widn, wide, widn, wide, wide, wids, wids, col, coln, col, rows(3), rows(2), rows(3), pl.BlockSpec(TILE, lambda b: (0, 0))],
-        out_specs=[cube, cube, plane, plane, plane, plane, col, pl.BlockSpec((LP, NC), lambda b: (0, 0))],
-        out_shape=[big, big, flat, flat, flat, flat, jax.ShapeDtypeStruct((NR, LN), F32), jax.ShapeDtypeStruct((LP, NC), F32)],
-        scratch_shapes=[VM(SLAB, F32)] * 6,
+        grid=(NB + 1,),
+        in_specs=[cube, cube, pack, first_rows(ahead), widn, widn, near, near, near, near, wids, wids, colw, cole, col, rows(3), rows(2), rows(3), pl.BlockSpec(TILE, lambda b: (0, 0))],
+        out_specs=[pack, pack, plane, plane, plane, plane, col, pl.BlockSpec((LP, NC), lambda b: (0, 0))],
+        out_shape=[PACK, PACK, flat, flat, flat, flat, jax.ShapeDtypeStruct((NR, LN), F32), jax.ShapeDtypeStruct((LP, NC), F32)],
+        scratch_shapes=[VM(SLAB, F32)] * 6 + [VM((NL,) + WIDE, F32)] * 2,
         compiler_params=pltpu.CompilerParams(dimension_semantics=("arbitrary",)),
         cost_estimate=pl.CostEstimate(flops=2 * 10**8, bytes_accessed=64 * 10**6, transcendentals=0),
         name="momentum",
-    )(u, u, v, v, p, p, ku, ku, kv, kv, du, dv, ku, kv, rw, rw, re, rnorth, rsouth, rown, corner)
+    )(u, v, p, first, ku, kv, ku, kv, du, dv, ku, kv, rw, re, re, rnorth, rsouth, rown, corner)
 
 
 def subcycle_kernel(planes, ku, kv, du, dv, force, tide, eta_o, u_o, v_o, ub_o, vb_o, eta, tu, tv, cu, cv, fu, fv, ub, vb):
@@ -451,9 +471,10 @@
 
 
 def finish_kernel(
-    us, vs, t, tn, s, sn, kc, ku, kv, du, dv, ub, vb, su, sv, kvs, dvs, vbs, rw, re, rnorth, rsouth, rown,
+    us_b, vs_b, t_b, s_b, first, kc, ku, kv, du, dv, ub, vb, su, sv, kvs, dvs, vbs, rw, re, rnorth, rsouth, rown,
     uo, vo, to, so, ct, cs,
 ):
+    us, vs, t, s = us_b.at[0], vs_b.at[0], t_b.at[0], s_b.at[0]
     b = pl.program_id(0)
     last = b == NB - 1
     row = iota(ROW, 0)
@@ -469,8 +490,8 @@
         kx = kvs[7:8, :NC]
         cor = correction(vbs[7:8, :NC], rsouth[0, NL : NL + 1, :], kx, dvs[7:8, :NC])
         vel = 0.5 * DT * only(lev < kx, rsouth[0] + cor)
-        ft = vel * (rsouth[1] + rown[0])
-        fs = vel * (rsouth[2] + rown[1])
+        ft = vel * (rsouth[1] + rown[0, 0])
+        fs = vel * (rsouth[2] + rown[0, 1])
         for k in range(NL):
             ct[k, 7:8, :] = ft[k : k + 1, :]
             cs[k, 7:8, :] = fs[k : k + 1, :]
@@ -488,23 +509,23 @@
         vo[k] = ve
         hx, hy = (0.5 * DT) * ue, (0.5 * DT) * ve
         wet = k < cnt
-        for i, (x, nxt, out, carry) in enumerate(((t, tn, to, ct), (s, sn, so, cs))):
+        for i, (x, out, carry) in enumerate(((t, to, ct), (s, so, cs))):
             base = NL * (i + 1) + k
             halo = jnp.where(lane == 0, lane_to(rev, base, 0), lane_to(rwv, base, LN - 1))
             own = x[k]
             xe = jnp.concatenate([own, halo], axis=1)
             f = hx * (xe + from_east(xe))
-            north = jnp.where(last, rnorth[i, k : k + 1, :], nxt[k])
+            north = jnp.where(last, rnorth[i, k : k + 1, :], first[0, i, k : k + 1, :])
             fy = hy * (own + up_row(own, north, row))
             div = (f - from_west(f))[:, :NC] + (fy - down_row(fy, carry[k], row))
             carry[k] = fy
             out[k] = only(wet, own - div)
 
 
-def finish(us, vs, tm, sm, kmt, geo, ub, vb, su, sv, rw, re, rnorth, rsouth, rown):
+def finish(us, vs, tm, sm, first, kmt, geo, ub, vb, su, sv, rw, re, rnorth, rsouth):
     ku, kv, du, dv = geo
     cube = pl.BlockSpec(SLAB, lambda b: (0, b, 0))
-    cubn = pl.BlockSpec(SLAB, lambda b: (0, jnp.minimum(b + 1, NB - 1), 0))
+    pack = block_major(lambda b: b)
     wide = pl.BlockSpec(WIDE, lambda b: (HT + b, 0))
     wids = pl.BlockSpec(WIDE, lambda b: (HT - 1, 0))
     bar = pl.BlockSpec(WIDE, lambda b: (b + 1, 0))
@@ -519,14 +540,14 @@
     return pl.pallas_call(
         finish_kernel,
         grid=(NB,),
-        in_specs=[cube, cube, cube, cubn, cube, cubn, plane, wide, wide, wide, wide, bar, bar, plane, plane, wids, wids, bars, col, col, rows(2), rows(3), rows(2)],
+        in_specs=[pack, pack, pack, pack, first_rows(lambda b: jnp.minimum(b + 1, NB - 1)), plane, wide, wide, wide, wide, bar, bar, plane, plane, wids, wids, bars, col, col, rows(3), rows(3), first_rows(lambda b: 0)],
         out_specs=[cube] * 4,
         out_shape=[big] * 4,
         scratch_shapes=[VM(SLAB, F32)] * 2,
         compiler_params=pltpu.CompilerParams(dimension_semantics=("arbitrary",)),
         cost_estimate=pl.CostEstimate(flops=10**8, bytes_accessed=80 * 10**6, transcendentals=0),
         name="finish",
-    )(us, vs, tm, tm, sm, sm, kmt, ku, kv, du, dv, ub, vb, su, sv, kv, dv, vb, rw, re, rnorth, rsouth, rown)
+    )(us, vs, tm, sm, first, kmt, ku, kv, du, dv, ub, vb, su, sv, kv, dv, vb, rw, re, rnorth, rsouth, first)
 
 
 def solution(mesh):
@@ -555,14 +576,14 @@
         nw = send(pke[:8], -1, 1)
         se = send(pkw[NR - 8 :], 1, -1)
         geo = geometry(planes)
-        tm, sm, pr, tke, tkw, trn, trs = tracers(t, s, kmt, depth)
+        tm, sm, pr, tke, tkw, trn, first = tracers(t, s, kmt, depth)
         rw = jnp.concatenate([rw, nw], axis=0)
-        us, vs, fx, fy, su, sv, uke, vrow = momentum(u, v, pr, geo, rw, re, rnorth, rsouth, prs, se)
+        us, vs, fx, fy, su, sv, uke, vrow = momentum(u, v, pr, first, geo, rw, re, rnorth, rsouth, prs, se)
         force = widen(jnp.stack([fx, fy]))
         fw, fe = send(tke + uke, 0, 1), send(tkw, 0, -1)
-        fsouth, fnorth = send(jnp.concatenate([vrow[None], trn]), 1, 0), send(trs, -1, 0)
+        fsouth, fnorth = send(jnp.concatenate([vrow[None], trn]), 1, 0), send(first[0], -1, 0)
         eta_n, u_n, v_n, ub, vb = subcycles(planes, geo, force, tide)
-        uo, vo, to, so = finish(us, vs, tm, sm, kmt, geo, ub, vb, su, sv, fw, fe, fnorth, fsouth, trs)
+        uo, vo, to, so = finish(us, vs, tm, sm, first, kmt, geo, ub, vb, su, sv, fw, fe, fnorth, fsouth)
         return eta_n, u_n, v_n, uo, vo, to, so
 
     cube, plane = P(None, "row", "col"), P("row", "col")

time: 328 us -> 308 us (0.939)
  Pallas kernels: 257 us -> 237 us
    pallas_call x2, Pallas kernels: 193 us -> 173 us  [the longest x1 122 us: finish(): pl.pallas_call(finish_kernel, grid=(NB,), in_specs=[pack, pack, pack, pac...]
  transfers between devices with their start and end apart: 18 -> 18, of which waited for: 4 -> 4; matrix products, arithmetic and copies ran while one was open for 2% -> 4% of each run, Pallas kernels for 20% -> 21%
where the time goes in v2:
time: 308 us; the launch traced here: 307 us
  Pallas kernels  237 us (77%)
  starting transfers between devices  35.1 us (11%)
  waiting for transfers between devices  14.6 us (5%)
  other arithmetic  9.7 us (3%)
  local copies, waits for them, and re-layouts  8.96 us (3%)
    pallas_call x1, Pallas kernels, finish(): pl.pallas_call(finish_kernel, grid=(NB,), in_specs=[pack, pack, pack, pac...  122 us
    pallas_call x1, Pallas kernels, momentum(): pl.pallas_call(momentum_kernel, grid=(NB + 1,), in_specs=[cube, cube, pac...  51 us
    ppermute x18, starting transfers between devices, send(): return lax.ppermute(x, ('col', 'row'), pairs)  35.1 us
    pallas_call x1, Pallas kernels, subcycles(): pl.pallas_call(subcycle_kernel, in_specs=[vm] * 6 + [pl.BlockSpec(memory_...  26.9 us
    pallas_call x1, Pallas kernels, tracers(): pl.pallas_call(tracer_kernel, grid=(NB,), in_specs=[cube, cube, plane, pl...  22 us
    ppermute x18, waiting for transfers between devices, send(): return lax.ppermute(x, ('col', 'row'), pairs)  14.6 us
    pallas_call x1, Pallas kernels, edges(): pl.pallas_call(edge_kernel, grid=(NB,), in_specs=[strip(0), strip(3), str...  12.7 us
  transfers between devices with their start and end apart: 18, of which 4 were waited for; matrix products, arithmetic and copies ran while one was open for 4% of the time, Pallas kernels for 21%

profile of v2, /device:TPU:0, one launch (start us, length us, event | category | flops | bytes accessed | tf_op | source)
XLA Modules:
  0.0 306.9 jit_solution(8741879584828059219)
XLA Ops:
  0.6 0.9 bitcast_dynamic-update-slice_fusion.4
  1.6 0.9 bitcast_dynamic-update-slice_fusion.3
  2.5 0.9 bitcast_dynamic-update-slice_fusion.2
  3.5 0.9 bitcast_dynamic-update-slice_fusion.1
  4.4 0.9 bitcast_dynamic-update-slice_fusion
  5.4 4.3 %collective-permute-start = (f32[5,96,128]{2,1,0:T(8,128)S(1)}, f32[5,96,128]{2,1,0:T(8,128)S(1)}, u32[]{:S(2)}, u32[]{:S(2)}) collective-permute-start(f32[5,96,128]{2,1,0:T(8,128)S(1)} %get-tuple-element.74), channel_id=1, source_target_pairs={{0,12},{1,13},{2,14},{3,15},{4,0},{5,1},{6,2},{7,3},{8,4},{9,5},{1... | collective-permute-start | bytes 737288 | tf_op jit(solution)/shard_map/ppermute | solution.py:562
  9.7 6.4 %collective-permute-done = f32[5,96,128]{2,1,0:T(8,128)S(1)} collective-permute-done((f32[5,96,128]{2,1,0:T(8,128)S(1)}, f32[5,96,128]{2,1,0:T(8,128)S(1)}, u32[]{:S(2)}, u32[]{:S(2)}) %collective-permute-start) | collective-permute-done | bytes 245792 | tf_op jit(solution)/shard_map/ppermute | solution.py:562
  16.2 5.2 %collective-permute-done.1 = f32[5,96,128]{2,1,0:T(8,128)S(1)} collective-permute-done((f32[5,96,128]{2,1,0:T(8,128)S(1)}, f32[5,96,128]{2,1,0:T(8,128)S(1)}, u32[]{:S(2)}, u32[]{:S(2)}) %collective-permute-start.1) | collective-permute-done | bytes 245792 | tf_op jit(solution)/shard_map/ppermute | solution.py:562
  21.5 1.3 collective-permute-start.3
  22.8 3.1 collective-permute-start.2
  25.9 12.7 %edges.1 = (f32[96,128]{1,0:T(8,128)}, f32[96,128]{1,0:T(8,128)}, f32[2,48,512]{2,1,0:T(8,128)}, f32[3,48,512]{2,1,0:T(8,128)}) custom-call(f32[41,96,512]{2,1,0:T(8,128)} %u.1, f32[41,96,512]{2,1,0:T(8,128)} %u.1, f32[41,96,512]{2,1,0:T(8,128)} %v.1, f32[41,96,512]{2,1,0:T(8,128)} %v.1, f32[41,96,512]{2,1,0:T(8,128)} %tf.1, f32[41,96,512]{2,1,0:T(8,128)} %sf.1, ...), custom_call_target="tpu_custom_call" | custom-call | flops 10000000 | bytes 16000000 | tf_op jit(solution)/shard_map/edges/pallas_call | solution.py:120
  38.6 1.3 collective-permute-start.4
  39.9 1.3 collective-permute-start.7
  41.2 0.7 slice.37
  41.9 1.3 collective-permute-start.5
  43.2 22.0 %tracers.1 = (f32[12,41,8,512]{3,2,1,0:T(8,128)}, f32[12,41,8,512]{3,2,1,0:T(8,128)}, f32[12,41,8,512]{3,2,1,0:T(8,128)}, f32[96,128]{1,0:T(8,128)}, f32[96,128]...) custom-call(f32[41,96,512]{2,1,0:T(8,128)} %tf.1, f32[41,96,512]{2,1,0:T(8,128)} %sf.1, s32[96,512]{1,0:T(8,128)} %kc.5, ...), custom_call_target="tpu_custom_call" | custom-call | flops 100000000 | bytes 40000000 | tf_op jit(solution)/shard_map/tracers/pallas_call | solution.py:206
  65.2 0.7 slice.38
  65.9 1.6 collective-permute-start.6
  67.5 0.6 copy-done.8
  68.1 3.7 %collective-permute-start.8 = (f32[2,48,512]{2,1,0:T(8,128)}, f32[2,48,512]{2,1,0:T(8,128)S(1)}, u32[]{:S(2)}, u32[]{:S(2)}) collective-permute-start(f32[2,48,512]{2,1,0:T(8,128)} %get-tuple-element.48), channel_id=1, source_target_pairs={{0,1},{1,2},{2,3},{4,5},{5,6},{6,7},{8,9},{9,10},{10,11},{12,13},{... | collective-permute-start | bytes 589832 | tf_op jit(solution)/shard_map/ppermute | solution.py:562
  71.8 1.4 pad_maximum_fusion.10.rwn
  73.3 5.0 %collective-permute-start.9 = (f32[8,128]{1,0:T(8,128)S(1)}, f32[8,128]{1,0:T(8,128)S(1)}, u32[]{:S(2)}, u32[]{:S(2)}) collective-permute-start(f32[8,128]{1,0:T(8,128)S(1)} %slice.38), channel_id=1, source_target_pairs={{0,13},{1,14},{2,15},{4,1},{5,2},{6,3},{8,5},{9,6},{10,7},{12,9},{... | collective-permute-start | bytes 12296 | tf_op jit(solution)/shard_map/ppermute | solution.py:562
  78.2 1.6 pad_maximum_fusion.pl5.planes
  79.8 3.0 geometry.1
  82.9 0.5 copy-done.9
  83.5 0.1 copy-done.2
  83.6 51.0 %momentum.1 = (f32[12,41,8,512]{3,2,1,0:T(8,128)}, f32[12,41,8,512]{3,2,1,0:T(8,128)}, f32[96,512]{1,0:T(8,128)}, f32[96,512]{1,0:T(8,128)}, f32[96,512]{1,0:T(8...) custom-call(f32[41,96,512]{2,1,0:T(8,128)} %u.1, f32[41,96,512]{2,1,0:T(8,128)} %v.1, ...), custom_call_target="tpu_custom_call" | custom-call | flops 200000000 | bytes 64000000 | tf_op jit(solution)/shard_map/momentum/pallas_call | solution.py:386
  134.5 0.9 pad_maximum_fusion.8
  135.4 1.2 collective-permute-start.10
  136.7 0.8 collective-permute-start.11
  137.5 1.0 slice_bitcast_fusion
  138.5 1.3 collective-permute-start.16
  139.8 0.8 collective-permute-done.10
  140.6 2.1 collective-permute-done.11
  142.7 1.0 pad_maximum_fusion.7
  143.8 1.3 collective-permute-start.13
  145.1 3.0 collective-permute-start.12
  148.1 0.9 pad_maximum_fusion.4
  149.0 2.3 collective-permute-start.17
  151.4 2.2 collective-permute-start.15
  153.6 0.7 copy.17.tide
  154.3 0.8 add.3
  155.1 2.0 pad_maximum_fusion.1.force
  157.1 26.9 %subcycles.1 = (f32[96,512]{1,0:T(8,128)}, f32[96,512]{1,0:T(8,128)}, f32[96,512]{1,0:T(8,128)}, f32[104,640]{1,0:T(8,128)}, f32[104,640]{1,0:T(8,128)}) custom-call(f32[5,176,640]{2,1,0:T(8,128)} %pad_maximum_fusion.pl5.planes, f32[176,640]{1,0:T(8,128)} %get-tuple-element.39.kun.kux.kus.ku, f32[176,640]{1,0:T(8,128)} %get-tuple-element.40.kvn.kvx.kvs.kv, ...), custom_call_target="tpu_custom_call" | custom-call | flops 100000000 | bytes 1000000 | tf_op jit(solution)/shard_map/subcycles/pallas_call | solution.py:462
  184.1 0.5 copy-done.5
  184.6 0.1 copy-done
  184.8 0.1 copy-done.1
  184.9 121.9 %finish.1 = (f32[41,96,512]{2,1,0:T(8,128)}, f32[41,96,512]{2,1,0:T(8,128)}, f32[41,96,512]{2,1,0:T(8,128)}, f32[41,96,512]{2,1,0:T(8,128)}) custom-call(f32[12,41,8,512]{3,2,1,0:T(8,128)} %get-tuple-element.54.us_b, f32[12,41,8,512]{3,2,1,0:T(8,128)} %get-tuple-element.55.vs_b, f32[12,41,8,512]{3,2,1,0:T(8,128)} %get-tuple-element.56.t_b, ...), custom_call_target="tpu_custom_call" | custom-call | flops 100000000 | bytes 80000000 | tf_op jit(solution)/shard_map/finish/pallas_call | solution.py:540
  (39 shorter events, 0.4 us)
Async XLA Ops:
  5.4 10.8 %collective-permute-start = (f32[5,96,128]{2,1,0:T(8,128)S(1)}, f32[5,96,128]{2,1,0:T(8,128)S(1)}, u32[]{:S(2)}, u32[]{:S(2)}) collective-permute-start(f32[5,96,128]{2,1,0:T(8,128)S(1)} %get-tuple-element.74), channel_id=1, source_target_pairs={{0,12},{1,13},{2,14},{3,15},{4,0},{5,1},{6,2},{7,3},{8,4},{9,5},{1... | collective-permute-start | bytes 737288 | tf_op jit(solution)/shard_map/ppermute | solution.py:562
  9.7 11.7 %collective-permute-start.1 = (f32[5,96,128]{2,1,0:T(8,128)S(1)}, f32[5,96,128]{2,1,0:T(8,128)S(1)}, u32[]{:S(2)}, u32[]{:S(2)}) collective-permute-start(f32[5,96,128]{2,1,0:T(8,128)S(1)} %get-tuple-element.73), channel_id=1, source_target_pairs={{0,4},{1,5},{2,6},{3,7},{4,8},{5,9},{6,10},{7,11},{8,12},{9,13},{1... | collective-permute-start | bytes 737288 | tf_op jit(solution)/shard_map/ppermute | solution.py:562
  21.5 51.8 %collective-permute-start.3 = (f32[5,40,640]{2,1,0:T(8,128)S(1)}, f32[5,40,640]{2,1,0:T(8,128)S(1)}, u32[]{:S(2)}, u32[]{:S(2)}) collective-permute-start(f32[5,40,640]{2,1,0:T(8,128)S(1)} %get-tuple-element.72), channel_id=1, source_target_pairs={{1,0},{2,1},{3,2},{5,4},{6,5},{7,6},{9,8},{10,9},{11,10},{13,12},{... | collective-permute-start | bytes 1536008 | tf_op jit(solution)/shard_map/ppermute | solution.py:562
  22.8 55.4 %collective-permute-start.2 = (f32[5,40,640]{2,1,0:T(8,128)S(1)}, f32[5,40,640]{2,1,0:T(8,128)S(1)}, u32[]{:S(2)}, u32[]{:S(2)}) collective-permute-start(f32[5,40,640]{2,1,0:T(8,128)S(1)} %get-tuple-element.71), channel_id=1, source_target_pairs={{0,1},{1,2},{2,3},{4,5},{5,6},{6,7},{8,9},{9,10},{10,11},{12,13},{... | collective-permute-start | bytes 1536008 | tf_op jit(solution)/shard_map/ppermute | solution.py:562
  38.6 29.0 %collective-permute-start.4 = (f32[96,128]{1,0:T(8,128)}, f32[96,128]{1,0:T(8,128)S(1)}, u32[]{:S(2)}, u32[]{:S(2)}) collective-permute-start(f32[96,128]{1,0:T(8,128)} %get-tuple-element.45), channel_id=1, source_target_pairs={{0,4},{1,5},{2,6},{3,7},{4,8},{5,9},{6,10},{7,11},{8,12},{9,13},{1... | collective-permute-start | bytes 147464 | tf_op jit(solution)/shard_map/ppermute | solution.py:562
  39.9 43.0 %collective-permute-start.7 = (f32[3,48,512]{2,1,0:T(8,128)}, f32[3,48,512]{2,1,0:T(8,128)}, u32[]{:S(2)}, u32[]{:S(2)}) collective-permute-start(f32[3,48,512]{2,1,0:T(8,128)} %get-tuple-element.47.rown), channel_id=1, source_target_pairs={{1,0},{2,1},{3,2},{5,4},{6,5},{7,6},{9,8},{10,9},{11,10},{13,12},{... | collective-permute-start | bytes 884744 | tf_op jit(solution)/shard_map/ppermute | solution.py:562
  41.9 24.0 %collective-permute-start.5 = (f32[8,128]{1,0:T(8,128)S(1)}, f32[8,128]{1,0:T(8,128)S(1)}, u32[]{:S(2)}, u32[]{:S(2)}) collective-permute-start(f32[8,128]{1,0:T(8,128)S(1)} %slice.37), channel_id=1, source_target_pairs={{1,4},{2,5},{3,6},{5,8},{6,9},{7,10},{9,12},{10,13},{11,14},{13,0}... | collective-permute-start | bytes 12296 | tf_op jit(solution)/shard_map/ppermute | solution.py:562
  65.9 17.0 %collective-permute-start.6 = (f32[96,128]{1,0:T(8,128)}, f32[96,128]{1,0:T(8,128)S(1)}, u32[]{:S(2)}, u32[]{:S(2)}) collective-permute-start(f32[96,128]{1,0:T(8,128)} %get-tuple-element.46), channel_id=1, source_target_pairs={{0,12},{1,13},{2,14},{3,15},{4,0},{5,1},{6,2},{7,3},{8,4},{9,5},{1... | collective-permute-start | bytes 147464 | tf_op jit(solution)/shard_map/ppermute | solution.py:562
  67.5 0.6 copy-start.8
  68.1 14.7 %collective-permute-start.8 = (f32[2,48,512]{2,1,0:T(8,128)}, f32[2,48,512]{2,1,0:T(8,128)S(1)}, u32[]{:S(2)}, u32[]{:S(2)}) collective-permute-start(f32[2,48,512]{2,1,0:T(8,128)} %get-tuple-element.48), channel_id=1, source_target_pairs={{0,1},{1,2},{2,3},{4,5},{5,6},{6,7},{8,9},{9,10},{10,11},{12,13},{... | collective-permute-start | bytes 589832 | tf_op jit(solution)/shard_map/ppermute | solution.py:562
  73.3 9.6 %collective-permute-start.9 = (f32[8,128]{1,0:T(8,128)S(1)}, f32[8,128]{1,0:T(8,128)S(1)}, u32[]{:S(2)}, u32[]{:S(2)}) collective-permute-start(f32[8,128]{1,0:T(8,128)S(1)} %slice.38), channel_id=1, source_target_pairs={{0,13},{1,14},{2,15},{4,1},{5,2},{6,3},{8,5},{9,6},{10,7},{12,9},{... | collective-permute-start | bytes 12296 | tf_op jit(solution)/shard_map/ppermute | solution.py:562
  82.9 0.6 copy-start.9
  82.9 0.6 copy-start.3
  82.9 0.7 copy-start.2
  83.6 64.6 %copy-start.4 = (f32[2,48,512]{2,1,0:T(8,128)S(1)}, f32[2,48,512]{2,1,0:T(8,128)}, u32[]{:S(2)}) copy-start(f32[2,48,512]{2,1,0:T(8,128)} %get-tuple-element.66) | copy-start | bytes 589828
  83.6 67.8 %copy-start.11 = (f32[96,128]{1,0:T(8,128)S(1)}, f32[96,128]{1,0:T(8,128)}, u32[]{:S(2)}) copy-start(f32[96,128]{1,0:T(8,128)} %get-tuple-element.64) | copy-start | bytes 147460
  83.6 70.0 %copy-start.10 = (f32[36,2]{0,1:T(2,128)S(1)}, f32[36,2]{0,1:T(2,128)}, u32[]{:S(2)}) copy-start(f32[36,2]{0,1:T(2,128)} %param.19) | copy-start | bytes 868
  83.6 70.7 %copy-start.7 = (f32[96,128]{1,0:T(8,128)S(1)}, f32[96,128]{1,0:T(8,128)}, u32[]{:S(2)}) copy-start(f32[96,128]{1,0:T(8,128)} %get-tuple-element.62) | copy-start | bytes 147460
  135.4 5.2 %collective-permute-start.10 = (f32[2,96,128]{2,1,0:T(8,128)S(1)}, f32[2,96,128]{2,1,0:T(8,128)S(1)}, u32[]{:S(2)}, u32[]{:S(2)}) collective-permute-start(f32[2,96,128]{2,1,0:T(8,128)S(1)} %get-tuple-element.78), channel_id=1, source_target_pairs={{0,12},{1,13},{2,14},{3,15},{4,0},{5,1},{6,2},{7,3},{8,4},{9,5},{1... | collective-permute-start | bytes 294920 | tf_op jit(solution)/shard_map/ppermute | solution.py:562
  136.7 6.0 %collective-permute-start.11 = (f32[2,96,128]{2,1,0:T(8,128)S(1)}, f32[2,96,128]{2,1,0:T(8,128)S(1)}, u32[]{:S(2)}, u32[]{:S(2)}) collective-permute-start(f32[2,96,128]{2,1,0:T(8,128)S(1)} %get-tuple-element.77), channel_id=1, source_target_pairs={{0,4},{1,5},{2,6},{3,7},{4,8},{5,9},{6,10},{7,11},{8,12},{9,13},{1... | collective-permute-start | bytes 294920 | tf_op jit(solution)/shard_map/ppermute | solution.py:562
  138.5 45.5 %collective-permute-start.16 = (f32[3,48,512]{2,1,0:T(8,128)S(1)}, f32[3,48,512]{2,1,0:T(8,128)S(1)}, u32[]{:S(2)}, u32[]{:S(2)}) collective-permute-start(f32[3,48,512]{2,1,0:T(8,128)S(1)} %slice_bitcast_fusion), channel_id=1, source_target_pairs={{1,0},{2,1},{3,2},{5,4},{6,5},{7,6},{9,8},{10,9},{11,10},{13,12},{... | collective-permute-start | bytes 884744 | tf_op jit(solution)/shard_map/ppermute | solution.py:562
  143.8 11.3 %collective-permute-start.13 = (f32[2,40,640]{2,1,0:T(8,128)S(1)}, f32[2,40,640]{2,1,0:T(8,128)S(1)}, u32[]{:S(2)}, u32[]{:S(2)}) collective-permute-start(f32[2,40,640]{2,1,0:T(8,128)S(1)} %get-tuple-element.76), channel_id=1, source_target_pairs={{1,0},{2,1},{3,2},{5,4},{6,5},{7,6},{9,8},{10,9},{11,10},{13,12},{... | collective-permute-start | bytes 614408 | tf_op jit(solution)/shard_map/ppermute | solution.py:562
  145.1 10.1 %collective-permute-start.12 = (f32[2,40,640]{2,1,0:T(8,128)S(1)}, f32[2,40,640]{2,1,0:T(8,128)S(1)}, u32[]{:S(2)}, u32[]{:S(2)}) collective-permute-start(f32[2,40,640]{2,1,0:T(8,128)S(1)} %get-tuple-element.75), channel_id=1, source_target_pairs={{0,1},{1,2},{2,3},{4,5},{5,6},{6,7},{8,9},{9,10},{10,11},{12,13},{... | collective-permute-start | bytes 614408 | tf_op jit(solution)/shard_map/ppermute | solution.py:562
  149.0 35.0 %collective-permute-start.17 = (f32[3,48,512]{2,1,0:T(8,128)S(1)}, f32[3,48,512]{2,1,0:T(8,128)S(1)}, u32[]{:S(2)}, u32[]{:S(2)}) collective-permute-start(f32[3,48,512]{2,1,0:T(8,128)S(1)} %pad_maximum_fusion.4), channel_id=1, source_target_pairs={{0,1},{1,2},{2,3},{4,5},{5,6},{6,7},{8,9},{9,10},{10,11},{12,13},{... | collective-permute-start | bytes 884744 | tf_op jit(solution)/shard_map/ppermute | solution.py:562
  151.4 32.6 %collective-permute-start.15 = (f32[96,128]{1,0:T(8,128)S(1)}, f32[96,128]{1,0:T(8,128)S(1)}, u32[]{:S(2)}, u32[]{:S(2)}) collective-permute-start(f32[96,128]{1,0:T(8,128)S(1)} %copy-done.11), channel_id=1, source_target_pairs={{0,12},{1,13},{2,14},{3,15},{4,0},{5,1},{6,2},{7,3},{8,4},{9,5},{1... | collective-permute-start | bytes 147464 | tf_op jit(solution)/shard_map/ppermute | solution.py:562
  155.1 29.0 %collective-permute-start.14 = (f32[96,128]{1,0:T(8,128)S(1)}, f32[96,128]{1,0:T(8,128)S(1)}, u32[]{:S(2)}, u32[]{:S(2)}) collective-permute-start(f32[96,128]{1,0:T(8,128)S(1)} %add.3), channel_id=1, source_target_pairs={{0,4},{1,5},{2,6},{3,7},{4,8},{5,9},{6,10},{7,11},{8,12},{9,13},{1... | collective-permute-start | bytes 147464 | tf_op jit(solution)/shard_map/ppermute | solution.py:562
  184.0 0.6 copy-start.5
  184.0 0.7 copy-start
  184.0 0.7 copy-start.6
  184.1 0.8 copy-start.1

commit v3 on v2

--- a/solution.py
+++ b/solution.py
@@ -17,6 +17,8 @@
 EC = NC + 128
 NB = NR // 8
 SUB = 36
+GROUP = 2
+TILES = 3
 DT = 4.0
 DTB = DT / SUB
 KV = 0.001
@@ -59,6 +61,16 @@
 
 def down_row(x, prev, row):
     return pltpu.roll(jnp.where(row == 7, prev, x), 1, axis=0)
+
+
+def skewed(stages, group, count=NL):
+    blocks = [range(k, min(k + group, count)) for k in range(0, count, group)]
+    held = {}
+    for i in range(len(blocks) + len(stages) - 1):
+        for n, stage in enumerate(stages):
+            if 0 <= i - n < len(blocks):
+                for k in blocks[i - n]:
+                    held[k] = stage(k, held[k]) if n else stage(k)
 
 
 def couple(count, thick, kappa):
@@ -135,11 +147,24 @@
 
 
 def tracer_kernel(t, s, kc, hc, tm_b, sm_b, pr_b, pke, pkw, rn, rs_b, gains):
-    tm, sm, pr, rs = tm_b.at[0], sm_b.at[0], pr_b.at[0], rs_b.at[0]
     b = pl.program_id(0)
+    for half in range(2):
+        sl = tile_rows(half)
+        tm, sm, rs = tm_b.at[half], sm_b.at[half], rs_b.at[half]
+        mix_tracers(t.at[:, sl, :], s.at[:, sl, :], kc[sl, :], hc[sl, :], tm, sm, pr_b.at[half], pke.at[sl, :], pkw.at[sl, :], rs, gains)
+
+    @pl.when(b == NB // 2 - 1)
+    def _():
+        for k in range(NL):
+            rn[0, k : k + 1, :] = tm[k, 7:8, :]
+            rn[1, k : k + 1, :] = sm[k, 7:8, :]
+        for i in range(2):
+            rn[i, NL:LP, :] = jnp.zeros((LP - NL, NC), F32)
+
+
+def mix_tracers(t, s, cnt, depth, tm, sm, pr, pke, pkw, rs, gains):
     lane = iota(TILE, 1)
-    cnt = kc[:]
-    thick = hc[:] / jnp.maximum(cnt, 1).astype(F32)
+    thick = depth / jnp.maximum(cnt, 1).astype(F32)
     c = couple(cnt, thick, KT)
     zero = jnp.zeros(ROW, F32)
     cum = lower = pt = ps = zero
@@ -177,37 +202,29 @@
     pke[:] = ae
     pkw[:] = aw
 
-    @pl.when(b == NB - 1)
-    def _():
-        for k in range(NL):
-            rn[0, k : k + 1, :] = tm[k, 7:8, :]
-            rn[1, k : k + 1, :] = sm[k, 7:8, :]
-        for i in range(2):
-            rn[i, NL:LP, :] = jnp.zeros((LP - NL, NC), F32)
-
 
 PACK = jax.ShapeDtypeStruct((NB,) + SLAB, F32)
 
 
-def block_major(f):
-    return pl.BlockSpec((1,) + SLAB, lambda b: (f(b), 0, 0, 0))
-
-
-def first_rows(f):
-    return pl.BlockSpec((1, 3, LP, NC), lambda b: (f(b), 0, 0, 0))
+def block_major(f, n=1):
+    return pl.BlockSpec((n,) + SLAB, lambda b: (f(b), 0, 0, 0))
+
+
+def first_rows(f, n=1):
+    return pl.BlockSpec((n, 3, LP, NC), lambda b: (f(b), 0, 0, 0))
 
 
 def tracers(t, s, kmt, depth):
-    cube = pl.BlockSpec(SLAB, lambda b: (0, b, 0))
-    pack = block_major(lambda b: b)
-    plane = pl.BlockSpec(ROW, lambda b: (b, 0))
-    col = pl.BlockSpec(TILE, lambda b: (b, 0))
+    cube = pl.BlockSpec((NL, 16, NC), lambda b: (0, b, 0))
+    pack = block_major(lambda b: b, 2)
+    plane = pl.BlockSpec((16, NC), lambda b: (b, 0))
+    col = pl.BlockSpec((16, LN), lambda b: (b, 0))
     rows = pl.BlockSpec((2, LP, NC), lambda b: (0, 0, 0))
     return pl.pallas_call(
         tracer_kernel,
-        grid=(NB,),
+        grid=(NB // 2,),
         in_specs=[cube, cube, plane, plane],
-        out_specs=[pack, pack, pack, col, col, rows, first_rows(lambda b: b)],
+        out_specs=[pack, pack, pack, col, col, rows, first_rows(lambda b: b, 2)],
         out_shape=[PACK, PACK, PACK] + [jax.ShapeDtypeStruct((NR, LN), F32)] * 2 + [jax.ShapeDtypeStruct((2, LP, NC), F32), jax.ShapeDtypeStruct((NB, 3, LP, NC), F32)],
         scratch_shapes=[VM(SLAB, F32)],
         compiler_params=pltpu.CompilerParams(dimension_semantics=("arbitrary",)),
@@ -278,16 +295,19 @@
     kxn, kyn = kun[:], kvn[:]
     rwv, rev = rwn[:], ren[:]
 
-    def masked(k, uk, vk):
+    def halos(k):
         hu = jnp.where(lane == 0, lane_to(rev, k, 0), lane_to(rwv, k, LN - 1))
         hv = jnp.where(lane == 0, lane_to(rev, NL + k, 0), lane_to(rwv, NL + k, LN - 1))
-        um = only(k < kxn, jnp.concatenate([uk, hu], axis=1))
-        return um, only(k < kyn, jnp.concatenate([vk, hv], axis=1))
+        return hu, hv
+
+    def masked(k, uk, vk, halo):
+        um = only(k < kxn, jnp.concatenate([uk, halo[0]], axis=1))
+        return um, only(k < kyn, jnp.concatenate([vk, halo[1]], axis=1))
 
     @pl.when(step == 0)
     def _():
         for k in range(NL):
-            ums[k], vms[k] = masked(k, u[k], v[k])
+            ums[k], vms[k] = masked(k, u[k], v[k], halos(k))
         lev = iota((LP, NC), 0).astype(F32)
         lev1 = iota((LP, LN), 0)
         ks, kw = kus[7:8, :NC], kvs[7:8, :NC]
@@ -310,39 +330,47 @@
     def _():
         kx, ky = kux[:], kvx[:]
         pev = re[:]
-        zx = jnp.zeros(ROW, F32)
-        ax, ay = zx, zx
-        for k in range(NL):
+        total = [jnp.zeros(ROW, F32)] * 2
+
+        def edge(k):
+            return halos(k) + (lane_to(pev, 2 * NL + k, 0),)
+
+        def shift(k, halo):
             um, vm = ums[k], vms[k]
-            pe = jnp.concatenate([p[k], lane_to(pev, 2 * NL + k, 0)], axis=1)
             uk = jnp.where(last, rnorth[0, k : k + 1, :], u[k])
             vk = jnp.where(last, rnorth[1, k : k + 1, :], v[k])
-            np_ = jnp.where(last, rnorth[2, k : k + 1, :], pfirst[0, 2, k : k + 1, :])
-            nu, nv = masked(k, uk, vk)
-            ums[k], vms[k] = nu, nv
-            u_n = up_row(um, nu, rowx)
-            c = 0.25 * ((vm + from_east(vm)) * (um + u_n))
-            g = from_west(um) + um
+            pe = jnp.concatenate([p[k], halo[2]], axis=1)
+            return masked(k, uk, vk, halo), pe, from_west(um), from_east(vm)
+
+        def flux(k, arg):
+            new, pe, u_w, v_e = arg
+            um, vm = ums[k], vms[k]
+            c = 0.25 * ((vm + v_e) * (um + up_row(um, new[0], rowx)))
+            g = u_w + um
             g = 0.25 * (g * g) + pe
-            ge = from_east(g)[:, :NC]
-            v5 = vm[:, :NC]
-            h = v5 + up_row(v5, nv[:, :NC], row)
-            h = 0.25 * (h * h) + up_row(pe[:, :NC], np_, row)
-            cw = from_west(c)[:, :NC]
             c5 = c[:, :NC]
-            tu = (ge - g[:, :NC]) + (c5 - down_row(c5, cc[k], row))
-            tv = (h - down_row(h, hh[k], row)) + (c5 - cw)
-            tu = only(k < kx, tu)
-            tv = only(k < ky, tv)
-            ax += tu
-            ay += tv
-            srcu[k] = um[:, :NC] - DT * tu
+            return new, from_east(g)[:, :NC] - g[:, :NC], c5, c5 - from_west(c)[:, :NC]
+
+        def tend(k, arg):
+            new, dx, c5, dc = arg
+            u5, v5, pk = ums[k, :, :NC], vms[k, :, :NC], p[k]
+            north = jnp.where(last, rnorth[2, k : k + 1, :], pfirst[0, 2, k : k + 1, :])
+            h = v5 + up_row(v5, new[1][:, :NC], row)
+            h = 0.25 * (h * h) + up_row(pk, north, row)
+            tu = only(k < kx, dx + (c5 - down_row(c5, cc[k], row)))
+            tv = only(k < ky, (h - down_row(h, hh[k], row)) + dc)
+            total[0] += tu
+            total[1] += tv
+            srcu[k] = u5 - DT * tu
             srcv[k] = v5 - DT * tv
             cc[k] = c5
             hh[k] = h
+            ums[k], vms[k] = new
+
+        skewed((edge, shift, flux, tend), GROUP)
         dzu, dzv = du[:], dv[:]
-        fx[:] = -dzu * ax
-        fy[:] = -dzv * ay
+        fx[:] = -dzu * total[0]
+        fy[:] = -dzv * total[1]
         sa, sb = solve_pair(srcu, srcv, couple(kx, dzu, KV), couple(ky, dzv, KV), kx, ky, us, vs, gu, gv)
         sa, sb = dzu * sa, dzv * sb
         su[:] = sa
@@ -418,30 +446,40 @@
         def step(n, _):
             tx, ty = tide[n, 0], tide[n, 1]
             w = norm * ((n + 1) * (SUB - n)).astype(F32)
-            prev_eta = None
-            vsouth = tv[8 * lo - 8 : 8 * lo, :] if lo else zero
-            for i in range(lo, hi):
+
+            def west(i):
+                return from_west(tu[tile_rows(i), :])
+
+            def surface(i, u_w):
                 sl = tile_rows(i)
-                un, vn = tu[sl, :], tv[sl, :]
-                e = eta[sl, :] - DTB * ((un - from_west(un)) + (vn - down_row(vn, vsouth, row)))
+                vn = tv[sl, :]
+                south = tv[tile_rows(i - 1), :] if i else zero
+                e = eta[sl, :] - DTB * ((tu[sl, :] - u_w) + (vn - down_row(vn, south, row)))
                 eta[sl, :] = e
-                un = un + (cu[sl, :] * (tx - (from_east(e) - e)) + fu[sl, :])
+                return from_east(e)
+
+            def update(i, e_e):
+                sl = tile_rows(i)
+                e = eta[sl, :]
+                un = tu[sl, :] + (cu[sl, :] * (tx - (e_e - e)) + fu[sl, :])
                 tu[sl, :] = un
                 if lo_bar <= i < hi_bar:
                     ub[sl, :] = ub[sl, :] + w * un
                 if i > lo:
-                    finish(i - 1, prev_eta, e, vsouth, ty, w)
-                prev_eta, vsouth = e, vn
-            finish(hi - 1, prev_eta, prev_eta, vsouth, ty, w)
+                    north(i - 1, e, ty, w)
+
+            skewed((lambda i: west(lo + i), lambda i, x: surface(lo + i, x), lambda i, x: update(lo + i, x)), TILES, hi - lo)
+            north(hi - 1, eta[tile_rows(hi - 1), :], ty, w)
             return 0
 
         lax.fori_loop(first, last, step, 0)
 
     lo_bar, hi_bar = HT - 1, HT + NB
 
-    def finish(i, e, north, vold, ty, w):
+    def north(i, ahead, ty, w):
         sl = tile_rows(i)
-        x = vold + (cv[sl, :] * (ty - (up_row(e, north, row) - e)) + fv[sl, :])
+        e = eta[sl, :]
+        x = tv[sl, :] + (cv[sl, :] * (ty - (up_row(e, ahead, row) - e)) + fv[sl, :])
         tv[sl, :] = x
         if lo_bar <= i < hi_bar:
             vb[sl, :] = vb[sl, :] + w * x
@@ -501,25 +539,39 @@
     tot = jnp.concatenate([su[:], lane_to(rwv, 3 * NL, LN - 1)], axis=1)
     cx = correction(ub[:], tot, kx, du[:])
     cy = correction(vb[:, :NC], sv[:], ky, dv[:, :NC])
-    for k in range(NL):
-        ue = jnp.concatenate([us[k], lane_to(rwv, k, LN - 1)], axis=1)
-        ue = only(k < kx, ue + cx)
+    fields = ((t, to, ct), (s, so, cs))
+
+    def load(k):
+        out = [lane_to(rwv, k, LN - 1)]
+        for i in range(2):
+            base = NL * (i + 1) + k
+            out.append(jnp.where(lane == 0, lane_to(rev, base, 0), lane_to(rwv, base, LN - 1)))
+        return out
+
+    def east(k, halo):
+        wide = [jnp.concatenate([f[0][k], h], axis=1) for f, h in zip(fields, halo[1:])]
+        return halo[0], [x + from_east(x) for x in wide]
+
+    def flux(k, arg):
+        halo, sums = arg
+        ue = only(k < kx, jnp.concatenate([us[k], halo], axis=1) + cx)
         uo[k] = ue[:, :NC]
+        f = [(0.5 * DT) * ue * x for x in sums]
+        return [(x - from_west(x))[:, :NC] for x in f]
+
+    def store(k, div):
         ve = only(k < ky, vs[k] + cy)
         vo[k] = ve
-        hx, hy = (0.5 * DT) * ue, (0.5 * DT) * ve
-        wet = k < cnt
-        for i, (x, out, carry) in enumerate(((t, to, ct), (s, so, cs))):
-            base = NL * (i + 1) + k
-            halo = jnp.where(lane == 0, lane_to(rev, base, 0), lane_to(rwv, base, LN - 1))
+        hy = (0.5 * DT) * ve
+        for i, (x, out, carry) in enumerate(fields):
             own = x[k]
-            xe = jnp.concatenate([own, halo], axis=1)
-            f = hx * (xe + from_east(xe))
             north = jnp.where(last, rnorth[i, k : k + 1, :], first[0, i, k : k + 1, :])
             fy = hy * (own + up_row(own, north, row))
-            div = (f - from_west(f))[:, :NC] + (fy - down_row(fy, carry[k], row))
+            new = own - (div[i] + (fy - down_row(fy, carry[k], row)))
             carry[k] = fy
-            out[k] = only(wet, own - div)
+            out[k] = only(k < cnt, new)
+
+    skewed((load, east, flux, store), GROUP)
 
 
 def finish(us, vs, tm, sm, first, kmt, geo, ub, vb, su, sv, rw, re, rnorth, rsouth):

time: 308 us -> 185 us (0.60)
  Pallas kernels: 237 us -> 114 us
    pallas_call x1, Pallas kernels: 122 us -> 31.3 us  [finish(): pl.pallas_call(finish_kernel, grid=(NB,), in_specs=[pack, pack, pack, pac...]
    pallas_call x1, Pallas kernels: 51 us -> 30.5 us  [momentum(): pl.pallas_call(momentum_kernel, grid=(NB + 1,), in_specs=[cube, cube, pac...]
    pallas_call x1, Pallas kernels: 26.9 us -> 16.8 us  [subcycles(): pl.pallas_call(subcycle_kernel, in_specs=[vm] * 6 + [pl.BlockSpec(memory_...]
  transfers between devices with their start and end apart: 18 -> 18, of which waited for: 4 -> 4; matrix products, arithmetic and copies ran while one was open for 4% -> 6% of each run, Pallas kernels for 21% -> 29%
where the time goes in v3:
time: 185 us; the launch traced here: 184 us
  Pallas kernels  114 us (62%)
  starting transfers between devices  34.9 us (19%)
  waiting for transfers between devices  14.6 us (8%)
  other arithmetic  9.7 us (5%)
  local copies, waits for them, and re-layouts  8.96 us (5%)
    ppermute x18, starting transfers between devices, send(): return lax.ppermute(x, ('col', 'row'), pairs)  34.9 us
    pallas_call x1, Pallas kernels, finish(): pl.pallas_call(finish_kernel, grid=(NB,), in_specs=[pack, pack, pack, pac...  31.3 us
    pallas_call x1, Pallas kernels, momentum(): pl.pallas_call(momentum_kernel, grid=(NB + 1,), in_specs=[cube, cube, pac...  30.5 us
    pallas_call x1, Pallas kernels, tracers(): pl.pallas_call(tracer_kernel, grid=(NB // 2,), in_specs=[cube, cube, plan...  20.1 us
    pallas_call x1, Pallas kernels, subcycles(): pl.pallas_call(subcycle_kernel, in_specs=[vm] * 6 + [pl.BlockSpec(memory_...  16.8 us
    ppermute x18, waiting for transfers between devices, send(): return lax.ppermute(x, ('col', 'row'), pairs)  14.6 us
    pallas_call x1, Pallas kernels, edges(): pl.pallas_call(edge_kernel, grid=(NB,), in_specs=[strip(0), strip(3), str...  12.7 us
    unnamed x28, local copies, waits for them, and re-layouts  5.62 us
  transfers between devices with their start and end apart: 18, of which 4 were waited for; matrix products, arithmetic and copies ran while one was open for 6% of the time, Pallas kernels for 29%

profile of v3, /device:TPU:0, one launch (start us, length us, event | category | flops | bytes accessed | tf_op | source)
XLA Modules:
  0.0 183.6 jit_solution(11462214896124433018)
XLA Ops:
  0.6 0.9 bitcast_dynamic-update-slice_fusion.4
  1.6 0.9 bitcast_dynamic-update-slice_fusion.3
  2.5 0.9 bitcast_dynamic-update-slice_fusion.2
  3.5 0.9 bitcast_dynamic-update-slice_fusion.1
  4.4 0.9 bitcast_dynamic-update-slice_fusion
  5.4 4.3 %collective-permute-start = (f32[5,96,128]{2,1,0:T(8,128)S(1)}, f32[5,96,128]{2,1,0:T(8,128)S(1)}, u32[]{:S(2)}, u32[]{:S(2)}) collective-permute-start(f32[5,96,128]{2,1,0:T(8,128)S(1)} %get-tuple-element.74), channel_id=1, source_target_pairs={{0,12},{1,13},{2,14},{3,15},{4,0},{5,1},{6,2},{7,3},{8,4},{9,5},{1... | collective-permute-start | bytes 737288 | tf_op jit(solution)/shard_map/ppermute | solution.py:614
  9.7 6.4 %collective-permute-done = f32[5,96,128]{2,1,0:T(8,128)S(1)} collective-permute-done((f32[5,96,128]{2,1,0:T(8,128)S(1)}, f32[5,96,128]{2,1,0:T(8,128)S(1)}, u32[]{:S(2)}, u32[]{:S(2)}) %collective-permute-start) | collective-permute-done | bytes 245792 | tf_op jit(solution)/shard_map/ppermute | solution.py:614
  16.2 5.2 %collective-permute-done.1 = f32[5,96,128]{2,1,0:T(8,128)S(1)} collective-permute-done((f32[5,96,128]{2,1,0:T(8,128)S(1)}, f32[5,96,128]{2,1,0:T(8,128)S(1)}, u32[]{:S(2)}, u32[]{:S(2)}) %collective-permute-start.1) | collective-permute-done | bytes 245792 | tf_op jit(solution)/shard_map/ppermute | solution.py:614
  21.5 1.3 collective-permute-start.3
  22.8 3.1 %collective-permute-start.2 = (f32[5,40,640]{2,1,0:T(8,128)S(1)}, f32[5,40,640]{2,1,0:T(8,128)S(1)}, u32[]{:S(2)}, u32[]{:S(2)}) collective-permute-start(f32[5,40,640]{2,1,0:T(8,128)S(1)} %get-tuple-element.71), channel_id=1, source_target_pairs={{0,1},{1,2},{2,3},{4,5},{5,6},{6,7},{8,9},{9,10},{10,11},{12,13},{... | collective-permute-start | bytes 1536008 | tf_op jit(solution)/shard_map/ppermute | solution.py:614
  25.9 12.7 %edges.1 = (f32[96,128]{1,0:T(8,128)}, f32[96,128]{1,0:T(8,128)}, f32[2,48,512]{2,1,0:T(8,128)}, f32[3,48,512]{2,1,0:T(8,128)}) custom-call(f32[41,96,512]{2,1,0:T(8,128)} %u.1, f32[41,96,512]{2,1,0:T(8,128)} %u.1, f32[41,96,512]{2,1,0:T(8,128)} %v.1, f32[41,96,512]{2,1,0:T(8,128)} %v.1, f32[41,96,512]{2,1,0:T(8,128)} %tf.1, f32[41,96,512]{2,1,0:T(8,128)} %sf.1, ...), custom_call_target="tpu_custom_call" | custom-call | flops 10000000 | bytes 16000000 | tf_op jit(solution)/shard_map/edges/pallas_call | solution.py:132
  38.6 1.3 collective-permute-start.4
  39.9 1.3 collective-permute-start.7
  41.2 0.7 slice.37
  41.9 1.3 collective-permute-start.5
  43.2 20.1 %tracers.1 = (f32[12,41,8,512]{3,2,1,0:T(8,128)}, f32[12,41,8,512]{3,2,1,0:T(8,128)}, f32[12,41,8,512]{3,2,1,0:T(8,128)}, f32[96,128]{1,0:T(8,128)}, f32[96,128]...) custom-call(f32[41,96,512]{2,1,0:T(8,128)} %tf.1, f32[41,96,512]{2,1,0:T(8,128)} %sf.1, s32[96,512]{1,0:T(8,128)} %kc.5, ...), custom_call_target="tpu_custom_call" | custom-call | flops 100000000 | bytes 40000000 | tf_op jit(solution)/shard_map/tracers/pallas_call | solution.py:223
  63.3 0.7 slice.38
  64.0 1.6 collective-permute-start.6
  65.6 0.6 copy-done.8
  66.2 3.7 %collective-permute-start.8 = (f32[2,48,512]{2,1,0:T(8,128)}, f32[2,48,512]{2,1,0:T(8,128)S(1)}, u32[]{:S(2)}, u32[]{:S(2)}) collective-permute-start(f32[2,48,512]{2,1,0:T(8,128)} %get-tuple-element.48), channel_id=1, source_target_pairs={{0,1},{1,2},{2,3},{4,5},{5,6},{6,7},{8,9},{9,10},{10,11},{12,13},{... | collective-permute-start | bytes 589832 | tf_op jit(solution)/shard_map/ppermute | solution.py:614
  69.9 1.4 pad_maximum_fusion.10.rwn
  71.4 5.0 %collective-permute-start.9 = (f32[8,128]{1,0:T(8,128)S(1)}, f32[8,128]{1,0:T(8,128)S(1)}, u32[]{:S(2)}, u32[]{:S(2)}) collective-permute-start(f32[8,128]{1,0:T(8,128)S(1)} %slice.38), channel_id=1, source_target_pairs={{0,13},{1,14},{2,15},{4,1},{5,2},{6,3},{8,5},{9,6},{10,7},{12,9},{... | collective-permute-start | bytes 12296 | tf_op jit(solution)/shard_map/ppermute | solution.py:614
  76.4 1.6 pad_maximum_fusion.pl5.planes
  77.9 3.0 %geometry.1 = (f32[176,640]{1,0:T(8,128)}, f32[176,640]{1,0:T(8,128)}, f32[176,640]{1,0:T(8,128)}, f32[176,640]{1,0:T(8,128)}) custom-call(f32[5,176,640]{2,1,0:T(8,128)} %pad_maximum_fusion.pl5.planes), custom_call_target="tpu_custom_call" | custom-call | tf_op jit(solution)/shard_map/geometry/pallas_call | solution.py:252
  81.0 0.5 copy-done.9
  81.6 0.1 copy-done.2
  81.7 30.5 %momentum.1 = (f32[12,41,8,512]{3,2,1,0:T(8,128)}, f32[12,41,8,512]{3,2,1,0:T(8,128)}, f32[96,512]{1,0:T(8,128)}, f32[96,512]{1,0:T(8,128)}, f32[96,512]{1,0:T(8...) custom-call(f32[41,96,512]{2,1,0:T(8,128)} %u.1, f32[41,96,512]{2,1,0:T(8,128)} %v.1, ...), custom_call_target="tpu_custom_call" | custom-call | flops 200000000 | bytes 64000000 | tf_op jit(solution)/shard_map/momentum/pallas_call | solution.py:414
  112.2 0.9 pad_maximum_fusion.8
  113.1 1.2 collective-permute-start.10
  114.3 0.8 collective-permute-start.11
  115.1 1.0 slice_bitcast_fusion
  116.1 1.3 collective-permute-start.16
  117.4 0.8 collective-permute-done.10
  118.2 2.1 %collective-permute-done.11 = f32[2,96,128]{2,1,0:T(8,128)S(1)} collective-permute-done((f32[2,96,128]{2,1,0:T(8,128)S(1)}, f32[2,96,128]{2,1,0:T(8,128)S(1)}, u32[]{:S(2)}, u32[]{:S(2)}) %collective-permute-start.11) | collective-permute-done | bytes 98336 | tf_op jit(solution)/shard_map/ppermute | solution.py:614
  120.3 1.0 pad_maximum_fusion.7
  121.4 1.3 collective-permute-start.13
  122.7 3.0 %collective-permute-start.12 = (f32[2,40,640]{2,1,0:T(8,128)S(1)}, f32[2,40,640]{2,1,0:T(8,128)S(1)}, u32[]{:S(2)}, u32[]{:S(2)}) collective-permute-start(f32[2,40,640]{2,1,0:T(8,128)S(1)} %get-tuple-element.75), channel_id=1, source_target_pairs={{0,1},{1,2},{2,3},{4,5},{5,6},{6,7},{8,9},{9,10},{10,11},{12,13},{... | collective-permute-start | bytes 614408 | tf_op jit(solution)/shard_map/ppermute | solution.py:614
  125.7 0.9 pad_maximum_fusion.4
  126.7 2.1 %collective-permute-start.17 = (f32[3,48,512]{2,1,0:T(8,128)S(1)}, f32[3,48,512]{2,1,0:T(8,128)S(1)}, u32[]{:S(2)}, u32[]{:S(2)}) collective-permute-start(f32[3,48,512]{2,1,0:T(8,128)S(1)} %pad_maximum_fusion.4), channel_id=1, source_target_pairs={{0,1},{1,2},{2,3},{4,5},{5,6},{6,7},{8,9},{9,10},{10,11},{12,13},{... | collective-permute-start | bytes 884744 | tf_op jit(solution)/shard_map/ppermute | solution.py:614
  128.8 2.2 %collective-permute-start.15 = (f32[96,128]{1,0:T(8,128)S(1)}, f32[96,128]{1,0:T(8,128)S(1)}, u32[]{:S(2)}, u32[]{:S(2)}) collective-permute-start(f32[96,128]{1,0:T(8,128)S(1)} %copy-done.11), channel_id=1, source_target_pairs={{0,12},{1,13},{2,14},{3,15},{4,0},{5,1},{6,2},{7,3},{8,4},{9,5},{1... | collective-permute-start | bytes 147464 | tf_op jit(solution)/shard_map/ppermute | solution.py:614
  131.0 0.7 copy.17.tide
  131.7 0.8 add.3
  132.6 2.0 %pad_maximum_fusion.1.force = f32[2,176,640]{2,1,0:T(8,128)} fusion(f32[2,40,640]{2,1,0:T(8,128)S(1)} %collective-permute-done.13, f32[2,96,128]{2,1,0:T(8,128)S(1)} %broadcast_select_fusion.1, f32[1,96,512]{2,1,0:T(8,128)} %bitcast.20, f32[1,96,512]{2,1,0:T(8,128)} %bitcast.17, f32[2,40,640]{2,1,0:T(8,128)S(1)} %collective-permute-done.12), kind=kLoop, calls=%fused_computation.1 | loop fusion | flops 901120 | bytes 1802240 | tf_op jit(solution)/shard_map/concatenate | solution.py:621
  134.6 16.8 %subcycles.1 = (f32[96,512]{1,0:T(8,128)}, f32[96,512]{1,0:T(8,128)}, f32[96,512]{1,0:T(8,128)}, f32[104,640]{1,0:T(8,128)}, f32[104,640]{1,0:T(8,128)}) custom-call(f32[5,176,640]{2,1,0:T(8,128)} %pad_maximum_fusion.pl5.planes, f32[176,640]{1,0:T(8,128)} %get-tuple-element.39.kun.kux.kus.ku, f32[176,640]{1,0:T(8,128)} %get-tuple-element.40.kvn.kvx.kvs.kv, ...), custom_call_target="tpu_custom_call" | custom-call | flops 100000000 | bytes 1000000 | tf_op jit(solution)/shard_map/subcycles/pallas_call | solution.py:500
  151.5 0.5 copy-done.5
  152.0 0.1 copy-done
  152.2 0.1 copy-done.1
  152.3 31.3 %finish.1 = (f32[41,96,512]{2,1,0:T(8,128)}, f32[41,96,512]{2,1,0:T(8,128)}, f32[41,96,512]{2,1,0:T(8,128)}, f32[41,96,512]{2,1,0:T(8,128)}) custom-call(f32[12,41,8,512]{3,2,1,0:T(8,128)} %get-tuple-element.54.us_b, f32[12,41,8,512]{3,2,1,0:T(8,128)} %get-tuple-element.55.vs_b, f32[12,41,8,512]{3,2,1,0:T(8,128)} %get-tuple-element.56.t_b, ...), custom_call_target="tpu_custom_call" | custom-call | flops 100000000 | bytes 80000000 | tf_op jit(solution)/shard_map/finish/pallas_call | solution.py:592
  (39 shorter events, 0.4 us)
Async XLA Ops:
  5.4 10.8 %collective-permute-start = (f32[5,96,128]{2,1,0:T(8,128)S(1)}, f32[5,96,128]{2,1,0:T(8,128)S(1)}, u32[]{:S(2)}, u32[]{:S(2)}) collective-permute-start(f32[5,96,128]{2,1,0:T(8,128)S(1)} %get-tuple-element.74), channel_id=1, source_target_pairs={{0,12},{1,13},{2,14},{3,15},{4,0},{5,1},{6,2},{7,3},{8,4},{9,5},{1... | collective-permute-start | bytes 737288 | tf_op jit(solution)/shard_map/ppermute | solution.py:614
  9.7 11.7 %collective-permute-start.1 = (f32[5,96,128]{2,1,0:T(8,128)S(1)}, f32[5,96,128]{2,1,0:T(8,128)S(1)}, u32[]{:S(2)}, u32[]{:S(2)}) collective-permute-start(f32[5,96,128]{2,1,0:T(8,128)S(1)} %get-tuple-element.73), channel_id=1, source_target_pairs={{0,4},{1,5},{2,6},{3,7},{4,8},{5,9},{6,10},{7,11},{8,12},{9,13},{1... | collective-permute-start | bytes 737288 | tf_op jit(solution)/shard_map/ppermute | solution.py:614
  21.5 49.9 %collective-permute-start.3 = (f32[5,40,640]{2,1,0:T(8,128)S(1)}, f32[5,40,640]{2,1,0:T(8,128)S(1)}, u32[]{:S(2)}, u32[]{:S(2)}) collective-permute-start(f32[5,40,640]{2,1,0:T(8,128)S(1)} %get-tuple-element.72), channel_id=1, source_target_pairs={{1,0},{2,1},{3,2},{5,4},{6,5},{7,6},{9,8},{10,9},{11,10},{13,12},{... | collective-permute-start | bytes 1536008 | tf_op jit(solution)/shard_map/ppermute | solution.py:614
  22.8 53.5 %collective-permute-start.2 = (f32[5,40,640]{2,1,0:T(8,128)S(1)}, f32[5,40,640]{2,1,0:T(8,128)S(1)}, u32[]{:S(2)}, u32[]{:S(2)}) collective-permute-start(f32[5,40,640]{2,1,0:T(8,128)S(1)} %get-tuple-element.71), channel_id=1, source_target_pairs={{0,1},{1,2},{2,3},{4,5},{5,6},{6,7},{8,9},{9,10},{10,11},{12,13},{... | collective-permute-start | bytes 1536008 | tf_op jit(solution)/shard_map/ppermute | solution.py:614
  38.6 27.1 %collective-permute-start.4 = (f32[96,128]{1,0:T(8,128)}, f32[96,128]{1,0:T(8,128)S(1)}, u32[]{:S(2)}, u32[]{:S(2)}) collective-permute-start(f32[96,128]{1,0:T(8,128)} %get-tuple-element.45), channel_id=1, source_target_pairs={{0,4},{1,5},{2,6},{3,7},{4,8},{5,9},{6,10},{7,11},{8,12},{9,13},{1... | collective-permute-start | bytes 147464 | tf_op jit(solution)/shard_map/ppermute | solution.py:614
  39.9 41.1 %collective-permute-start.7 = (f32[3,48,512]{2,1,0:T(8,128)}, f32[3,48,512]{2,1,0:T(8,128)}, u32[]{:S(2)}, u32[]{:S(2)}) collective-permute-start(f32[3,48,512]{2,1,0:T(8,128)} %get-tuple-element.47.rown), channel_id=1, source_target_pairs={{1,0},{2,1},{3,2},{5,4},{6,5},{7,6},{9,8},{10,9},{11,10},{13,12},{... | collective-permute-start | bytes 884744 | tf_op jit(solution)/shard_map/ppermute | solution.py:614
  41.9 22.1 %collective-permute-start.5 = (f32[8,128]{1,0:T(8,128)S(1)}, f32[8,128]{1,0:T(8,128)S(1)}, u32[]{:S(2)}, u32[]{:S(2)}) collective-permute-start(f32[8,128]{1,0:T(8,128)S(1)} %slice.37), channel_id=1, source_target_pairs={{1,4},{2,5},{3,6},{5,8},{6,9},{7,10},{9,12},{10,13},{11,14},{13,0}... | collective-permute-start | bytes 12296 | tf_op jit(solution)/shard_map/ppermute | solution.py:614
  64.0 17.0 %collective-permute-start.6 = (f32[96,128]{1,0:T(8,128)}, f32[96,128]{1,0:T(8,128)S(1)}, u32[]{:S(2)}, u32[]{:S(2)}) collective-permute-start(f32[96,128]{1,0:T(8,128)} %get-tuple-element.46), channel_id=1, source_target_pairs={{0,12},{1,13},{2,14},{3,15},{4,0},{5,1},{6,2},{7,3},{8,4},{9,5},{1... | collective-permute-start | bytes 147464 | tf_op jit(solution)/shard_map/ppermute | solution.py:614
  65.6 0.6 copy-start.8
  66.2 14.7 %collective-permute-start.8 = (f32[2,48,512]{2,1,0:T(8,128)}, f32[2,48,512]{2,1,0:T(8,128)S(1)}, u32[]{:S(2)}, u32[]{:S(2)}) collective-permute-start(f32[2,48,512]{2,1,0:T(8,128)} %get-tuple-element.48), channel_id=1, source_target_pairs={{0,1},{1,2},{2,3},{4,5},{5,6},{6,7},{8,9},{9,10},{10,11},{12,13},{... | collective-permute-start | bytes 589832 | tf_op jit(solution)/shard_map/ppermute | solution.py:614
  71.4 9.6 %collective-permute-start.9 = (f32[8,128]{1,0:T(8,128)S(1)}, f32[8,128]{1,0:T(8,128)S(1)}, u32[]{:S(2)}, u32[]{:S(2)}) collective-permute-start(f32[8,128]{1,0:T(8,128)S(1)} %slice.38), channel_id=1, source_target_pairs={{0,13},{1,14},{2,15},{4,1},{5,2},{6,3},{8,5},{9,6},{10,7},{12,9},{... | collective-permute-start | bytes 12296 | tf_op jit(solution)/shard_map/ppermute | solution.py:614
  81.0 0.6 copy-start.9
  81.0 0.6 copy-start.3
  81.0 0.7 copy-start.2
  81.7 44.1 %copy-start.4 = (f32[2,48,512]{2,1,0:T(8,128)S(1)}, f32[2,48,512]{2,1,0:T(8,128)}, u32[]{:S(2)}) copy-start(f32[2,48,512]{2,1,0:T(8,128)} %get-tuple-element.66) | copy-start | bytes 589828
  81.7 47.1 %copy-start.11 = (f32[96,128]{1,0:T(8,128)S(1)}, f32[96,128]{1,0:T(8,128)}, u32[]{:S(2)}) copy-start(f32[96,128]{1,0:T(8,128)} %get-tuple-element.64) | copy-start | bytes 147460
  81.7 49.3 %copy-start.10 = (f32[36,2]{0,1:T(2,128)S(1)}, f32[36,2]{0,1:T(2,128)}, u32[]{:S(2)}) copy-start(f32[36,2]{0,1:T(2,128)} %param.19) | copy-start | bytes 868
  81.7 50.0 %copy-start.7 = (f32[96,128]{1,0:T(8,128)S(1)}, f32[96,128]{1,0:T(8,128)}, u32[]{:S(2)}) copy-start(f32[96,128]{1,0:T(8,128)} %get-tuple-element.62) | copy-start | bytes 147460
  113.1 5.2 %collective-permute-start.10 = (f32[2,96,128]{2,1,0:T(8,128)S(1)}, f32[2,96,128]{2,1,0:T(8,128)S(1)}, u32[]{:S(2)}, u32[]{:S(2)}) collective-permute-start(f32[2,96,128]{2,1,0:T(8,128)S(1)} %get-tuple-element.78), channel_id=1, source_target_pairs={{0,12},{1,13},{2,14},{3,15},{4,0},{5,1},{6,2},{7,3},{8,4},{9,5},{1... | collective-permute-start | bytes 294920 | tf_op jit(solution)/shard_map/ppermute | solution.py:614
  114.3 6.0 %collective-permute-start.11 = (f32[2,96,128]{2,1,0:T(8,128)S(1)}, f32[2,96,128]{2,1,0:T(8,128)S(1)}, u32[]{:S(2)}, u32[]{:S(2)}) collective-permute-start(f32[2,96,128]{2,1,0:T(8,128)S(1)} %get-tuple-element.77), channel_id=1, source_target_pairs={{0,4},{1,5},{2,6},{3,7},{4,8},{5,9},{6,10},{7,11},{8,12},{9,13},{1... | collective-permute-start | bytes 294920 | tf_op jit(solution)/shard_map/ppermute | solution.py:614
  116.1 35.3 %collective-permute-start.16 = (f32[3,48,512]{2,1,0:T(8,128)S(1)}, f32[3,48,512]{2,1,0:T(8,128)S(1)}, u32[]{:S(2)}, u32[]{:S(2)}) collective-permute-start(f32[3,48,512]{2,1,0:T(8,128)S(1)} %slice_bitcast_fusion), channel_id=1, source_target_pairs={{1,0},{2,1},{3,2},{5,4},{6,5},{7,6},{9,8},{10,9},{11,10},{13,12},{... | collective-permute-start | bytes 884744 | tf_op jit(solution)/shard_map/ppermute | solution.py:614
  121.4 11.1 %collective-permute-start.13 = (f32[2,40,640]{2,1,0:T(8,128)S(1)}, f32[2,40,640]{2,1,0:T(8,128)S(1)}, u32[]{:S(2)}, u32[]{:S(2)}) collective-permute-start(f32[2,40,640]{2,1,0:T(8,128)S(1)} %get-tuple-element.76), channel_id=1, source_target_pairs={{1,0},{2,1},{3,2},{5,4},{6,5},{7,6},{9,8},{10,9},{11,10},{13,12},{... | collective-permute-start | bytes 614408 | tf_op jit(solution)/shard_map/ppermute | solution.py:614
  122.7 9.9 %collective-permute-start.12 = (f32[2,40,640]{2,1,0:T(8,128)S(1)}, f32[2,40,640]{2,1,0:T(8,128)S(1)}, u32[]{:S(2)}, u32[]{:S(2)}) collective-permute-start(f32[2,40,640]{2,1,0:T(8,128)S(1)} %get-tuple-element.75), channel_id=1, source_target_pairs={{0,1},{1,2},{2,3},{4,5},{5,6},{6,7},{8,9},{9,10},{10,11},{12,13},{... | collective-permute-start | bytes 614408 | tf_op jit(solution)/shard_map/ppermute | solution.py:614
  126.7 24.8 %collective-permute-start.17 = (f32[3,48,512]{2,1,0:T(8,128)S(1)}, f32[3,48,512]{2,1,0:T(8,128)S(1)}, u32[]{:S(2)}, u32[]{:S(2)}) collective-permute-start(f32[3,48,512]{2,1,0:T(8,128)S(1)} %pad_maximum_fusion.4), channel_id=1, source_target_pairs={{0,1},{1,2},{2,3},{4,5},{5,6},{6,7},{8,9},{9,10},{10,11},{12,13},{... | collective-permute-start | bytes 884744 | tf_op jit(solution)/shard_map/ppermute | solution.py:614
  128.8 22.6 %collective-permute-start.15 = (f32[96,128]{1,0:T(8,128)S(1)}, f32[96,128]{1,0:T(8,128)S(1)}, u32[]{:S(2)}, u32[]{:S(2)}) collective-permute-start(f32[96,128]{1,0:T(8,128)S(1)} %copy-done.11), channel_id=1, source_target_pairs={{0,12},{1,13},{2,14},{3,15},{4,0},{5,1},{6,2},{7,3},{8,4},{9,5},{1... | collective-permute-start | bytes 147464 | tf_op jit(solution)/shard_map/ppermute | solution.py:614
  132.5 18.9 %collective-permute-start.14 = (f32[96,128]{1,0:T(8,128)S(1)}, f32[96,128]{1,0:T(8,128)S(1)}, u32[]{:S(2)}, u32[]{:S(2)}) collective-permute-start(f32[96,128]{1,0:T(8,128)S(1)} %add.3), channel_id=1, source_target_pairs={{0,4},{1,5},{2,6},{3,7},{4,8},{5,9},{6,10},{7,11},{8,12},{9,13},{1... | collective-permute-start | bytes 147464 | tf_op jit(solution)/shard_map/ppermute | solution.py:614
  151.4 0.6 copy-start.5
  151.4 0.7 copy-start
  151.4 0.7 copy-start.6
  151.5 0.8 copy-start.1

commit v4 on v3

--- a/solution.py
+++ b/solution.py
@@ -18,6 +18,9 @@
 NB = NR // 8
 SUB = 36
 GROUP = 2
+HALF = 64
+SIDES = (-1, 0, 1)
+FIRST, LAST = slice(0, 1), slice(7, 8)
 TILES = 3
 DT = 4.0
 DTB = DT / SUB
@@ -36,6 +39,18 @@
 
 def iota(shape, dim):
     return lax.broadcasted_iota(jnp.int32, shape, dim)
+
+
+def whole(*shape):
+    return pl.BlockSpec(shape, lambda *_: (0,) * len(shape))
+
+
+def shape(*dims):
+    return jax.ShapeDtypeStruct(dims, F32)
+
+
+def one(k):
+    return slice(k, k + 1)
 
 
 def tile_rows(i):
@@ -109,11 +124,11 @@
         acc = jnp.zeros(ROW, F32)
         for k in range(NL):
             p, acc = pressure_step(tf[k], sf[k], k < count, acc, dz)
-            rn[0, k : k + 1, :] = ul[k, 7:8, :]
-            rn[1, k : k + 1, :] = vl[k, 7:8, :]
-            rs[0, k : k + 1, :] = uf[k, 0:1, :]
-            rs[1, k : k + 1, :] = vf[k, 0:1, :]
-            rs[2, k : k + 1, :] = p[0:1, :]
+            rn[0, one(k), :] = ul[k, LAST, :]
+            rn[1, one(k), :] = vl[k, LAST, :]
+            rs[0, one(k), :] = uf[k, FIRST, :]
+            rs[1, one(k), :] = vf[k, FIRST, :]
+            rs[2, one(k), :] = p[FIRST, :]
         for i in range(3):
             rs[i, NL:LP, :] = jnp.zeros((LP - NL, NC), F32)
             if i < 2:
@@ -140,8 +155,6 @@
             jax.ShapeDtypeStruct((2, LP, NC), F32),
             jax.ShapeDtypeStruct((3, LP, NC), F32),
         ],
-        compiler_params=pltpu.CompilerParams(dimension_semantics=("arbitrary",)),
-        cost_estimate=pl.CostEstimate(flops=10**7, bytes_accessed=16 * 10**6, transcendentals=0),
         name="edges",
     )(u, u, v, v, t, s, kmt, depth, u, v, u, v, t, s, kmt, depth)
 
@@ -156,8 +169,8 @@
     @pl.when(b == NB // 2 - 1)
     def _():
         for k in range(NL):
-            rn[0, k : k + 1, :] = tm[k, 7:8, :]
-            rn[1, k : k + 1, :] = sm[k, 7:8, :]
+            rn[0, one(k), :] = tm[k, LAST, :]
+            rn[1, one(k), :] = sm[k, LAST, :]
         for i in range(2):
             rn[i, NL:LP, :] = jnp.zeros((LP - NL, NC), F32)
 
@@ -174,7 +187,7 @@
         tk, sk = t[k], s[k]
         p, cum = pressure_step(tk, sk, wet, cum, thick)
         pr[k] = p
-        rs[2, k : k + 1, :] = p[0:1, :]
+        rs[2, one(k), :] = p[FIRST, :]
         upper = jnp.where(k + 1 < cnt, c, 0.0) if k + 1 < NL else zero
         top = 1.0 + lower * keep if k else jnp.ones_like(zero)
         inv = 1.0 / (top + upper)
@@ -194,8 +207,8 @@
         bs = sm[k] + gain * bs
         tm[k] = bt
         sm[k] = bs
-        rs[0, k : k + 1, :] = bt[0:1, :]
-        rs[1, k : k + 1, :] = bs[0:1, :]
+        rs[0, one(k), :] = bt[FIRST, :]
+        rs[1, one(k), :] = bs[FIRST, :]
         for x, base in ((bt, NL), (bs, 2 * NL)):
             ae = jnp.where(lane == base + k, lane_to(x[:, NC - LN :], LN - 1, base + k), ae)
             aw = jnp.where(lane == base + k, lane_to(x[:, :LN], 0, base + k), aw)
@@ -227,29 +240,188 @@
         out_specs=[pack, pack, pack, col, col, rows, first_rows(lambda b: b, 2)],
         out_shape=[PACK, PACK, PACK] + [jax.ShapeDtypeStruct((NR, LN), F32)] * 2 + [jax.ShapeDtypeStruct((2, LP, NC), F32), jax.ShapeDtypeStruct((NB, 3, LP, NC), F32)],
         scratch_shapes=[VM(SLAB, F32)],
-        compiler_params=pltpu.CompilerParams(dimension_semantics=("arbitrary",)),
-        cost_estimate=pl.CostEstimate(flops=10**8, bytes_accessed=40 * 10**6, transcendentals=0),
         name="tracers",
     )(t, s, kmt, depth)
 
 
-def geometry_kernel(pl5, ku, kv, du, dv):
+class Exchange:
+    def __init__(self, sizes, send_sem, recv_sem):
+        self.rows, self.cols = sizes
+        self.row, self.col = lax.axis_index("row"), lax.axis_index("col")
+        self.sems = send_sem, recv_sem
+        self.used = 0
+
+    def inside(self, drow):
+        return (self.row + drow >= 0) & (self.row + drow < self.rows)
+
+    def at(self, drow, dcol):
+        return {"row": self.row + drow, "col": lax.rem(self.col + dcol + self.cols, self.cols)}
+
+    def when(self, drow, action):
+        if drow:
+            pl.when(self.inside(drow))(action)
+        else:
+            action()
+
+    def barrier(self):
+        ready = pltpu.get_barrier_semaphore()
+        for drow in SIDES:
+            for dcol in SIDES:
+                if drow or dcol:
+                    self.when(drow, functools.partial(pl.semaphore_signal, ready, device_id=self.at(drow, dcol), device_id_type=pl.DeviceIdType.MESH))
+        per_row = len(SIDES)
+        known = [self.inside(drow).astype(jnp.int32) for drow in SIDES if drow]
+        pl.semaphore_wait(ready, per_row - 1 + per_row * sum(known))
+
+    def clear(self, plan):
+        for _, dst, drow, _ in plan:
+            if drow:
+
+                @pl.when(jnp.logical_not(self.inside(-drow)))
+                def _():
+                    dst[:] = jnp.zeros(dst.shape, F32)
+
+    def start(self, plan):
+        out = []
+        for src, dst, drow, dcol in plan:
+            copy = pltpu.make_async_remote_copy(
+                src_ref=src,
+                dst_ref=dst,
+                send_sem=self.sems[0].at[self.used],
+                recv_sem=self.sems[1].at[self.used],
+                device_id=self.at(drow, dcol),
+                device_id_type=pl.DeviceIdType.MESH,
+            )
+            self.used += 1
+            self.when(drow, copy.start)
+            out.append((copy, drow))
+        return out
+
+    def wait(self, copies):
+        for copy, drow in copies:
+            self.when(drow, copy.wait_send)
+            self.when(-drow, copy.wait_recv)
+
+
+def pack_strips(pairs, to_west, to_east):
+    lane = iota(TILE, 1)
+    first, last = slice(0, LN), slice(NC - LN, NC)
+
+    def turn(n):
+        q, sl = n // NB, tile_rows(n % NB)
+        b = pairs[q][-1]
+        return pltpu.roll(b[sl, first], HALF, axis=1), pltpu.roll(b[sl, last], HALF, axis=1)
+
+    def store(n, turned):
+        q, sl = n // NB, tile_rows(n % NB)
+        a = pairs[q][0]
+        to_west[q, sl, :] = jnp.where(lane < HALF, a[sl, first], turned[0])
+        to_east[q, sl, :] = jnp.where(lane < HALF, turned[1], a[sl, last])
+
+    skewed((turn, store), NB, NB * len(pairs))
+
+
+def strip_plan(to_west, to_east, strips):
+    top, bottom = pl.ds(NR - HR, HR), pl.ds(0, HR)
+    return [
+        (to_east, strips[0], 0, 1),
+        (to_west, strips[1], 0, -1),
+        (to_east.at[:, top], strips[2], 1, 1),
+        (to_west.at[:, top], strips[3], 1, -1),
+        (to_east.at[:, bottom], strips[4], -1, 1),
+        (to_west.at[:, bottom], strips[5], -1, -1),
+    ]
+
+
+def row_plan(planes, south, north):
+    plan = []
+    for i, x in enumerate(planes):
+        plan.append((x.at[pl.ds(NR - HR, HR), :], south.at[i], 1, 0))
+        plan.append((x.at[pl.ds(0, HR), :], north.at[i], -1, 0))
+    return plan
+
+
+def strip_scratch(n):
+    return [VM((n, NR, LN), F32)] * 4 + [VM((n, HR, LN), F32)] * 4
+
+
+def side(i, own, south, north):
+    if i < HT:
+        return south, tile_rows(i)
+    return (own, tile_rows(i - HT)) if i < HT + NB else (north, tile_rows(i - HT - NB))
+
+
+def halo_pair(i, q, strips):
+    (w, e), sl = side(i, strips[:2], strips[2:4], strips[4:])
+    lane = iota(TILE, 1)
+    w, e = w[q, sl, :], e[q, sl, :]
+    return jnp.where(lane < HALF, e, w), pltpu.roll(jnp.where(lane < HALF, w, e), HALF, axis=1)
+
+
+def gather_kernel(sizes, kmt, depth, eta, tu, tv, pke, pkw, prn, prs, rw, re, rsouth, rnorth, corner, ku, kv, du, dv, eta_o, tu_o, tv_o, kf, south, north, *rest):
+    to_west, to_east, *strips, send_sem, recv_sem = rest
+    net = Exchange(sizes, send_sem, recv_sem)
+    kf[:] = kmt[:].astype(F32)
+    planes = (kf, depth, eta, tu, tv)
+    pack_strips((planes[:2], planes[2:4], planes[4:]), to_west, to_east)
+    plan = [
+        (pke, rw.at[pl.ds(0, NR), :], 0, 1),
+        (pkw, re, 0, -1),
+        (prn, rsouth, 1, 0),
+        (prs, rnorth, -1, 0),
+        (pke.at[pl.ds(0, 8), :], rw.at[pl.ds(NR, 8), :], -1, 1),
+        (pkw.at[pl.ds(NR - 8, 8), :], corner, 1, -1),
+    ]
+    plan = strip_plan(to_west, to_east, strips) + plan + row_plan(planes, south, north)
+    net.clear(plan)
+    net.barrier()
+    net.wait(net.start(plan))
     row = iota(WIDE, 0)
-    for i in range(ET):
-        lo = tile_rows(i)
-        hi = slice(8 * (i + 1), 8 * i + 16) if i + 1 < ET else lo
-        k, h = pl5[0, lo, :], pl5[1, lo, :]
+
+    def turn(i):
+        return [halo_pair(i, q, strips) for q in range(3)]
+
+    def build(i, halo):
+        halo = [x for pair in halo for x in pair]
+        vals = []
+        for n in range(len(planes)):
+            part, sl = side(i, planes[n], south.at[n], north.at[n])
+            vals.append(jnp.concatenate([part[sl, :], halo[n]], axis=1))
+        k, h = vals[:2]
         dz = h / jnp.maximum(k, 1.0)
-        kn, hn = pl5[0, hi, :], pl5[1, hi, :]
-        dzn = hn / jnp.maximum(kn, 1.0)
-        ku[lo, :] = jnp.minimum(k, from_east(k))
-        kv[lo, :] = jnp.minimum(k, up_row(k, kn, row))
-        du[lo, :] = 0.5 * (dz + from_east(dz))
-        dv[lo, :] = 0.5 * (dz + up_row(dz, dzn, row))
-
-
-def geometry(planes):
-    return pl.pallas_call(geometry_kernel, out_shape=[jax.ShapeDtypeStruct((ER, EC), F32)] * 4, name="geometry")(planes)
+        kv[tile_rows(i), :] = k
+        dv[tile_rows(i), :] = dz
+        return vals[2:], from_east(k), from_east(dz)
+
+    def store(i, arg):
+        vals, ke, dze = arg
+        sl = tile_rows(i)
+        hi = tile_rows(min(i + 1, ET - 1))
+        k, dz = kv[sl, :], dv[sl, :]
+        k_u, k_v = jnp.minimum(k, ke), jnp.minimum(k, up_row(k, kv[hi, :], row))
+        dv[sl, :] = 0.5 * (dz + up_row(dz, dv[hi, :], row))
+        du[sl, :] = 0.5 * (dz + dze)
+        ku[sl, :] = k_u
+        kv[sl, :] = k_v
+        for out, x, wet in zip((eta_o, tu_o, tv_o), vals, (k, k_u, k_v)):
+            out[sl, :] = only(wet > 0, x)
+
+    skewed((turn, build, store), TILES, ET)
+
+
+def gather(sizes, *args):
+    vm = pl.BlockSpec(memory_space=VM)
+    outs = [shape(NR + 8, LN), shape(NR, LN), shape(2, LP, NC), shape(3, LP, NC), shape(8, LN)] + [shape(ER, EC)] * 7
+    sems = [pltpu.SemaphoreType.DMA((6 + 6 + 10,))] * 2
+    return pl.pallas_call(
+        functools.partial(gather_kernel, sizes),
+        in_specs=[vm] * len(args),
+        out_specs=[vm] * len(outs),
+        out_shape=outs,
+        scratch_shapes=[VM((NR, NC), F32)] + [VM((5, HR, NC), F32)] * 2 + strip_scratch(3) + sems,
+        compiler_params=pltpu.CompilerParams(collective_id=0, has_side_effects=True),
+        name="gather",
+    )(*args)
 
 
 def solve_pair(src_a, src_b, ca, cb, na, nb, out_a, out_b, gain_a, gain_b):
@@ -310,21 +482,21 @@
             ums[k], vms[k] = masked(k, u[k], v[k], halos(k))
         lev = iota((LP, NC), 0).astype(F32)
         lev1 = iota((LP, LN), 0)
-        ks, kw = kus[7:8, :NC], kvs[7:8, :NC]
+        ks, kw = kus[LAST, :NC], kvs[LAST, :NC]
         s_u = only(lev < ks, rsouth[0])
         s_v = only(lev < kw, rsouth[1])
-        pick = only(iota((LP, LN), 1) == lev1 + NL, corner[7:8, :])
+        pick = only(iota((LP, LN), 1) == lev1 + NL, corner[LAST, :])
         edge = jnp.sum(pick, axis=1, keepdims=True)
-        edge = only(lev[:, :1] < kvs[7:8, NC : NC + 1], edge)
+        edge = only(lev[:, :1] < kvs[LAST, one(NC)], edge)
         s_ve = jnp.where(iota((LP, NC), 1) == NC - 1, edge, from_east(s_v))
-        u_0 = only(lev < kxn[0:1, :NC], rown[0])
-        v_0 = only(lev < kyn[0:1, :NC], rown[1])
+        u_0 = only(lev < kxn[FIRST, :NC], rown[0])
+        v_0 = only(lev < kyn[FIRST, :NC], rown[1])
         c_s = 0.25 * ((s_v + s_ve) * (s_u + u_0))
         h_s = s_v + v_0
         h_s = 0.25 * (h_s * h_s) + rown[2]
         for k in range(NL):
-            cc[k, 7:8, :] = c_s[k : k + 1, :]
-            hh[k, 7:8, :] = h_s[k : k + 1, :]
+            cc[k, LAST, :] = c_s[one(k), :]
+            hh[k, LAST, :] = h_s[one(k), :]
 
     @pl.when(step > 0)
     def _():
@@ -337,8 +509,8 @@
 
         def shift(k, halo):
             um, vm = ums[k], vms[k]
-            uk = jnp.where(last, rnorth[0, k : k + 1, :], u[k])
-            vk = jnp.where(last, rnorth[1, k : k + 1, :], v[k])
+            uk = jnp.where(last, rnorth[0, one(k), :], u[k])
+            vk = jnp.where(last, rnorth[1, one(k), :], v[k])
             pe = jnp.concatenate([p[k], halo[2]], axis=1)
             return masked(k, uk, vk, halo), pe, from_west(um), from_east(vm)
 
@@ -354,7 +526,7 @@
         def tend(k, arg):
             new, dx, c5, dc = arg
             u5, v5, pk = ums[k, :, :NC], vms[k, :, :NC], p[k]
-            north = jnp.where(last, rnorth[2, k : k + 1, :], pfirst[0, 2, k : k + 1, :])
+            north = jnp.where(last, rnorth[2, one(k), :], pfirst[0, 2, one(k), :])
             h = v5 + up_row(v5, new[1][:, :NC], row)
             h = 0.25 * (h * h) + up_row(pk, north, row)
             tu = only(k < kx, dx + (c5 - down_row(c5, cc[k], row)))
@@ -383,8 +555,8 @@
         @pl.when(last)
         def _():
             for k in range(NL):
-                vrow[k : k + 1, :] = vs[k, 7:8, :]
-            vrow[NL : NL + 1, :] = sb[7:8, :]
+                vrow[one(k), :] = vs[k, LAST, :]
+            vrow[one(NL), :] = sb[LAST, :]
             vrow[NL + 1 : LP, :] = jnp.zeros((LP - NL - 1, NC), F32)
 
 
@@ -418,28 +590,51 @@
         out_specs=[pack, pack, plane, plane, plane, plane, col, pl.BlockSpec((LP, NC), lambda b: (0, 0))],
         out_shape=[PACK, PACK, flat, flat, flat, flat, jax.ShapeDtypeStruct((NR, LN), F32), jax.ShapeDtypeStruct((LP, NC), F32)],
         scratch_shapes=[VM(SLAB, F32)] * 6 + [VM((NL,) + WIDE, F32)] * 2,
-        compiler_params=pltpu.CompilerParams(dimension_semantics=("arbitrary",)),
-        cost_estimate=pl.CostEstimate(flops=2 * 10**8, bytes_accessed=64 * 10**6, transcendentals=0),
         name="momentum",
     )(u, v, p, first, ku, kv, ku, kv, du, dv, ku, kv, rw, re, re, rnorth, rsouth, rown, corner)
 
 
-def subcycle_kernel(planes, ku, kv, du, dv, force, tide, eta_o, u_o, v_o, ub_o, vb_o, eta, tu, tv, cu, cv, fu, fv, ub, vb):
-    nt = ET
+def subcycle_kernel(
+    sizes, eta_i, tu_i, tv_i, ku, kv, du, dv, fx, fy, tide, uke, tke, tkw, vrow, trn, trs,
+    eta_o, u_o, v_o, ub_o, vb_o, fw, fe, fsouth, fnorth,
+    eta, tu, tv, cu, cv, fu, fv, ub, vb, edge, south, north, *rest,
+):
+    to_west, to_east, *strips, send_sem, recv_sem = rest
+    net = Exchange(sizes, send_sem, recv_sem)
+    edge[:] = uke[:] + tke[:]
+    pack_strips(((fx, fy),), to_west, to_east)
+    plan = strip_plan(to_west, to_east, strips) + row_plan((fx, fy), south, north)
+    late = [
+        (edge, fw, 0, 1),
+        (tkw, fe, 0, -1),
+        (vrow, fsouth.at[0], 1, 0),
+        (trn, fsouth.at[pl.ds(1, 2)], 1, 0),
+        (trs.at[0], fnorth, -1, 0),
+    ]
+    net.clear(plan + late)
+    net.barrier()
+    plan, late = net.start(plan), net.start(late)
     row = iota(WIDE, 0)
     zero = jnp.zeros(WIDE, F32)
-    for i in range(nt):
+    ub[:] = jnp.zeros(ub.shape, F32)
+    vb[:] = jnp.zeros(vb.shape, F32)
+    eta[:] = eta_i[:]
+    tu[:] = tu_i[:]
+    tv[:] = tv_i[:]
+    cu[:] = DTB * (ku[:] * du[:])
+    cv[:] = DTB * (kv[:] * dv[:])
+    net.wait(plan)
+
+    def turn(i):
+        return halo_pair(i, 0, strips)
+
+    def build(i, halo):
         sl = tile_rows(i)
-        kx, ky = ku[sl, :], kv[sl, :]
-        eta[sl, :] = only(planes[0, sl, :] > 0, planes[2, sl, :])
-        tu[sl, :] = only(kx > 0, planes[3, sl, :])
-        tv[sl, :] = only(ky > 0, planes[4, sl, :])
-        cu[sl, :] = DTB * (kx * du[sl, :])
-        cv[sl, :] = DTB * (ky * dv[sl, :])
-        fu[sl, :] = only(kx > 0, DTB * force[0, sl, :])
-        fv[sl, :] = only(ky > 0, DTB * force[1, sl, :])
-        ub[sl, :] = zero
-        vb[sl, :] = zero
+        for n, (x, out, wet) in enumerate(((fx, fu, ku), (fy, fv, kv))):
+            part, rows = side(i, x, south.at[n], north.at[n])
+            out[sl, :] = only(wet[sl, :] > 0, DTB * jnp.concatenate([part[rows, :], halo[n]], axis=1))
+
+    skewed((turn, build), TILES, ET)
     norm = 6.0 / (SUB * (SUB + 1) * (SUB + 2))
 
     def stage(first, last, lo, hi):
@@ -485,27 +680,29 @@
             vb[sl, :] = vb[sl, :] + w * x
 
     for s in range(0, SUB, 8):
-        stage(s, min(s + 8, SUB), s // 8, nt - s // 8)
+        stage(s, min(s + 8, SUB), s // 8, ET - s // 8)
     eta_o[:] = eta[HR : HR + NR, :NC]
     u_o[:] = tu[HR : HR + NR, :NC]
     v_o[:] = tv[HR : HR + NR, :NC]
     ub_o[:] = ub[HR - 8 : HR + NR, :]
     vb_o[:] = vb[HR - 8 : HR + NR, :]
-
-
-def subcycles(planes, geo, force, tide):
-    flat = jax.ShapeDtypeStruct((NR, NC), F32)
-    bar = jax.ShapeDtypeStruct((NR + 8, EC), F32)
+    net.wait(late)
+
+
+def subcycles(sizes, *args):
     vm = pl.BlockSpec(memory_space=VM)
+    outs = [shape(NR, NC)] * 3 + [shape(NR + 8, EC)] * 2 + [shape(NR, LN)] * 2 + [shape(3, LP, NC)] * 2
+    sems = [pltpu.SemaphoreType.DMA((6 + 4 + 5,))] * 2
+    wide = [VM((ER, EC), F32)] * 9
     return pl.pallas_call(
-        subcycle_kernel,
-        in_specs=[vm] * 6 + [pl.BlockSpec(memory_space=pltpu.SMEM)],
-        out_specs=[vm] * 5,
-        out_shape=[flat, flat, flat, bar, bar],
-        scratch_shapes=[VM((ER, EC), F32)] * 9,
-        cost_estimate=pl.CostEstimate(flops=10**8, bytes_accessed=10**6, transcendentals=0),
+        functools.partial(subcycle_kernel, sizes),
+        in_specs=[vm] * 9 + [pl.BlockSpec(memory_space=pltpu.SMEM)] + [vm] * 5 + [pl.BlockSpec(memory_space=pl.ANY)],
+        out_specs=[vm] * len(outs),
+        out_shape=outs,
+        scratch_shapes=wide + [VM((NR, LN), F32)] + [VM((2, HR, NC), F32)] * 2 + strip_scratch(1) + sems,
+        compiler_params=pltpu.CompilerParams(collective_id=1, has_side_effects=True),
         name="subcycles",
-    )(planes, *geo, force, tide)
+    )(*args)
 
 
 def finish_kernel(
@@ -525,14 +722,14 @@
     @pl.when(b == 0)
     def _():
         lev = iota((LP, NC), 0).astype(F32)
-        kx = kvs[7:8, :NC]
-        cor = correction(vbs[7:8, :NC], rsouth[0, NL : NL + 1, :], kx, dvs[7:8, :NC])
+        kx = kvs[LAST, :NC]
+        cor = correction(vbs[LAST, :NC], rsouth[0, one(NL), :], kx, dvs[LAST, :NC])
         vel = 0.5 * DT * only(lev < kx, rsouth[0] + cor)
         ft = vel * (rsouth[1] + rown[0, 0])
         fs = vel * (rsouth[2] + rown[0, 1])
         for k in range(NL):
-            ct[k, 7:8, :] = ft[k : k + 1, :]
-            cs[k, 7:8, :] = fs[k : k + 1, :]
+            ct[k, LAST, :] = ft[one(k), :]
+            cs[k, LAST, :] = fs[one(k), :]
 
     kx, ky, cnt = ku[:], kv[:, :NC], kc[:]
     rwv, rev = rw[:], re[:]
@@ -565,7 +762,7 @@
         hy = (0.5 * DT) * ve
         for i, (x, out, carry) in enumerate(fields):
             own = x[k]
-            north = jnp.where(last, rnorth[i, k : k + 1, :], first[0, i, k : k + 1, :])
+            north = jnp.where(last, rnorth[i, one(k), :], first[0, i, one(k), :])
             fy = hy * (own + up_row(own, north, row))
             new = own - (div[i] + (fy - down_row(fy, carry[k], row)))
             carry[k] = fy
@@ -596,45 +793,20 @@
         out_specs=[cube] * 4,
         out_shape=[big] * 4,
         scratch_shapes=[VM(SLAB, F32)] * 2,
-        compiler_params=pltpu.CompilerParams(dimension_semantics=("arbitrary",)),
-        cost_estimate=pl.CostEstimate(flops=10**8, bytes_accessed=80 * 10**6, transcendentals=0),
         name="finish",
     )(us, vs, tm, sm, first, kmt, ku, kv, du, dv, ub, vb, su, sv, kv, dv, vb, rw, re, rnorth, rsouth, first)
 
 
 def solution(mesh):
-    n_cols, n_rows = mesh.shape["col"], mesh.shape["row"]
-
-    def send(x, drow, dcol):
-        pairs = []
-        for c in range(n_cols):
-            for r in range(n_rows):
-                if 0 <= r + drow < n_rows:
-                    pairs.append((c * n_rows + r, ((c + dcol) % n_cols) * n_rows + r + drow))
-        return lax.ppermute(x, ("col", "row"), pairs)
-
-    def widen(x):
-        lane = lax.broadcasted_iota(jnp.int32, (1, 1, 128), 2)
-        east, west = send(x[..., :LN], 0, -1), send(x[..., NC - LN :], 0, 1)
-        wide = jnp.concatenate([x, jnp.where(lane < 64, east, west)], axis=-1)
-        north, south = send(wide[:, :HR], -1, 0), send(wide[:, NR - HR :], 1, 0)
-        return jnp.concatenate([south, wide, north], axis=1)
+    sizes = mesh.shape["row"], mesh.shape["col"]
 
     def local_step(u, v, t, s, eta, tu, tv, depth, kmt, tide):
         pke, pkw, prn, prs = edges(u, v, t, s, kmt, depth)
-        planes = widen(jnp.stack([kmt.astype(F32), depth, eta, tu, tv]))
-        rw, re = send(pke, 0, 1), send(pkw, 0, -1)
-        rsouth, rnorth = send(prn, 1, 0), send(prs, -1, 0)
-        nw = send(pke[:8], -1, 1)
-        se = send(pkw[NR - 8 :], 1, -1)
-        geo = geometry(planes)
+        rw, re, rsouth, rnorth, corner, *wide = gather(sizes, kmt, depth, eta, tu, tv, pke, pkw, prn, prs)
+        geo, state = wide[:4], wide[4:]
         tm, sm, pr, tke, tkw, trn, first = tracers(t, s, kmt, depth)
-        rw = jnp.concatenate([rw, nw], axis=0)
-        us, vs, fx, fy, su, sv, uke, vrow = momentum(u, v, pr, first, geo, rw, re, rnorth, rsouth, prs, se)
-        force = widen(jnp.stack([fx, fy]))
-        fw, fe = send(tke + uke, 0, 1), send(tkw, 0, -1)
-        fsouth, fnorth = send(jnp.concatenate([vrow[None], trn]), 1, 0), send(first[0], -1, 0)
-        eta_n, u_n, v_n, ub, vb = subcycles(planes, geo, force, tide)
+        us, vs, fx, fy, su, sv, uke, vrow = momentum(u, v, pr, first, geo, rw, re, rnorth, rsouth, prs, corner)
+        eta_n, u_n, v_n, ub, vb, fw, fe, fsouth, fnorth = subcycles(sizes, *state, *geo, fx, fy, tide, uke, tke, tkw, vrow, trn, first)
         uo, vo, to, so = finish(us, vs, tm, sm, first, kmt, geo, ub, vb, su, sv, fw, fe, fnorth, fsouth)
         return eta_n, u_n, v_n, uo, vo, to, so
 

time: 185 us -> 146 us (0.79)
  starting transfers between devices: 34.9 us -> 0 us
  Pallas kernels: 114 us -> 142 us
  waiting for transfers between devices: 14.6 us -> 0 us
  other arithmetic: 9.7 us -> 0 us
  local copies, waits for them, and re-layouts: 8.96 us -> 2.75 us
    ppermute x18 -> x0, starting transfers between devices: 34.9 us -> none  [send(): return lax.ppermute(x, ('col', 'row'), pairs)]
    pallas_call x2, Pallas kernels: 19.9 us -> 47.4 us  [the longest x1 24.3 us: subcycles(): pl.pallas_call(functools.partial(subcycle_kernel, sizes), in_specs=[vm] *...]
    ppermute x18 -> x0, waiting for transfers between devices: 14.6 us -> none  [send(): return lax.ppermute(x, ('col', 'row'), pairs)]
    concatenate x4 -> x0, other arithmetic: 5.9 us -> none  [the longest x2 3.56 us: widen(): return jnp.concatenate([south, wide, north], axis=1)]
    unnamed x28 -> x12, local copies, waits for them, and re-layouts: 5.62 us -> 2.75 us
  transfers between devices with their start and end apart: 18 -> 0, of which waited for: 4 -> 0; matrix products, arithmetic and copies ran while one was open for 6% -> 0% of each run, Pallas kernels for 29% -> 0%
where the time goes in v4:
time: 146 us; the launch traced here: 145 us
  Pallas kernels  142 us (97%)
  local copies, waits for them, and re-layouts  2.75 us (2%)
    pallas_call x1, Pallas kernels, finish(): pl.pallas_call(finish_kernel, grid=(NB,), in_specs=[pack, pack, pack, pac...  31.5 us
    pallas_call x1, Pallas kernels, momentum(): pl.pallas_call(momentum_kernel, grid=(NB + 1,), in_specs=[cube, cube, pac...  30.5 us
    pallas_call x1, Pallas kernels, subcycles(): pl.pallas_call(functools.partial(subcycle_kernel, sizes), in_specs=[vm] *...  24.3 us
    pallas_call x1, Pallas kernels, gather(): pl.pallas_call(functools.partial(gather_kernel, sizes), in_specs=[vm] * l...  23 us
    pallas_call x1, Pallas kernels, tracers(): pl.pallas_call(tracer_kernel, grid=(NB // 2,), in_specs=[cube, cube, plan...  20 us
    pallas_call x1, Pallas kernels, edges(): pl.pallas_call(edge_kernel, grid=(NB,), in_specs=[strip(0), strip(3), str...  12.8 us

profile of v4, /device:TPU:0, one launch (start us, length us, event | category | flops | bytes accessed | tf_op | source)
XLA Modules:
  0.0 145.5 jit_solution(2974184833991599117)
XLA Ops:
  0.6 12.8 %edges.1 = (f32[96,128]{1,0:T(8,128)}, f32[96,128]{1,0:T(8,128)}, f32[2,48,512]{2,1,0:T(8,128)}, f32[3,48,512]{2,1,0:T(8,128)}) custom-call(f32[41,96,512]{2,1,0:T(8,128)} %u.1, f32[41,96,512]{2,1,0:T(8,128)} %u.1, f32[41,96,512]{2,1,0:T(8,128)} %v.1, f32[41,96,512]{2,1,0:T(8,128)} %v.1, f32[41,96,512]{2,1,0:T(8,128)} %t.1, f32[41,96,512]{2,1,0:T(8,128)} %s.1, ...), custom_call_target="tpu_custom_call" | custom-call | tf_op jit(solution)/shard_map/edges/pallas_call | solution.py:147
  13.4 23.0 %gather.1 = (f32[104,128]{1,0:T(8,128)}, f32[96,128]{1,0:T(8,128)}, f32[2,48,512]{2,1,0:T(8,128)}, f32[3,48,512]{2,1,0:T(8,128)}, f32[8,128]{1,0:T(8,128)}, /*in...) custom-call(s32[96,512]{1,0:T(8,128)} %kc.5, ...), custom_call_target="tpu_custom_call" | custom-call | tf_op jit(solution)/shard_map/gather/pallas_call | solution.py:416
  36.4 20.0 %tracers.1 = (f32[12,41,8,512]{3,2,1,0:T(8,128)}, f32[12,41,8,512]{3,2,1,0:T(8,128)}, f32[12,41,8,512]{3,2,1,0:T(8,128)}, f32[96,128]{1,0:T(8,128)}, f32[96,128]...) custom-call(f32[41,96,512]{2,1,0:T(8,128)} %t.1, f32[41,96,512]{2,1,0:T(8,128)} %s.1, s32[96,512]{1,0:T(8,128)} %kc.5, ...), custom_call_target="tpu_custom_call" | custom-call | tf_op jit(solution)/shard_map/tracers/pallas_call | solution.py:236
  56.4 0.0 copy-start.3
  56.4 30.5 %momentum.1 = (f32[12,41,8,512]{3,2,1,0:T(8,128)}, f32[12,41,8,512]{3,2,1,0:T(8,128)}, f32[96,512]{1,0:T(8,128)}, f32[96,512]{1,0:T(8,128)}, f32[96,512]{1,0:T(8...) custom-call(f32[41,96,512]{2,1,0:T(8,128)} %u.1, f32[41,96,512]{2,1,0:T(8,128)} %v.1, ...), custom_call_target="tpu_custom_call" | custom-call | tf_op jit(solution)/shard_map/momentum/pallas_call | solution.py:586
  86.9 0.0 copy-done.3
  86.9 0.7 copy.17.tide
  87.6 24.3 %subcycles.1 = (f32[96,512]{1,0:T(8,128)}, f32[96,512]{1,0:T(8,128)}, f32[96,512]{1,0:T(8,128)}, f32[104,640]{1,0:T(8,128)}, f32[104,640]{1,0:T(8,128)}, /*index...) custom-call(f32[176,640]{1,0:T(8,128)} %get-tuple-element.55.eta_i, ...), custom_call_target="tpu_custom_call" | custom-call | tf_op jit(solution)/shard_map/subcycles/pallas_call | solution.py:697
  112.0 0.0 copy-start.2
  112.0 0.0 copy-start.1
  112.0 0.0 copy-start
  112.0 31.5 %finish.1 = (f32[41,96,512]{2,1,0:T(8,128)}, f32[41,96,512]{2,1,0:T(8,128)}, f32[41,96,512]{2,1,0:T(8,128)}, f32[41,96,512]{2,1,0:T(8,128)}) custom-call(f32[12,41,8,512]{3,2,1,0:T(8,128)} %get-tuple-element.79.us_b, f32[12,41,8,512]{3,2,1,0:T(8,128)} %get-tuple-element.80.vs_b, f32[12,41,8,512]{3,2,1,0:T(8,128)} %get-tuple-element.81.t_b, ...), custom_call_target="tpu_custom_call" | custom-call | tf_op jit(solution)/shard_map/finish/pallas_call | solution.py:789
  143.4 0.0 copy-done.2
  143.5 0.7 copy.21
  144.1 0.0 copy-done.1
  144.1 0.7 copy.22
  144.8 0.0 copy-done
  144.8 0.7 copy.23
Async XLA Ops:
  56.4 30.5 %copy-start.3 = (f32[36,2]{0,1:T(2,128)S(1)}, f32[36,2]{0,1:T(2,128)}, u32[]{:S(2)}) copy-start(f32[36,2]{0,1:T(2,128)} %param.19) | copy-start | bytes 868
  112.0 31.5 %copy-start.2 = (f32[96,512]{1,0:T(8,128)S(1)}, f32[96,512]{1,0:T(8,128)}, u32[]{:S(2)}) copy-start(f32[96,512]{1,0:T(8,128)} %get-tuple-element.102) | copy-start | bytes 589828
  112.0 32.2 %copy-start.1 = (f32[96,512]{1,0:T(8,128)S(1)}, f32[96,512]{1,0:T(8,128)}, u32[]{:S(2)}) copy-start(f32[96,512]{1,0:T(8,128)} %get-tuple-element.103) | copy-start | bytes 589828
  112.0 32.8 %copy-start = (f32[96,512]{1,0:T(8,128)S(1)}, f32[96,512]{1,0:T(8,128)}, u32[]{:S(2)}) copy-start(f32[96,512]{1,0:T(8,128)} %get-tuple-element.104) | copy-start | bytes 589828

commit v5 on v4

--- a/solution.py
+++ b/solution.py
@@ -99,94 +99,142 @@
     return thick * mid, mid + half
 
 
-def edge_kernel(u0, u3, v0, v3, t0, s0, kc, hc, uf, vf, ul, vl, tf, sf, kr, hr, pke, pkw, rn, rs):
-    b = pl.program_id(0)
+class Exchange:
+    def __init__(self, sizes, send_sem, recv_sem):
+        self.rows, self.cols = sizes
+        self.row, self.col = lax.axis_index("row"), lax.axis_index("col")
+        self.sems = send_sem, recv_sem
+        self.used = 0
+
+    def inside(self, drow):
+        return (self.row + drow >= 0) & (self.row + drow < self.rows)
+
+    def at(self, drow, dcol):
+        return {"row": self.row + drow, "col": lax.rem(self.col + dcol + self.cols, self.cols)}
+
+    def when(self, drow, action):
+        if drow:
+            pl.when(self.inside(drow))(action)
+        else:
+            action()
+
+    def barrier(self):
+        ready = pltpu.get_barrier_semaphore()
+        for drow in SIDES:
+            for dcol in SIDES:
+                if drow or dcol:
+                    self.when(drow, functools.partial(pl.semaphore_signal, ready, device_id=self.at(drow, dcol), device_id_type=pl.DeviceIdType.MESH))
+        per_row = len(SIDES)
+        known = [self.inside(drow).astype(jnp.int32) for drow in SIDES if drow]
+        pl.semaphore_wait(ready, per_row - 1 + per_row * sum(known))
+
+    def clear(self, plan):
+        for _, dst, drow, _ in plan:
+            if drow:
+
+                @pl.when(jnp.logical_not(self.inside(-drow)))
+                def _():
+                    dst[:] = jnp.zeros(dst.shape, F32)
+
+    def make(self, plan):
+        out = []
+        for src, dst, drow, dcol in plan:
+            copy = pltpu.make_async_remote_copy(
+                src_ref=src,
+                dst_ref=dst,
+                send_sem=self.sems[0].at[self.used],
+                recv_sem=self.sems[1].at[self.used],
+                device_id=self.at(drow, dcol),
+                device_id_type=pl.DeviceIdType.MESH,
+            )
+            self.used += 1
+            out.append((copy, drow))
+        return out
+
+    def start(self, copies):
+        for copy, drow in copies:
+            self.when(drow, copy.start)
+
+    def wait(self, copies):
+        for copy, drow in copies:
+            self.when(drow, copy.wait_send)
+            self.when(-drow, copy.wait_recv)
+
+
+def pack_strips(pairs, to_west, to_east):
     lane = iota(TILE, 1)
-    cnt = kc[:]
-    thick = hc[:] / jnp.maximum(cnt, 1).astype(F32)
-    ae = jnp.zeros(TILE, F32)
-    aw = jnp.zeros(TILE, F32)
-    cum = jnp.zeros(TILE, F32)
-    for k in range(NL):
-        p, cum = pressure_step(t0[k], s0[k], k < cnt, cum, thick)
-        ae = jnp.where(lane == k, lane_to(u3[k], LN - 1, k), ae)
-        ae = jnp.where(lane == NL + k, lane_to(v3[k], LN - 1, NL + k), ae)
-        aw = jnp.where(lane == k, lane_to(u0[k], 0, k), aw)
-        aw = jnp.where(lane == NL + k, lane_to(v0[k], 0, NL + k), aw)
-        aw = jnp.where(lane == 2 * NL + k, lane_to(p, 0, 2 * NL + k), aw)
-    pke[:] = ae
-    pkw[:] = aw
-
-    @pl.when(b == 0)
-    def _():
-        count = kr[:]
-        dz = hr[:] / jnp.maximum(count, 1).astype(F32)
-        acc = jnp.zeros(ROW, F32)
-        for k in range(NL):
-            p, acc = pressure_step(tf[k], sf[k], k < count, acc, dz)
-            rn[0, one(k), :] = ul[k, LAST, :]
-            rn[1, one(k), :] = vl[k, LAST, :]
-            rs[0, one(k), :] = uf[k, FIRST, :]
-            rs[1, one(k), :] = vf[k, FIRST, :]
-            rs[2, one(k), :] = p[FIRST, :]
-        for i in range(3):
-            rs[i, NL:LP, :] = jnp.zeros((LP - NL, NC), F32)
-            if i < 2:
-                rn[i, NL:LP, :] = jnp.zeros((LP - NL, NC), F32)
-
-
-def edges(u, v, t, s, kmt, depth):
-    def strip(j):
-        return pl.BlockSpec((NL, 8, 128), lambda b: (0, b, j))
-
-    def slab(i):
-        return pl.BlockSpec(SLAB, lambda b: (0, i, 0))
-
-    col = pl.BlockSpec(TILE, lambda b: (b, 0))
-    row0 = pl.BlockSpec(ROW, lambda b: (0, 0))
-    return pl.pallas_call(
-        edge_kernel,
-        grid=(NB,),
-        in_specs=[strip(0), strip(3), strip(0), strip(3), strip(0), strip(0), col, col, slab(0), slab(0), slab(NB - 1), slab(NB - 1), slab(0), slab(0), row0, row0],
-        out_specs=[col, col, pl.BlockSpec((2, LP, NC), lambda b: (0, 0, 0)), pl.BlockSpec((3, LP, NC), lambda b: (0, 0, 0))],
-        out_shape=[
-            jax.ShapeDtypeStruct((NR, LN), F32),
-            jax.ShapeDtypeStruct((NR, LN), F32),
-            jax.ShapeDtypeStruct((2, LP, NC), F32),
-            jax.ShapeDtypeStruct((3, LP, NC), F32),
-        ],
-        name="edges",
-    )(u, u, v, v, t, s, kmt, depth, u, v, u, v, t, s, kmt, depth)
-
-
-def tracer_kernel(t, s, kc, hc, tm_b, sm_b, pr_b, pke, pkw, rn, rs_b, gains):
-    b = pl.program_id(0)
-    for half in range(2):
-        sl = tile_rows(half)
-        tm, sm, rs = tm_b.at[half], sm_b.at[half], rs_b.at[half]
-        mix_tracers(t.at[:, sl, :], s.at[:, sl, :], kc[sl, :], hc[sl, :], tm, sm, pr_b.at[half], pke.at[sl, :], pkw.at[sl, :], rs, gains)
-
-    @pl.when(b == NB // 2 - 1)
-    def _():
-        for k in range(NL):
-            rn[0, one(k), :] = tm[k, LAST, :]
-            rn[1, one(k), :] = sm[k, LAST, :]
-        for i in range(2):
-            rn[i, NL:LP, :] = jnp.zeros((LP - NL, NC), F32)
-
-
-def mix_tracers(t, s, cnt, depth, tm, sm, pr, pke, pkw, rs, gains):
+    first, last = slice(0, LN), slice(NC - LN, NC)
+
+    def turn(n):
+        q, sl = n // NB, tile_rows(n % NB)
+        b = pairs[q][-1]
+        return pltpu.roll(b[sl, first], HALF, axis=1), pltpu.roll(b[sl, last], HALF, axis=1)
+
+    def store(n, turned):
+        q, sl = n // NB, tile_rows(n % NB)
+        a = pairs[q][0]
+        to_west[q, sl, :] = jnp.where(lane < HALF, a[sl, first], turned[0])
+        to_east[q, sl, :] = jnp.where(lane < HALF, turned[1], a[sl, last])
+
+    skewed((turn, store), NB, NB * len(pairs))
+
+
+def strip_plan(to_west, to_east, strips):
+    top, bottom = pl.ds(NR - HR, HR), pl.ds(0, HR)
+    return [
+        (to_east, strips[0], 0, 1),
+        (to_west, strips[1], 0, -1),
+        (to_east.at[:, top], strips[2], 1, 1),
+        (to_west.at[:, top], strips[3], 1, -1),
+        (to_east.at[:, bottom], strips[4], -1, 1),
+        (to_west.at[:, bottom], strips[5], -1, -1),
+    ]
+
+
+def row_plan(planes, south, north):
+    plan = []
+    for i, x in enumerate(planes):
+        plan.append((x.at[pl.ds(NR - HR, HR), :], south.at[i], 1, 0))
+        plan.append((x.at[pl.ds(0, HR), :], north.at[i], -1, 0))
+    return plan
+
+
+def strip_scratch(n):
+    return [VM((n, NR, LN), F32)] * 4 + [VM((n, HR, LN), F32)] * 4
+
+
+def side(i, own, south, north):
+    if i < HT:
+        return south, tile_rows(i)
+    return (own, tile_rows(i - HT)) if i < HT + NB else (north, tile_rows(i - HT - NB))
+
+
+def halo_pair(i, q, strips):
+    (w, e), sl = side(i, strips[:2], strips[2:4], strips[4:])
+    lane = iota(TILE, 1)
+    w, e = w[q, sl, :], e[q, sl, :]
+    return jnp.where(lane < HALF, e, w), pltpu.roll(jnp.where(lane < HALF, w, e), HALF, axis=1)
+
+
+def mix_tracers(t, s, cnt, depth, strips, tm, sm, pr, pke, pkw, tke, tkw, rs, gains):
     lane = iota(TILE, 1)
     thick = depth / jnp.maximum(cnt, 1).astype(F32)
     c = couple(cnt, thick, KT)
     zero = jnp.zeros(ROW, F32)
     cum = lower = pt = ps = zero
     keep = zero
+    ae = aw = jnp.zeros(TILE, F32)
+    u0, u3, v0, v3 = strips
     for k in range(NL):
         wet = k < cnt
         tk, sk = t[k], s[k]
         p, cum = pressure_step(tk, sk, wet, cum, thick)
         pr[k] = p
+        for n, (x0, x3) in enumerate(((u0, u3), (v0, v3))):
+            base = NL * n + k
+            ae = jnp.where(lane == base, lane_to(x3[k], LN - 1, base), ae)
+            aw = jnp.where(lane == base, lane_to(x0[k], 0, base), aw)
+        aw = jnp.where(lane == 2 * NL + k, lane_to(p[:, :LN], 0, 2 * NL + k), aw)
         rs[2, one(k), :] = p[FIRST, :]
         upper = jnp.where(k + 1 < cnt, c, 0.0) if k + 1 < NL else zero
         top = 1.0 + lower * keep if k else jnp.ones_like(zero)
@@ -198,8 +246,9 @@
         tm[k] = pt
         sm[k] = ps
         lower = upper
-    ae = jnp.zeros(TILE, F32)
-    aw = jnp.zeros(TILE, F32)
+    pke[:] = ae
+    pkw[:] = aw
+    ae = aw = jnp.zeros(TILE, F32)
     bt = bs = zero
     for k in reversed(range(NL)):
         gain = gains[k]
@@ -212,170 +261,12 @@
         for x, base in ((bt, NL), (bs, 2 * NL)):
             ae = jnp.where(lane == base + k, lane_to(x[:, NC - LN :], LN - 1, base + k), ae)
             aw = jnp.where(lane == base + k, lane_to(x[:, :LN], 0, base + k), aw)
-    pke[:] = ae
-    pkw[:] = aw
-
-
-PACK = jax.ShapeDtypeStruct((NB,) + SLAB, F32)
-
-
-def block_major(f, n=1):
-    return pl.BlockSpec((n,) + SLAB, lambda b: (f(b), 0, 0, 0))
-
-
-def first_rows(f, n=1):
-    return pl.BlockSpec((n, 3, LP, NC), lambda b: (f(b), 0, 0, 0))
-
-
-def tracers(t, s, kmt, depth):
-    cube = pl.BlockSpec((NL, 16, NC), lambda b: (0, b, 0))
-    pack = block_major(lambda b: b, 2)
-    plane = pl.BlockSpec((16, NC), lambda b: (b, 0))
-    col = pl.BlockSpec((16, LN), lambda b: (b, 0))
-    rows = pl.BlockSpec((2, LP, NC), lambda b: (0, 0, 0))
-    return pl.pallas_call(
-        tracer_kernel,
-        grid=(NB // 2,),
-        in_specs=[cube, cube, plane, plane],
-        out_specs=[pack, pack, pack, col, col, rows, first_rows(lambda b: b, 2)],
-        out_shape=[PACK, PACK, PACK] + [jax.ShapeDtypeStruct((NR, LN), F32)] * 2 + [jax.ShapeDtypeStruct((2, LP, NC), F32), jax.ShapeDtypeStruct((NB, 3, LP, NC), F32)],
-        scratch_shapes=[VM(SLAB, F32)],
-        name="tracers",
-    )(t, s, kmt, depth)
-
-
-class Exchange:
-    def __init__(self, sizes, send_sem, recv_sem):
-        self.rows, self.cols = sizes
-        self.row, self.col = lax.axis_index("row"), lax.axis_index("col")
-        self.sems = send_sem, recv_sem
-        self.used = 0
-
-    def inside(self, drow):
-        return (self.row + drow >= 0) & (self.row + drow < self.rows)
-
-    def at(self, drow, dcol):
-        return {"row": self.row + drow, "col": lax.rem(self.col + dcol + self.cols, self.cols)}
-
-    def when(self, drow, action):
-        if drow:
-            pl.when(self.inside(drow))(action)
-        else:
-            action()
-
-    def barrier(self):
-        ready = pltpu.get_barrier_semaphore()
-        for drow in SIDES:
-            for dcol in SIDES:
-                if drow or dcol:
-                    self.when(drow, functools.partial(pl.semaphore_signal, ready, device_id=self.at(drow, dcol), device_id_type=pl.DeviceIdType.MESH))
-        per_row = len(SIDES)
-        known = [self.inside(drow).astype(jnp.int32) for drow in SIDES if drow]
-        pl.semaphore_wait(ready, per_row - 1 + per_row * sum(known))
-
-    def clear(self, plan):
-        for _, dst, drow, _ in plan:
-            if drow:
-
-                @pl.when(jnp.logical_not(self.inside(-drow)))
-                def _():
-                    dst[:] = jnp.zeros(dst.shape, F32)
-
-    def start(self, plan):
-        out = []
-        for src, dst, drow, dcol in plan:
-            copy = pltpu.make_async_remote_copy(
-                src_ref=src,
-                dst_ref=dst,
-                send_sem=self.sems[0].at[self.used],
-                recv_sem=self.sems[1].at[self.used],
-                device_id=self.at(drow, dcol),
-                device_id_type=pl.DeviceIdType.MESH,
-            )
-            self.used += 1
-            self.when(drow, copy.start)
-            out.append((copy, drow))
-        return out
-
-    def wait(self, copies):
-        for copy, drow in copies:
-            self.when(drow, copy.wait_send)
-            self.when(-drow, copy.wait_recv)
-
-
-def pack_strips(pairs, to_west, to_east):
-    lane = iota(TILE, 1)
-    first, last = slice(0, LN), slice(NC - LN, NC)
-
-    def turn(n):
-        q, sl = n // NB, tile_rows(n % NB)
-        b = pairs[q][-1]
-        return pltpu.roll(b[sl, first], HALF, axis=1), pltpu.roll(b[sl, last], HALF, axis=1)
-
-    def store(n, turned):
-        q, sl = n // NB, tile_rows(n % NB)
-        a = pairs[q][0]
-        to_west[q, sl, :] = jnp.where(lane < HALF, a[sl, first], turned[0])
-        to_east[q, sl, :] = jnp.where(lane < HALF, turned[1], a[sl, last])
-
-    skewed((turn, store), NB, NB * len(pairs))
-
-
-def strip_plan(to_west, to_east, strips):
-    top, bottom = pl.ds(NR - HR, HR), pl.ds(0, HR)
-    return [
-        (to_east, strips[0], 0, 1),
-        (to_west, strips[1], 0, -1),
-        (to_east.at[:, top], strips[2], 1, 1),
-        (to_west.at[:, top], strips[3], 1, -1),
-        (to_east.at[:, bottom], strips[4], -1, 1),
-        (to_west.at[:, bottom], strips[5], -1, -1),
-    ]
-
-
-def row_plan(planes, south, north):
-    plan = []
-    for i, x in enumerate(planes):
-        plan.append((x.at[pl.ds(NR - HR, HR), :], south.at[i], 1, 0))
-        plan.append((x.at[pl.ds(0, HR), :], north.at[i], -1, 0))
-    return plan
-
-
-def strip_scratch(n):
-    return [VM((n, NR, LN), F32)] * 4 + [VM((n, HR, LN), F32)] * 4
-
-
-def side(i, own, south, north):
-    if i < HT:
-        return south, tile_rows(i)
-    return (own, tile_rows(i - HT)) if i < HT + NB else (north, tile_rows(i - HT - NB))
-
-
-def halo_pair(i, q, strips):
-    (w, e), sl = side(i, strips[:2], strips[2:4], strips[4:])
-    lane = iota(TILE, 1)
-    w, e = w[q, sl, :], e[q, sl, :]
-    return jnp.where(lane < HALF, e, w), pltpu.roll(jnp.where(lane < HALF, w, e), HALF, axis=1)
-
-
-def gather_kernel(sizes, kmt, depth, eta, tu, tv, pke, pkw, prn, prs, rw, re, rsouth, rnorth, corner, ku, kv, du, dv, eta_o, tu_o, tv_o, kf, south, north, *rest):
-    to_west, to_east, *strips, send_sem, recv_sem = rest
-    net = Exchange(sizes, send_sem, recv_sem)
-    kf[:] = kmt[:].astype(F32)
-    planes = (kf, depth, eta, tu, tv)
-    pack_strips((planes[:2], planes[2:4], planes[4:]), to_west, to_east)
-    plan = [
-        (pke, rw.at[pl.ds(0, NR), :], 0, 1),
-        (pkw, re, 0, -1),
-        (prn, rsouth, 1, 0),
-        (prs, rnorth, -1, 0),
-        (pke.at[pl.ds(0, 8), :], rw.at[pl.ds(NR, 8), :], -1, 1),
-        (pkw.at[pl.ds(NR - 8, 8), :], corner, 1, -1),
-    ]
-    plan = strip_plan(to_west, to_east, strips) + plan + row_plan(planes, south, north)
-    net.clear(plan)
-    net.barrier()
-    net.wait(net.start(plan))
+    tke[:] = ae
+    tkw[:] = aw
+
+
+def wide_geometry(planes, strips, south, north, outs):
+    ku, kv, du, dv, *state = outs
     row = iota(WIDE, 0)
 
     def turn(i):
@@ -403,25 +294,116 @@
         du[sl, :] = 0.5 * (dz + dze)
         ku[sl, :] = k_u
         kv[sl, :] = k_v
-        for out, x, wet in zip((eta_o, tu_o, tv_o), vals, (k, k_u, k_v)):
+        for out, x, wet in zip(state, vals, (k, k_u, k_v)):
             out[sl, :] = only(wet > 0, x)
 
     skewed((turn, build, store), TILES, ET)
 
 
-def gather(sizes, *args):
-    vm = pl.BlockSpec(memory_space=VM)
-    outs = [shape(NR + 8, LN), shape(NR, LN), shape(2, LP, NC), shape(3, LP, NC), shape(8, LN)] + [shape(ER, EC)] * 7
-    sems = [pltpu.SemaphoreType.DMA((6 + 6 + 10,))] * 2
+def tracer_kernel(sizes, t, s, u0, u3, v0, v3, kc, hc, uf, ul, vf, vl, kmt, depth, eta, tu, tv, *rest):
+    tm_b, sm_b, pr_b, tke, tkw, rn, rs_b, *rest = rest
+    received, rown, wide, rest = rest[:5], rest[5], rest[6:13], rest[13:]
+    gains, kf, pke, pkw, prn, prs, south, north, rw, re, rsouth, rnorth, corner, to_west, to_east, *strips, send_sem, recv_sem = rest
+    b = pl.program_id(0)
+    last = NB // 2 - 1
+    net = Exchange(sizes, send_sem, recv_sem)
+    planes = (kf, depth, eta, tu, tv)
+    head = strip_plan(to_west, to_east, strips) + [(prn, rsouth, 1, 0)] + row_plan(planes, south, north)
+    middle = [(prs, rnorth, -1, 0), (pke.at[pl.ds(0, 8), :], rw.at[pl.ds(NR, 8), :], -1, 1)]
+    tail = [(pkw.at[pl.ds(NR - 8, 8), :], corner, 1, -1)]
+
+    def piece(i):
+        part = pl.ds(16 * i, 16)
+        return net.make([(pke.at[part, :], rw.at[part, :], 0, 1), (pkw.at[part, :], re.at[part, :], 0, -1)])
+
+    first_plan = head + middle + tail
+    head, middle, tail = net.make(head), net.make(middle), net.make(tail)
+    pieces = [piece(i) for i in range(last + 1)]
+
+    @pl.when(b == 0)
+    def _():
+        kf[:] = kmt[:].astype(F32)
+        pack_strips((planes[:2], planes[2:4], planes[4:]), to_west, to_east)
+        prn[:] = jnp.zeros(prn.shape, F32)
+        prs[:] = jnp.zeros(prs.shape, F32)
+        for k in range(NL):
+            for n, (lo, hi) in enumerate(((uf, ul), (vf, vl))):
+                prn[n, one(k), :] = hi[k, LAST, :]
+                prs[n, one(k), :] = lo[k, FIRST, :]
+        net.clear(first_plan)
+        net.barrier()
+        net.start(head)
+
+    for i in range(last):
+
+        @pl.when(b == i + 1)
+        def _():
+            net.start(pieces[i])
+
+    for half in range(2):
+        sl = tile_rows(half)
+        tm, sm, rs = tm_b.at[half], sm_b.at[half], rs_b.at[half]
+        out = pl.ds(pl.multiple_of(16 * b + 8 * half, 8), 8)
+        parts = [x.at[:, sl, :] for x in (t, s, u0, u3, v0, v3)]
+        mix_tracers(*parts[:2], kc[sl, :], hc[sl, :], parts[2:], tm, sm, pr_b.at[half], pke.at[out, :], pkw.at[out, :], tke.at[sl, :], tkw.at[sl, :], rs, gains)
+
+    @pl.when(b == 0)
+    def _():
+        prs[2] = rs_b[0, 2]
+        net.start(middle)
+
+    @pl.when(b == last)
+    def _():
+        net.start(pieces[last] + tail)
+        for k in range(NL):
+            rn[0, one(k), :] = tm[k, LAST, :]
+            rn[1, one(k), :] = sm[k, LAST, :]
+        rown[:] = prs[:]
+        net.wait(head)
+        wide_geometry(planes, strips, south, north, wide)
+        net.wait(middle + tail)
+        for copies in pieces:
+            net.wait(copies)
+        for out, x in zip(received, (rw, re, rsouth, rnorth, corner)):
+            out[:] = x[:]
+
+
+PACK = shape(NB, *SLAB)
+
+
+def block_major(f, n=1):
+    return pl.BlockSpec((n,) + SLAB, lambda b: (f(b), 0, 0, 0))
+
+
+def first_rows(f, n=1):
+    return pl.BlockSpec((n, 3, LP, NC), lambda b: (f(b), 0, 0, 0))
+
+
+def tracers(sizes, t, s, u, v, kmt, depth, eta, tu, tv):
+    def cols(width, j):
+        return pl.BlockSpec((NL, 16, width), lambda b: (0, b, j))
+
+    def slab(i):
+        return pl.BlockSpec(SLAB, lambda b: (0, i, 0))
+
+    pack = block_major(lambda b: b, 2)
+    plane = pl.BlockSpec((16, NC), lambda b: (b, 0))
+    col = pl.BlockSpec((16, LN), lambda b: (b, 0))
+    ends = [slab(0), slab(NB - 1)]
+    edge = [(NR + 8, LN), (NR, LN), (2, LP, NC), (3, LP, NC), (8, LN)]
+    extra = edge + [(3, LP, NC)] + [(ER, EC)] * 7
+    sems = [pltpu.SemaphoreType.DMA((6 + 1 + 10 + 3 + NB,))] * 2
+    rows = [VM((2, LP, NC), F32), VM((3, LP, NC), F32)] + [VM((5, HR, NC), F32)] * 2
     return pl.pallas_call(
-        functools.partial(gather_kernel, sizes),
-        in_specs=[vm] * len(args),
-        out_specs=[vm] * len(outs),
-        out_shape=outs,
-        scratch_shapes=[VM((NR, NC), F32)] + [VM((5, HR, NC), F32)] * 2 + strip_scratch(3) + sems,
+        functools.partial(tracer_kernel, sizes),
+        grid=(NB // 2,),
+        in_specs=[cols(NC, 0)] * 2 + [cols(LN, 0), cols(LN, 3)] * 2 + [plane] * 2 + ends * 2 + [whole(NR, NC)] * 5,
+        out_specs=[pack] * 3 + [col] * 2 + [whole(2, LP, NC), first_rows(lambda b: b, 2)] + [whole(*x) for x in extra],
+        out_shape=[PACK] * 3 + [shape(NR, LN)] * 2 + [shape(2, LP, NC), shape(NB, 3, LP, NC)] + [shape(*x) for x in extra],
+        scratch_shapes=[VM(SLAB, F32), VM((NR, NC), F32)] + [VM((NR, LN), F32)] * 2 + rows + [VM(x, F32) for x in edge] + strip_scratch(3) + sems,
         compiler_params=pltpu.CompilerParams(collective_id=0, has_side_effects=True),
-        name="gather",
-    )(*args)
+        name="tracers",
+    )(t, s, u, u, v, v, kmt, depth, u, u, v, v, kmt, depth, eta, tu, tv)
 
 
 def solve_pair(src_a, src_b, ca, cb, na, nb, out_a, out_b, gain_a, gain_b):
@@ -613,7 +595,8 @@
     ]
     net.clear(plan + late)
     net.barrier()
-    plan, late = net.start(plan), net.start(late)
+    plan, late = net.make(plan), net.make(late)
+    net.start(plan + late)
     row = iota(WIDE, 0)
     zero = jnp.zeros(WIDE, F32)
     ub[:] = jnp.zeros(ub.shape, F32)
@@ -801,11 +784,9 @@
     sizes = mesh.shape["row"], mesh.shape["col"]
 
     def local_step(u, v, t, s, eta, tu, tv, depth, kmt, tide):
-        pke, pkw, prn, prs = edges(u, v, t, s, kmt, depth)
-        rw, re, rsouth, rnorth, corner, *wide = gather(sizes, kmt, depth, eta, tu, tv, pke, pkw, prn, prs)
+        tm, sm, pr, tke, tkw, trn, first, rw, re, rsouth, rnorth, corner, rown, *wide = tracers(sizes, t, s, u, v, kmt, depth, eta, tu, tv)
         geo, state = wide[:4], wide[4:]
-        tm, sm, pr, tke, tkw, trn, first = tracers(t, s, kmt, depth)
-        us, vs, fx, fy, su, sv, uke, vrow = momentum(u, v, pr, first, geo, rw, re, rnorth, rsouth, prs, corner)
+        us, vs, fx, fy, su, sv, uke, vrow = momentum(u, v, pr, first, geo, rw, re, rnorth, rsouth, rown, corner)
         eta_n, u_n, v_n, ub, vb, fw, fe, fsouth, fnorth = subcycles(sizes, *state, *geo, fx, fy, tide, uke, tke, tkw, vrow, trn, first)
         uo, vo, to, so = finish(us, vs, tm, sm, first, kmt, geo, ub, vb, su, sv, fw, fe, fnorth, fsouth)
         return eta_n, u_n, v_n, uo, vo, to, so

time: 146 us -> 126 us (0.86)
  Pallas kernels: 142 us -> 122 us
    pallas_call x3 -> x1, Pallas kernels: 55.7 us -> 34.5 us  [tracers(): pl.pallas_call(functools.partial(tracer_kernel, sizes), grid=(NB // 2,),...]
where the time goes in v5:
time: 126 us; the launch traced here: 125 us
  Pallas kernels  122 us (97%)
  local copies, waits for them, and re-layouts  2.75 us (2%)
    pallas_call x1, Pallas kernels, tracers(): pl.pallas_call(functools.partial(tracer_kernel, sizes), grid=(NB // 2,),...  34.5 us
    pallas_call x1, Pallas kernels, finish(): pl.pallas_call(finish_kernel, grid=(NB,), in_specs=[pack, pack, pack, pac...  31.5 us
    pallas_call x1, Pallas kernels, momentum(): pl.pallas_call(momentum_kernel, grid=(NB + 1,), in_specs=[cube, cube, pac...  30.5 us
    pallas_call x1, Pallas kernels, subcycles(): pl.pallas_call(functools.partial(subcycle_kernel, sizes), in_specs=[vm] *...  25.5 us
    unnamed x12, local copies, waits for them, and re-layouts  2.75 us

profile of v5, /device:TPU:0, one launch (start us, length us, event | category | flops | bytes accessed | tf_op | source)
XLA Modules:
  0.0 125.5 jit_solution(10061540175580756284)
XLA Ops:
  0.6 34.5 %tracers.1 = (f32[12,41,8,512]{3,2,1,0:T(8,128)}, f32[12,41,8,512]{3,2,1,0:T(8,128)}, f32[12,41,8,512]{3,2,1,0:T(8,128)}, f32[96,128]{1,0:T(8,128)}, f32[96,128]...) custom-call(f32[41,96,512]{2,1,0:T(8,128)} %t.1, ...), custom_call_target="tpu_custom_call" | custom-call | tf_op jit(solution)/shard_map/tracers/pallas_call | solution.py:397
  35.2 0.0 copy-start.3
  35.2 30.5 %momentum.1 = (f32[12,41,8,512]{3,2,1,0:T(8,128)}, f32[12,41,8,512]{3,2,1,0:T(8,128)}, f32[96,512]{1,0:T(8,128)}, f32[96,512]{1,0:T(8,128)}, f32[96,512]{1,0:T(8...) custom-call(f32[41,96,512]{2,1,0:T(8,128)} %u.1, f32[41,96,512]{2,1,0:T(8,128)} %v.1, ...), custom_call_target="tpu_custom_call" | custom-call | tf_op jit(solution)/shard_map/momentum/pallas_call | solution.py:568
  65.7 0.0 copy-done.3
  65.7 0.7 copy.17.tide
  66.4 25.5 %subcycles.1 = (f32[96,512]{1,0:T(8,128)}, f32[96,512]{1,0:T(8,128)}, f32[96,512]{1,0:T(8,128)}, f32[104,640]{1,0:T(8,128)}, f32[104,640]{1,0:T(8,128)}, /*index...) custom-call(f32[176,640]{1,0:T(8,128)} %get-tuple-element.48.eta_i, ...), custom_call_target="tpu_custom_call" | custom-call | tf_op jit(solution)/shard_map/subcycles/pallas_call | solution.py:680
  91.9 0.0 copy-start.2
  91.9 0.0 copy-start.1
  91.9 0.0 copy-start
  91.9 31.5 %finish.1 = (f32[41,96,512]{2,1,0:T(8,128)}, f32[41,96,512]{2,1,0:T(8,128)}, f32[41,96,512]{2,1,0:T(8,128)}, f32[41,96,512]{2,1,0:T(8,128)}) custom-call(f32[12,41,8,512]{3,2,1,0:T(8,128)} %get-tuple-element.73.us_b, f32[12,41,8,512]{3,2,1,0:T(8,128)} %get-tuple-element.74.vs_b, f32[12,41,8,512]{3,2,1,0:T(8,128)} %get-tuple-element.75.t_b, ...), custom_call_target="tpu_custom_call" | custom-call | tf_op jit(solution)/shard_map/finish/pallas_call | solution.py:772
  123.4 0.0 copy-done.2
  123.4 0.7 copy.21
  124.1 0.0 copy-done.1
  124.1 0.7 copy.22
  124.8 0.0 copy-done
  124.8 0.7 copy.23
Async XLA Ops:
  35.2 30.5 %copy-start.3 = (f32[36,2]{0,1:T(2,128)S(1)}, f32[36,2]{0,1:T(2,128)}, u32[]{:S(2)}) copy-start(f32[36,2]{0,1:T(2,128)} %param.19) | copy-start | bytes 868
  91.9 31.5 %copy-start.2 = (f32[96,512]{1,0:T(8,128)S(1)}, f32[96,512]{1,0:T(8,128)}, u32[]{:S(2)}) copy-start(f32[96,512]{1,0:T(8,128)} %get-tuple-element.96) | copy-start | bytes 589828
  91.9 32.2 %copy-start.1 = (f32[96,512]{1,0:T(8,128)S(1)}, f32[96,512]{1,0:T(8,128)}, u32[]{:S(2)}) copy-start(f32[96,512]{1,0:T(8,128)} %get-tuple-element.97) | copy-start | bytes 589828
  91.9 32.8 %copy-start = (f32[96,512]{1,0:T(8,128)S(1)}, f32[96,512]{1,0:T(8,128)}, u32[]{:S(2)}) copy-start(f32[96,512]{1,0:T(8,128)} %get-tuple-element.98) | copy-start | bytes 589828

commit v6 on v5

--- a/solution.py
+++ b/solution.py
@@ -688,19 +688,13 @@
     )(*args)
 
 
-def finish_kernel(
-    us_b, vs_b, t_b, s_b, first, kc, ku, kv, du, dv, ub, vb, su, sv, kvs, dvs, vbs, rw, re, rnorth, rsouth, rown,
-    uo, vo, to, so, ct, cs,
-):
-    us, vs, t, s = us_b.at[0], vs_b.at[0], t_b.at[0], s_b.at[0]
+def finish_kernel(*refs):
+    ins, kvs, dvs, vbs, eta, tu, tv, rnorth, rsouth, rown, eta_o, tu_o, tv_o, uo, vo, to, so, ct, cs = refs[:23], *refs[23:]
+    cubes, planes, wide = ins[:4], ins[4:9], ins[9:]
     b = pl.program_id(0)
-    last = b == NB - 1
-    row = iota(ROW, 0)
-    lane = iota(TILE, 1)
-
-    def correction(mean, total, k, dz):
-        deep = k * dz
-        return (mean - total) / jnp.where(deep > 0, deep, 1.0)
+    eta_o[:] = eta[:]
+    tu_o[:] = tu[:]
+    tv_o[:] = tv[:]
 
     @pl.when(b == 0)
     def _():
@@ -714,11 +708,26 @@
             ct[k, LAST, :] = ft[one(k), :]
             cs[k, LAST, :] = fs[one(k), :]
 
-    kx, ky, cnt = ku[:], kv[:, :NC], kc[:]
-    rwv, rev = rw[:], re[:]
-    tot = jnp.concatenate([su[:], lane_to(rwv, 3 * NL, LN - 1)], axis=1)
+    for half in range(2):
+        sl = tile_rows(half)
+        outs = [x.at[:, sl, :] for x in (uo, vo, to, so)]
+        last = (b == NB // 2 - 1) if half else None
+        finish_rows(last, *[x.at[half] for x in cubes], *[x[sl, :] for x in planes], *wide[half::2], rnorth, *outs, ct, cs)
+
+
+def correction(mean, total, k, dz):
+    deep = k * dz
+    return (mean - total) / jnp.where(deep > 0, deep, 1.0)
+
+
+def finish_rows(last, us, vs, t, s, cnt, su, sv, rwv, rev, ku, kv, du, dv, ub, vb, first, rnorth, uo, vo, to, so, ct, cs):
+    row = iota(ROW, 0)
+    lane = iota(TILE, 1)
+
+    kx, ky = ku[:], kv[:, :NC]
+    tot = jnp.concatenate([su, lane_to(rwv, 3 * NL, LN - 1)], axis=1)
     cx = correction(ub[:], tot, kx, du[:])
-    cy = correction(vb[:, :NC], sv[:], ky, dv[:, :NC])
+    cy = correction(vb[:, :NC], sv, ky, dv[:, :NC])
     fields = ((t, to, ct), (s, so, cs))
 
     def load(k):
@@ -745,7 +754,9 @@
         hy = (0.5 * DT) * ve
         for i, (x, out, carry) in enumerate(fields):
             own = x[k]
-            north = jnp.where(last, rnorth[i, one(k), :], first[0, i, one(k), :])
+            north = first[0, i, one(k), :]
+            if last is not None:
+                north = jnp.where(last, rnorth[i, one(k), :], north)
             fy = hy * (own + up_row(own, north, row))
             new = own - (div[i] + (fy - down_row(fy, carry[k], row)))
             carry[k] = fy
@@ -754,30 +765,31 @@
     skewed((load, east, flux, store), GROUP)
 
 
-def finish(us, vs, tm, sm, first, kmt, geo, ub, vb, su, sv, rw, re, rnorth, rsouth):
-    ku, kv, du, dv = geo
-    cube = pl.BlockSpec(SLAB, lambda b: (0, b, 0))
-    pack = block_major(lambda b: b)
-    wide = pl.BlockSpec(WIDE, lambda b: (HT + b, 0))
-    wids = pl.BlockSpec(WIDE, lambda b: (HT - 1, 0))
-    bar = pl.BlockSpec(WIDE, lambda b: (b + 1, 0))
-    bars = pl.BlockSpec(WIDE, lambda b: (0, 0))
-    plane = pl.BlockSpec(ROW, lambda b: (b, 0))
-    col = pl.BlockSpec(TILE, lambda b: (b, 0))
-    big = jax.ShapeDtypeStruct((NL, NR, NC), F32)
-
-    def rows(n):
-        return pl.BlockSpec((n, LP, NC), lambda b: (0, 0, 0))
-
+def finish(us, vs, tm, sm, first, kmt, geo, ub, vb, su, sv, rw, re, rnorth, rsouth, state):
+    kv, dv = geo[1], geo[3]
+
+    def rows(width):
+        return pl.BlockSpec((16, width), lambda b: (b, 0))
+
+    def pair(start):
+        return [pl.BlockSpec(WIDE, lambda b, h=h: (start + 2 * b + h, 0)) for h in range(2)]
+
+    def fixed(i):
+        return pl.BlockSpec(WIDE, lambda b: (i, 0))
+
+    ahead = [first_rows(lambda b: 2 * b + 1), first_rows(lambda b: jnp.minimum(2 * b + 2, NB - 1))]
+    cube = pl.BlockSpec((NL, 16, NC), lambda b: (0, b, 0))
+    south = [fixed(HT - 1)] * 2 + [fixed(0)]
+    wide = [x for x in (*geo, ub, vb, first) for _ in range(2)]
     return pl.pallas_call(
         finish_kernel,
-        grid=(NB,),
-        in_specs=[pack, pack, pack, pack, first_rows(lambda b: jnp.minimum(b + 1, NB - 1)), plane, wide, wide, wide, wide, bar, bar, plane, plane, wids, wids, bars, col, col, rows(3), rows(3), first_rows(lambda b: 0)],
-        out_specs=[cube] * 4,
-        out_shape=[big] * 4,
+        grid=(NB // 2,),
+        in_specs=[block_major(lambda b: b, 2)] * 4 + [rows(NC)] * 3 + [rows(LN)] * 2 + pair(HT) * 4 + pair(1) * 2 + ahead + south + [rows(NC)] * 3 + [whole(3, LP, NC)] * 2 + [first_rows(lambda b: 0)],
+        out_specs=[rows(NC)] * 3 + [cube] * 4,
+        out_shape=[shape(NR, NC)] * 3 + [shape(NL, NR, NC)] * 4,
         scratch_shapes=[VM(SLAB, F32)] * 2,
         name="finish",
-    )(us, vs, tm, sm, first, kmt, ku, kv, du, dv, ub, vb, su, sv, kv, dv, vb, rw, re, rnorth, rsouth, first)
+    )(us, vs, tm, sm, kmt, su, sv, rw, re, *wide, kv, dv, vb, *state, rnorth, rsouth, first)
 
 
 def solution(mesh):
@@ -788,8 +800,7 @@
         geo, state = wide[:4], wide[4:]
         us, vs, fx, fy, su, sv, uke, vrow = momentum(u, v, pr, first, geo, rw, re, rnorth, rsouth, rown, corner)
         eta_n, u_n, v_n, ub, vb, fw, fe, fsouth, fnorth = subcycles(sizes, *state, *geo, fx, fy, tide, uke, tke, tkw, vrow, trn, first)
-        uo, vo, to, so = finish(us, vs, tm, sm, first, kmt, geo, ub, vb, su, sv, fw, fe, fnorth, fsouth)
-        return eta_n, u_n, v_n, uo, vo, to, so
+        return finish(us, vs, tm, sm, first, kmt, geo, ub, vb, su, sv, fw, fe, fnorth, fsouth, (eta_n, u_n, v_n))
 
     cube, plane = P(None, "row", "col"), P("row", "col")
     return jax.shard_map(

time: 126 us -> 122 us (0.968)
  Pallas kernels: 122 us -> 120 us
  local copies, waits for them, and re-layouts: 2.75 us -> 1.37 us
    pallas_call x1, Pallas kernels: 31.5 us -> 29.8 us  [finish(): pl.pallas_call(finish_kernel, grid=(NB // 2,), in_specs=[block_major(lamb...]
    unnamed x12 -> x1, local copies, waits for them, and re-layouts: 2.75 us -> 1.37 us
where the time goes in v6:
time: 122 us
  Pallas kernels  120 us (98%)
  local copies, waits for them, and re-layouts  1.37 us (1%)
    pallas_call x1, Pallas kernels, tracers(): pl.pallas_call(functools.partial(tracer_kernel, sizes), grid=(NB // 2,),...  34.4 us
    pallas_call x1, Pallas kernels, momentum(): pl.pallas_call(momentum_kernel, grid=(NB + 1,), in_specs=[cube, cube, pac...  30.4 us
    pallas_call x1, Pallas kernels, finish(): pl.pallas_call(finish_kernel, grid=(NB // 2,), in_specs=[block_major(lamb...  29.8 us
    pallas_call x1, Pallas kernels, subcycles(): pl.pallas_call(functools.partial(subcycle_kernel, sizes), in_specs=[vm] *...  25.6 us

profile of v6, /device:TPU:0, one launch (start us, length us, event | category | flops | bytes accessed | tf_op | source)
XLA Modules:
  0.0 122.3 jit_solution(9467043841828907878)
XLA Ops:
  0.6 1.4 %copy.17.tide = f32[36,2]{1,0:T(8,128)} copy(f32[36,2]{0,1:T(2,128)} %param.19) | data formatting | bytes 576 | tf_op args[9]
  2.0 34.4 %tracers.1 = (f32[12,41,8,512]{3,2,1,0:T(8,128)}, f32[12,41,8,512]{3,2,1,0:T(8,128)}, f32[12,41,8,512]{3,2,1,0:T(8,128)}, f32[96,128]{1,0:T(8,128)}, f32[96,128]...) custom-call(f32[41,96,512]{2,1,0:T(8,128)} %t.1, ...), custom_call_target="tpu_custom_call" | custom-call | tf_op jit(solution)/shard_map/tracers/pallas_call | solution.py:397
  36.4 30.4 %momentum.1 = (f32[12,41,8,512]{3,2,1,0:T(8,128)}, f32[12,41,8,512]{3,2,1,0:T(8,128)}, f32[96,512]{1,0:T(8,128)}, f32[96,512]{1,0:T(8,128)}, f32[96,512]{1,0:T(8...) custom-call(f32[41,96,512]{2,1,0:T(8,128)} %u.1, f32[41,96,512]{2,1,0:T(8,128)} %v.1, ...), custom_call_target="tpu_custom_call" | custom-call | tf_op jit(solution)/shard_map/momentum/pallas_call | solution.py:568
  66.9 25.6 %subcycles.1 = (f32[96,512]{1,0:T(8,128)}, f32[96,512]{1,0:T(8,128)}, f32[96,512]{1,0:T(8,128)}, f32[104,640]{1,0:T(8,128)}, f32[104,640]{1,0:T(8,128)}, /*index...) custom-call(f32[176,640]{1,0:T(8,128)} %get-tuple-element.62.eta_i, ...), custom_call_target="tpu_custom_call" | custom-call | tf_op jit(solution)/shard_map/subcycles/pallas_call | solution.py:680
  92.5 29.8 %finish.1 = (f32[96,512]{1,0:T(8,128)}, f32[96,512]{1,0:T(8,128)}, f32[96,512]{1,0:T(8,128)}, f32[41,96,512]{2,1,0:T(8,128)}, f32[41,96,512]{2,1,0:T(8,128)}, /*...) custom-call(f32[12,41,8,512]{3,2,1,0:T(8,128)} %get-tuple-element.56.refs_0_, f32[12,41,8,512]{3,2,1,0:T(8,128)} %get-tuple-element.57.refs_1_, ...), custom_call_target="tpu_custom_call" | custom-call | tf_op jit(solution)/shard_map/finish/pallas_call | solution.py:784

commit v7 on v6

--- a/solution.py
+++ b/solution.py
@@ -368,7 +368,8 @@
             out[:] = x[:]
 
 
-PACK = shape(NB, *SLAB)
+PACK = VM((NB,) + SLAB, F32)
+PACK_HBM = pltpu.HBM((NB,) + SLAB, F32)
 
 
 def block_major(f, n=1):
@@ -399,9 +400,9 @@
         grid=(NB // 2,),
         in_specs=[cols(NC, 0)] * 2 + [cols(LN, 0), cols(LN, 3)] * 2 + [plane] * 2 + ends * 2 + [whole(NR, NC)] * 5,
         out_specs=[pack] * 3 + [col] * 2 + [whole(2, LP, NC), first_rows(lambda b: b, 2)] + [whole(*x) for x in extra],
-        out_shape=[PACK] * 3 + [shape(NR, LN)] * 2 + [shape(2, LP, NC), shape(NB, 3, LP, NC)] + [shape(*x) for x in extra],
+        out_shape=[PACK] * 2 + [PACK_HBM] + [shape(NR, LN)] * 2 + [shape(2, LP, NC), pltpu.HBM((NB, 3, LP, NC), F32)] + [shape(*x) for x in extra],
         scratch_shapes=[VM(SLAB, F32), VM((NR, NC), F32)] + [VM((NR, LN), F32)] * 2 + rows + [VM(x, F32) for x in edge] + strip_scratch(3) + sems,
-        compiler_params=pltpu.CompilerParams(collective_id=0, has_side_effects=True),
+        compiler_params=pltpu.CompilerParams(collective_id=0, has_side_effects=True, vmem_limit_bytes=26 << 20),
         name="tracers",
     )(t, s, u, u, v, v, kmt, depth, u, u, v, v, kmt, depth, eta, tu, tv)
 
@@ -570,8 +571,9 @@
         grid=(NB + 1,),
         in_specs=[cube, cube, pack, first_rows(ahead), widn, widn, near, near, near, near, wids, wids, colw, cole, col, rows(3), rows(2), rows(3), pl.BlockSpec(TILE, lambda b: (0, 0))],
         out_specs=[pack, pack, plane, plane, plane, plane, col, pl.BlockSpec((LP, NC), lambda b: (0, 0))],
-        out_shape=[PACK, PACK, flat, flat, flat, flat, jax.ShapeDtypeStruct((NR, LN), F32), jax.ShapeDtypeStruct((LP, NC), F32)],
+        out_shape=[PACK, PACK_HBM, flat, flat, flat, flat, jax.ShapeDtypeStruct((NR, LN), F32), jax.ShapeDtypeStruct((LP, NC), F32)],
         scratch_shapes=[VM(SLAB, F32)] * 6 + [VM((NL,) + WIDE, F32)] * 2,
+        compiler_params=pltpu.CompilerParams(vmem_limit_bytes=22 << 20),
         name="momentum",
     )(u, v, p, first, ku, kv, ku, kv, du, dv, ku, kv, rw, re, re, rnorth, rsouth, rown, corner)
 
@@ -683,7 +685,7 @@
         out_specs=[vm] * len(outs),
         out_shape=outs,
         scratch_shapes=wide + [VM((NR, LN), F32)] + [VM((2, HR, NC), F32)] * 2 + strip_scratch(1) + sems,
-        compiler_params=pltpu.CompilerParams(collective_id=1, has_side_effects=True),
+        compiler_params=pltpu.CompilerParams(collective_id=1, has_side_effects=True, vmem_limit_bytes=22 << 20),
         name="subcycles",
     )(*args)
 
@@ -788,6 +790,7 @@
         out_specs=[rows(NC)] * 3 + [cube] * 4,
         out_shape=[shape(NR, NC)] * 3 + [shape(NL, NR, NC)] * 4,
         scratch_shapes=[VM(SLAB, F32)] * 2,
+        compiler_params=pltpu.CompilerParams(vmem_limit_bytes=26 << 20),
         name="finish",
     )(us, vs, tm, sm, kmt, su, sv, rw, re, *wide, kv, dv, vb, *state, rnorth, rsouth, first)
 
@@ -796,10 +799,16 @@
     sizes = mesh.shape["row"], mesh.shape["col"]
 
     def local_step(u, v, t, s, eta, tu, tv, depth, kmt, tide):
+        u, v, t, s = (pltpu.with_memory_space_constraint(x, pltpu.HBM) for x in (u, v, t, s))
         tm, sm, pr, tke, tkw, trn, first, rw, re, rsouth, rnorth, corner, rown, *wide = tracers(sizes, t, s, u, v, kmt, depth, eta, tu, tv)
         geo, state = wide[:4], wide[4:]
+        tm, sm = (pltpu.with_memory_space_constraint(x, pltpu.VMEM) for x in (tm, sm))
+        first = pltpu.with_memory_space_constraint(first, pltpu.HBM)
+        pr = pltpu.with_memory_space_constraint(pr, pltpu.HBM)
         us, vs, fx, fy, su, sv, uke, vrow = momentum(u, v, pr, first, geo, rw, re, rnorth, rsouth, rown, corner)
         eta_n, u_n, v_n, ub, vb, fw, fe, fsouth, fnorth = subcycles(sizes, *state, *geo, fx, fy, tide, uke, tke, tkw, vrow, trn, first)
+        us = pltpu.with_memory_space_constraint(us, pltpu.VMEM)
+        vs = pltpu.with_memory_space_constraint(vs, pltpu.HBM)
         return finish(us, vs, tm, sm, first, kmt, geo, ub, vb, su, sv, fw, fe, fnorth, fsouth, (eta_n, u_n, v_n))
 
     cube, plane = P(None, "row", "col"), P("row", "col")

time: 122 us -> 107 us (0.88)
  Pallas kernels: 120 us -> 100 us
  local copies, waits for them, and re-layouts: 1.37 us -> 5.41 us
    pallas_call x1, Pallas kernels: 34.4 us -> 26.1 us  [tracers(): pl.pallas_call(functools.partial(tracer_kernel, sizes), grid=(NB // 2,),...]
    pallas_call x1, Pallas kernels: 29.8 us -> 21.6 us  [finish(): pl.pallas_call(finish_kernel, grid=(NB // 2,), in_specs=[block_major(lamb...]
    unnamed x1 -> x13, local copies, waits for them, and re-layouts: 1.37 us -> 5.41 us
    pallas_call x1, Pallas kernels: 25.6 us -> 23.1 us  [subcycles(): pl.pallas_call(functools.partial(subcycle_kernel, sizes), in_specs=[vm] *...]
where the time goes in v7:
time: 107 us; the launch traced here: 106 us
  Pallas kernels  100 us (93%)
  local copies, waits for them, and re-layouts  5.41 us (5%)
    pallas_call x1, Pallas kernels, momentum(): pl.pallas_call(momentum_kernel, grid=(NB + 1,), in_specs=[cube, cube, pac...  29.4 us
    pallas_call x1, Pallas kernels, tracers(): pl.pallas_call(functools.partial(tracer_kernel, sizes), grid=(NB // 2,),...  26.1 us
    pallas_call x1, Pallas kernels, subcycles(): pl.pallas_call(functools.partial(subcycle_kernel, sizes), in_specs=[vm] *...  23.1 us
    pallas_call x1, Pallas kernels, finish(): pl.pallas_call(finish_kernel, grid=(NB // 2,), in_specs=[block_major(lamb...  21.6 us
    unnamed x13, local copies, waits for them, and re-layouts  5.41 us

profile of v7, /device:TPU:0, one launch (start us, length us, event | category | flops | bytes accessed | tf_op | source)
XLA Modules:
  0.0 106.2 jit_solution(12663004315659294280)
XLA Ops:
  0.6 0.8 copy.17.tide
  1.4 0.0 copy-start
  1.4 0.9 copy-done
  2.3 0.0 copy-start.2
  2.3 0.9 copy-done.2
  3.3 0.0 copy-start.3
  3.3 0.9 copy-done.3
  4.2 0.0 copy-start.4
  4.2 0.9 copy-done.4
  5.1 0.0 copy-start.5
  5.1 0.9 copy-done.5
  6.0 26.1 %tracers.1 = (f32[12,41,8,512]{3,2,1,0:T(8,128)S(1)}, f32[12,41,8,512]{3,2,1,0:T(8,128)S(1)}, f32[12,41,8,512]{3,2,1,0:T(8,128)}, f32[96,128]{1,0:T(8,128)S(1)},...) custom-call(f32[41,96,512]{2,1,0:T(8,128)} %t.1, ...), custom_call_target="tpu_custom_call" | custom-call | tf_op jit(solution)/shard_map/tracers/pallas_call | solution.py:398
  32.1 0.0 copy-start.1
  32.1 29.4 %momentum.1 = (f32[12,41,8,512]{3,2,1,0:T(8,128)S(1)}, f32[12,41,8,512]{3,2,1,0:T(8,128)}, f32[96,512]{1,0:T(8,128)S(1)}, f32[96,512]{1,0:T(8,128)S(1)}, f32[96,...) custom-call(f32[41,96,512]{2,1,0:T(8,128)} %u.1, f32[41,96,512]{2,1,0:T(8,128)} %v.1, ...), custom_call_target="tpu_custom_call" | custom-call | tf_op jit(solution)/shard_map/momentum/pallas_call | solution.py:569
  61.5 23.1 %subcycles.1 = (f32[96,512]{1,0:T(8,128)S(1)}, f32[96,512]{1,0:T(8,128)S(1)}, f32[96,512]{1,0:T(8,128)S(1)}, f32[104,640]{1,0:T(8,128)S(1)}, f32[104,640]{1,0:T(...) custom-call(f32[176,640]{1,0:T(8,128)S(1)} %get-tuple-element.62.eta, ...), custom_call_target="tpu_custom_call" | custom-call | tf_op jit(solution)/shard_map/subcycles/pallas_call | solution.py:682
  84.6 0.0 copy-done.1
  84.6 21.6 %finish.1 = (f32[96,512]{1,0:T(8,128)}, f32[96,512]{1,0:T(8,128)}, f32[96,512]{1,0:T(8,128)}, f32[41,96,512]{2,1,0:T(8,128)}, f32[41,96,512]{2,1,0:T(8,128)}, /*...) custom-call(f32[12,41,8,512]{3,2,1,0:T(8,128)S(1)} %get-tuple-element.56.refs_0_, ...), custom_call_target="tpu_custom_call" | custom-call | tf_op jit(solution)/shard_map/finish/pallas_call | solution.py:786
Async XLA Ops:
  1.4 0.9 copy-start
  2.3 0.9 copy-start.2
  3.3 0.9 copy-start.3
  4.2 0.9 copy-start.4
  5.1 0.9 copy-start.5
  32.1 52.5 %copy-start.1 = (s32[96,512]{1,0:T(8,128)S(1)}, s32[96,512]{1,0:T(8,128)}, u32[]{:S(2)}) copy-start(s32[96,512]{1,0:T(8,128)} %refs_4_.1) | copy-start | bytes 589828

commit v8 on v7

--- a/solution.py
+++ b/solution.py
@@ -624,7 +624,7 @@
 
     def stage(first, last, lo, hi):
         def step(n, _):
-            tx, ty = tide[n, 0], tide[n, 1]
+            tx, ty = tide[0, n], tide[1, n]
             w = norm * ((n + 1) * (SUB - n)).astype(F32)
 
             def west(i):
@@ -799,14 +799,14 @@
     sizes = mesh.shape["row"], mesh.shape["col"]
 
     def local_step(u, v, t, s, eta, tu, tv, depth, kmt, tide):
-        u, v, t, s = (pltpu.with_memory_space_constraint(x, pltpu.HBM) for x in (u, v, t, s))
+        u, v, t, s, eta, tu, tv, depth, kmt = (pltpu.with_memory_space_constraint(x, pltpu.HBM) for x in (u, v, t, s, eta, tu, tv, depth, kmt))
         tm, sm, pr, tke, tkw, trn, first, rw, re, rsouth, rnorth, corner, rown, *wide = tracers(sizes, t, s, u, v, kmt, depth, eta, tu, tv)
         geo, state = wide[:4], wide[4:]
         tm, sm = (pltpu.with_memory_space_constraint(x, pltpu.VMEM) for x in (tm, sm))
         first = pltpu.with_memory_space_constraint(first, pltpu.HBM)
         pr = pltpu.with_memory_space_constraint(pr, pltpu.HBM)
         us, vs, fx, fy, su, sv, uke, vrow = momentum(u, v, pr, first, geo, rw, re, rnorth, rsouth, rown, corner)
-        eta_n, u_n, v_n, ub, vb, fw, fe, fsouth, fnorth = subcycles(sizes, *state, *geo, fx, fy, tide, uke, tke, tkw, vrow, trn, first)
+        eta_n, u_n, v_n, ub, vb, fw, fe, fsouth, fnorth = subcycles(sizes, *state, *geo, fx, fy, tide.T, uke, tke, tkw, vrow, trn, first)
         us = pltpu.with_memory_space_constraint(us, pltpu.VMEM)
         vs = pltpu.with_memory_space_constraint(vs, pltpu.HBM)
         return finish(us, vs, tm, sm, first, kmt, geo, ub, vb, su, sv, fw, fe, fnorth, fsouth, (eta_n, u_n, v_n))

time: 107 us -> 102 us (0.953)
  local copies, waits for them, and re-layouts: 5.41 us -> 0.01 us
    unnamed x13 -> x2, local copies, waits for them, and re-layouts: 5.41 us -> 0.01 us
    pallas_call x1, Pallas kernels: 26.1 us -> 27.4 us  [tracers(): pl.pallas_call(functools.partial(tracer_kernel, sizes), grid=(NB // 2,),...]
where the time goes in v8:
time: 102 us; the launch traced here: 101 us
  Pallas kernels  101 us (99%)
    pallas_call x1, Pallas kernels, momentum(): pl.pallas_call(momentum_kernel, grid=(NB + 1,), in_specs=[cube, cube, pac...  29.1 us
    pallas_call x1, Pallas kernels, tracers(): pl.pallas_call(functools.partial(tracer_kernel, sizes), grid=(NB // 2,),...  27.4 us
    pallas_call x1, Pallas kernels, subcycles(): pl.pallas_call(functools.partial(subcycle_kernel, sizes), in_specs=[vm] *...  22.7 us
    pallas_call x1, Pallas kernels, finish(): pl.pallas_call(finish_kernel, grid=(NB // 2,), in_specs=[block_major(lamb...  21.5 us

profile of v8, /device:TPU:0, one launch (start us, length us, event | category | flops | bytes accessed | tf_op | source)
XLA Modules:
  0.0 101.4 jit_solution(13350069913471170676)
XLA Ops:
  0.6 27.4 %tracers.1 = (f32[12,41,8,512]{3,2,1,0:T(8,128)S(1)}, f32[12,41,8,512]{3,2,1,0:T(8,128)S(1)}, f32[12,41,8,512]{3,2,1,0:T(8,128)}, f32[96,128]{1,0:T(8,128)S(1)},...) custom-call(f32[41,96,512]{2,1,0:T(8,128)} %t.1, ...), custom_call_target="tpu_custom_call" | custom-call | tf_op jit(solution)/shard_map/tracers/pallas_call | solution.py:398
  28.1 0.0 copy-start
  28.1 29.1 %momentum.1 = (f32[12,41,8,512]{3,2,1,0:T(8,128)S(1)}, f32[12,41,8,512]{3,2,1,0:T(8,128)}, f32[96,512]{1,0:T(8,128)S(1)}, f32[96,512]{1,0:T(8,128)S(1)}, f32[96,...) custom-call(f32[41,96,512]{2,1,0:T(8,128)} %u.1, f32[41,96,512]{2,1,0:T(8,128)} %v.1, ...), custom_call_target="tpu_custom_call" | custom-call | tf_op jit(solution)/shard_map/momentum/pallas_call | solution.py:569
  57.2 0.0 copy-done
  57.2 22.7 %subcycles.1 = (f32[96,512]{1,0:T(8,128)S(1)}, f32[96,512]{1,0:T(8,128)S(1)}, f32[96,512]{1,0:T(8,128)S(1)}, f32[104,640]{1,0:T(8,128)S(1)}, f32[104,640]{1,0:T(...) custom-call(f32[176,640]{1,0:T(8,128)S(1)} %get-tuple-element.62.eta, ...), custom_call_target="tpu_custom_call" | custom-call | tf_op jit(solution)/shard_map/subcycles/pallas_call | solution.py:682
  79.9 21.5 %finish.1 = (f32[96,512]{1,0:T(8,128)}, f32[96,512]{1,0:T(8,128)}, f32[96,512]{1,0:T(8,128)}, f32[41,96,512]{2,1,0:T(8,128)}, f32[41,96,512]{2,1,0:T(8,128)}, /*...) custom-call(f32[12,41,8,512]{3,2,1,0:T(8,128)S(1)} %get-tuple-element.56.refs_0_, ...), custom_call_target="tpu_custom_call" | custom-call | tf_op jit(solution)/shard_map/finish/pallas_call | solution.py:786
Async XLA Ops:
  28.1 29.1 %copy-start = (f32[36,2]{0,1:T(2,128)S(1)}, f32[36,2]{0,1:T(2,128)}, u32[]{:S(2)}) copy-start(f32[36,2]{0,1:T(2,128)} %param.19) | copy-start | bytes 868

commit v9 on v8

--- a/solution.py
+++ b/solution.py
@@ -17,7 +17,8 @@
 EC = NC + 128
 NB = NR // 8
 SUB = 36
-GROUP = 2
+GROUP_M = 2
+GROUP_F = 3
 HALF = 64
 SIDES = (-1, 0, 1)
 FIRST, LAST = slice(0, 1), slice(7, 8)
@@ -474,9 +475,9 @@
         s_ve = jnp.where(iota((LP, NC), 1) == NC - 1, edge, from_east(s_v))
         u_0 = only(lev < kxn[FIRST, :NC], rown[0])
         v_0 = only(lev < kyn[FIRST, :NC], rown[1])
-        c_s = 0.25 * ((s_v + s_ve) * (s_u + u_0))
-        h_s = s_v + v_0
-        h_s = 0.25 * (h_s * h_s) + rown[2]
+        c_s = (0.25 * (s_v + s_ve)) * (s_u + u_0)
+        h_s = 0.5 * (s_v + v_0)
+        h_s = h_s * h_s + rown[2]
         for k in range(NL):
             cc[k, LAST, :] = c_s[one(k), :]
             hh[k, LAST, :] = h_s[one(k), :]
@@ -500,9 +501,9 @@
         def flux(k, arg):
             new, pe, u_w, v_e = arg
             um, vm = ums[k], vms[k]
-            c = 0.25 * ((vm + v_e) * (um + up_row(um, new[0], rowx)))
-            g = u_w + um
-            g = 0.25 * (g * g) + pe
+            c = (0.25 * (vm + v_e)) * (um + up_row(um, new[0], rowx))
+            g = 0.5 * (u_w + um)
+            g = g * g + pe
             c5 = c[:, :NC]
             return new, from_east(g)[:, :NC] - g[:, :NC], c5, c5 - from_west(c)[:, :NC]
 
@@ -510,8 +511,8 @@
             new, dx, c5, dc = arg
             u5, v5, pk = ums[k, :, :NC], vms[k, :, :NC], p[k]
             north = jnp.where(last, rnorth[2, one(k), :], pfirst[0, 2, one(k), :])
-            h = v5 + up_row(v5, new[1][:, :NC], row)
-            h = 0.25 * (h * h) + up_row(pk, north, row)
+            h = 0.5 * (v5 + up_row(v5, new[1][:, :NC], row))
+            h = h * h + up_row(pk, north, row)
             tu = only(k < kx, dx + (c5 - down_row(c5, cc[k], row)))
             tv = only(k < ky, (h - down_row(h, hh[k], row)) + dc)
             total[0] += tu
@@ -522,7 +523,7 @@
             hh[k] = h
             ums[k], vms[k] = new
 
-        skewed((edge, shift, flux, tend), GROUP)
+        skewed((edge, shift, flux, tend), GROUP_M)
         dzu, dzv = du[:], dv[:]
         fx[:] = -dzu * total[0]
         fy[:] = -dzv * total[1]
@@ -703,7 +704,7 @@
         lev = iota((LP, NC), 0).astype(F32)
         kx = kvs[LAST, :NC]
         cor = correction(vbs[LAST, :NC], rsouth[0, one(NL), :], kx, dvs[LAST, :NC])
-        vel = 0.5 * DT * only(lev < kx, rsouth[0] + cor)
+        vel = 0.5 * only(lev < kx, rsouth[0] + cor)
         ft = vel * (rsouth[1] + rown[0, 0])
         fs = vel * (rsouth[2] + rown[0, 1])
         for k in range(NL):
@@ -747,24 +748,25 @@
         halo, sums = arg
         ue = only(k < kx, jnp.concatenate([us[k], halo], axis=1) + cx)
         uo[k] = ue[:, :NC]
-        f = [(0.5 * DT) * ue * x for x in sums]
+        half = 0.5 * ue
+        f = [half * x for x in sums]
         return [(x - from_west(x))[:, :NC] for x in f]
 
     def store(k, div):
         ve = only(k < ky, vs[k] + cy)
         vo[k] = ve
-        hy = (0.5 * DT) * ve
+        hy = 0.5 * ve
         for i, (x, out, carry) in enumerate(fields):
             own = x[k]
             north = first[0, i, one(k), :]
             if last is not None:
                 north = jnp.where(last, rnorth[i, one(k), :], north)
             fy = hy * (own + up_row(own, north, row))
-            new = own - (div[i] + (fy - down_row(fy, carry[k], row)))
+            new = own - DT * (div[i] + (fy - down_row(fy, carry[k], row)))
             carry[k] = fy
             out[k] = only(k < cnt, new)
 
-    skewed((load, east, flux, store), GROUP)
+    skewed((load, east, flux, store), GROUP_F)
 
 
 def finish(us, vs, tm, sm, first, kmt, geo, ub, vb, su, sv, rw, re, rnorth, rsouth, state):

time: 102 us -> 101 us (level)
  no operation moved by 1% of the time
where the time goes in v9:
time: 101 us
  Pallas kernels  100 us (99%)
    pallas_call x1, Pallas kernels, momentum(): pl.pallas_call(momentum_kernel, grid=(NB + 1,), in_specs=[cube, cube, pac...  28.9 us
    pallas_call x1, Pallas kernels, tracers(): pl.pallas_call(functools.partial(tracer_kernel, sizes), grid=(NB // 2,),...  27.4 us
    pallas_call x1, Pallas kernels, subcycles(): pl.pallas_call(functools.partial(subcycle_kernel, sizes), in_specs=[vm] *...  22.7 us
    pallas_call x1, Pallas kernels, finish(): pl.pallas_call(finish_kernel, grid=(NB // 2,), in_specs=[block_major(lamb...  21.2 us

profile of v9, /device:TPU:0, one launch (start us, length us, event | category | flops | bytes accessed | tf_op | source)
XLA Modules:
  0.0 101.0 jit_solution(8354184172905439179)
XLA Ops:
  0.6 27.4 %tracers.1 = (f32[12,41,8,512]{3,2,1,0:T(8,128)S(1)}, f32[12,41,8,512]{3,2,1,0:T(8,128)S(1)}, f32[12,41,8,512]{3,2,1,0:T(8,128)}, f32[96,128]{1,0:T(8,128)S(1)},...) custom-call(f32[41,96,512]{2,1,0:T(8,128)} %t.1, ...), custom_call_target="tpu_custom_call" | custom-call | tf_op jit(solution)/shard_map/tracers/pallas_call | solution.py:399
  28.1 0.0 copy-start
  28.1 28.9 %momentum.1 = (f32[12,41,8,512]{3,2,1,0:T(8,128)S(1)}, f32[12,41,8,512]{3,2,1,0:T(8,128)}, f32[96,512]{1,0:T(8,128)S(1)}, f32[96,512]{1,0:T(8,128)S(1)}, f32[96,...) custom-call(f32[41,96,512]{2,1,0:T(8,128)} %u.1, f32[41,96,512]{2,1,0:T(8,128)} %v.1, ...), custom_call_target="tpu_custom_call" | custom-call | tf_op jit(solution)/shard_map/momentum/pallas_call | solution.py:570
  57.0 0.0 copy-done
  57.0 22.7 %subcycles.1 = (f32[96,512]{1,0:T(8,128)S(1)}, f32[96,512]{1,0:T(8,128)S(1)}, f32[96,512]{1,0:T(8,128)S(1)}, f32[104,640]{1,0:T(8,128)S(1)}, f32[104,640]{1,0:T(...) custom-call(f32[176,640]{1,0:T(8,128)S(1)} %get-tuple-element.62.eta, ...), custom_call_target="tpu_custom_call" | custom-call | tf_op jit(solution)/shard_map/subcycles/pallas_call | solution.py:683
  79.8 21.2 %finish.1 = (f32[96,512]{1,0:T(8,128)}, f32[96,512]{1,0:T(8,128)}, f32[96,512]{1,0:T(8,128)}, f32[41,96,512]{2,1,0:T(8,128)}, f32[41,96,512]{2,1,0:T(8,128)}, /*...) custom-call(f32[12,41,8,512]{3,2,1,0:T(8,128)S(1)} %get-tuple-element.56.refs_0_, ...), custom_call_target="tpu_custom_call" | custom-call | tf_op jit(solution)/shard_map/finish/pallas_call | solution.py:788
Async XLA Ops:
  28.1 28.9 %copy-start = (f32[36,2]{0,1:T(2,128)S(1)}, f32[36,2]{0,1:T(2,128)}, u32[]{:S(2)}) copy-start(f32[36,2]{0,1:T(2,128)} %param.19) | copy-start | bytes 868

commit v10 on v9

--- a/solution.py
+++ b/solution.py
@@ -119,15 +119,17 @@
         else:
             action()
 
-    def barrier(self):
+    def announce(self):
         ready = pltpu.get_barrier_semaphore()
         for drow in SIDES:
             for dcol in SIDES:
                 if drow or dcol:
                     self.when(drow, functools.partial(pl.semaphore_signal, ready, device_id=self.at(drow, dcol), device_id_type=pl.DeviceIdType.MESH))
+
+    def ready(self):
         per_row = len(SIDES)
         known = [self.inside(drow).astype(jnp.int32) for drow in SIDES if drow]
-        pl.semaphore_wait(ready, per_row - 1 + per_row * sum(known))
+        pl.semaphore_wait(pltpu.get_barrier_semaphore(), per_row - 1 + per_row * sum(known))
 
     def clear(self, plan):
         for _, dst, drow, _ in plan:
@@ -323,6 +325,8 @@
 
     @pl.when(b == 0)
     def _():
+        net.clear(first_plan)
+        net.announce()
         kf[:] = kmt[:].astype(F32)
         pack_strips((planes[:2], planes[2:4], planes[4:]), to_west, to_east)
         prn[:] = jnp.zeros(prn.shape, F32)
@@ -331,8 +335,7 @@
             for n, (lo, hi) in enumerate(((uf, ul), (vf, vl))):
                 prn[n, one(k), :] = hi[k, LAST, :]
                 prs[n, one(k), :] = lo[k, FIRST, :]
-        net.clear(first_plan)
-        net.barrier()
+        net.ready()
         net.start(head)
 
     for i in range(last):
@@ -586,8 +589,6 @@
 ):
     to_west, to_east, *strips, send_sem, recv_sem = rest
     net = Exchange(sizes, send_sem, recv_sem)
-    edge[:] = uke[:] + tke[:]
-    pack_strips(((fx, fy),), to_west, to_east)
     plan = strip_plan(to_west, to_east, strips) + row_plan((fx, fy), south, north)
     late = [
         (edge, fw, 0, 1),
@@ -597,9 +598,9 @@
         (trs.at[0], fnorth, -1, 0),
     ]
     net.clear(plan + late)
-    net.barrier()
-    plan, late = net.make(plan), net.make(late)
-    net.start(plan + late)
+    net.announce()
+    edge[:] = uke[:] + tke[:]
+    pack_strips(((fx, fy),), to_west, to_east)
     row = iota(WIDE, 0)
     zero = jnp.zeros(WIDE, F32)
     ub[:] = jnp.zeros(ub.shape, F32)
@@ -607,9 +608,13 @@
     eta[:] = eta_i[:]
     tu[:] = tu_i[:]
     tv[:] = tv_i[:]
+    plan, late = net.make(plan), net.make(late)
+    net.ready()
+    net.start(plan)
     cu[:] = DTB * (ku[:] * du[:])
     cv[:] = DTB * (kv[:] * dv[:])
     net.wait(plan)
+    net.start(late)
 
     def turn(i):
         return halo_pair(i, 0, strips)

time: 101 us -> 100 us (0.990)
  no operation moved by 1% of the time
where the time goes in v10:
time: 100 us
  Pallas kernels  99.5 us (100%)
    pallas_call x1, Pallas kernels, momentum(): pl.pallas_call(momentum_kernel, grid=(NB + 1,), in_specs=[cube, cube, pac...  28.9 us
    pallas_call x1, Pallas kernels, tracers(): pl.pallas_call(functools.partial(tracer_kernel, sizes), grid=(NB // 2,),...  27.2 us
    pallas_call x1, Pallas kernels, subcycles(): pl.pallas_call(functools.partial(subcycle_kernel, sizes), in_specs=[vm] *...  22.1 us
    pallas_call x1, Pallas kernels, finish(): pl.pallas_call(finish_kernel, grid=(NB // 2,), in_specs=[block_major(lamb...  21.2 us

profile of v10, /device:TPU:0, one launch (start us, length us, event | category | flops | bytes accessed | tf_op | source)
XLA Modules:
  0.0 100.1 jit_solution(2676858043461514903)
XLA Ops:
  0.6 27.2 %tracers.1 = (f32[12,41,8,512]{3,2,1,0:T(8,128)S(1)}, f32[12,41,8,512]{3,2,1,0:T(8,128)S(1)}, f32[12,41,8,512]{3,2,1,0:T(8,128)}, f32[96,128]{1,0:T(8,128)S(1)},...) custom-call(f32[41,96,512]{2,1,0:T(8,128)} %t.1, ...), custom_call_target="tpu_custom_call" | custom-call | tf_op jit(solution)/shard_map/tracers/pallas_call | solution.py:402
  27.9 0.0 copy-start
  27.9 28.9 %momentum.1 = (f32[12,41,8,512]{3,2,1,0:T(8,128)S(1)}, f32[12,41,8,512]{3,2,1,0:T(8,128)}, f32[96,512]{1,0:T(8,128)S(1)}, f32[96,512]{1,0:T(8,128)S(1)}, f32[96,...) custom-call(f32[41,96,512]{2,1,0:T(8,128)} %u.1, f32[41,96,512]{2,1,0:T(8,128)} %v.1, ...), custom_call_target="tpu_custom_call" | custom-call | tf_op jit(solution)/shard_map/momentum/pallas_call | solution.py:573
  56.8 0.0 copy-done
  56.8 22.1 %subcycles.1 = (f32[96,512]{1,0:T(8,128)S(1)}, f32[96,512]{1,0:T(8,128)S(1)}, f32[96,512]{1,0:T(8,128)S(1)}, f32[104,640]{1,0:T(8,128)S(1)}, f32[104,640]{1,0:T(...) custom-call(f32[176,640]{1,0:T(8,128)S(1)} %get-tuple-element.62.eta, ...), custom_call_target="tpu_custom_call" | custom-call | tf_op jit(solution)/shard_map/subcycles/pallas_call | solution.py:688
  78.9 21.2 %finish.1 = (f32[96,512]{1,0:T(8,128)}, f32[96,512]{1,0:T(8,128)}, f32[96,512]{1,0:T(8,128)}, f32[41,96,512]{2,1,0:T(8,128)}, f32[41,96,512]{2,1,0:T(8,128)}, /*...) custom-call(f32[12,41,8,512]{3,2,1,0:T(8,128)S(1)} %get-tuple-element.56.refs_0_, ...), custom_call_target="tpu_custom_call" | custom-call | tf_op jit(solution)/shard_map/finish/pallas_call | solution.py:793
Async XLA Ops:
  27.9 28.9 %copy-start = (f32[36,2]{0,1:T(2,128)S(1)}, f32[36,2]{0,1:T(2,128)}, u32[]{:S(2)}) copy-start(f32[36,2]{0,1:T(2,128)} %param.19) | copy-start | bytes 868

commit v11 on v10

--- a/solution.py
+++ b/solution.py
@@ -670,8 +670,8 @@
         if lo_bar <= i < hi_bar:
             vb[sl, :] = vb[sl, :] + w * x
 
-    for s in range(0, SUB, 8):
-        stage(s, min(s + 8, SUB), s // 8, ET - s // 8)
+    for s in range(HT):
+        stage(max(8 * s - 3, 0), min(8 * s + 5, SUB), s, ET - s)
     eta_o[:] = eta[HR : HR + NR, :NC]
     u_o[:] = tu[HR : HR + NR, :NC]
     v_o[:] = tv[HR : HR + NR, :NC]

time: 100 us -> 100 us (level)
  no operation moved by 1% of the time
where the time goes in v11:
time: 100 us; the launch traced here: 99.8 us
  Pallas kernels  99.1 us (99%)
    pallas_call x1, Pallas kernels, momentum(): pl.pallas_call(momentum_kernel, grid=(NB + 1,), in_specs=[cube, cube, pac...  28.9 us
    pallas_call x1, Pallas kernels, tracers(): pl.pallas_call(functools.partial(tracer_kernel, sizes), grid=(NB // 2,),...  27.2 us
    pallas_call x1, Pallas kernels, subcycles(): pl.pallas_call(functools.partial(subcycle_kernel, sizes), in_specs=[vm] *...  21.7 us
    pallas_call x1, Pallas kernels, finish(): pl.pallas_call(finish_kernel, grid=(NB // 2,), in_specs=[block_major(lamb...  21.2 us

profile of v11, /device:TPU:0, one launch (start us, length us, event | category | flops | bytes accessed | tf_op | source)
XLA Modules:
  0.0 99.8 jit_solution(11896850818733288782)
XLA Ops:
  0.6 27.2 %tracers.1 = (f32[12,41,8,512]{3,2,1,0:T(8,128)S(1)}, f32[12,41,8,512]{3,2,1,0:T(8,128)S(1)}, f32[12,41,8,512]{3,2,1,0:T(8,128)}, f32[96,128]{1,0:T(8,128)S(1)},...) custom-call(f32[41,96,512]{2,1,0:T(8,128)} %t.1, ...), custom_call_target="tpu_custom_call" | custom-call | tf_op jit(solution)/shard_map/tracers/pallas_call | solution.py:402
  27.9 0.0 copy-start
  27.9 28.9 %momentum.1 = (f32[12,41,8,512]{3,2,1,0:T(8,128)S(1)}, f32[12,41,8,512]{3,2,1,0:T(8,128)}, f32[96,512]{1,0:T(8,128)S(1)}, f32[96,512]{1,0:T(8,128)S(1)}, f32[96,...) custom-call(f32[41,96,512]{2,1,0:T(8,128)} %u.1, f32[41,96,512]{2,1,0:T(8,128)} %v.1, ...), custom_call_target="tpu_custom_call" | custom-call | tf_op jit(solution)/shard_map/momentum/pallas_call | solution.py:573
  56.8 0.0 copy-done
  56.8 21.7 %subcycles.1 = (f32[96,512]{1,0:T(8,128)S(1)}, f32[96,512]{1,0:T(8,128)S(1)}, f32[96,512]{1,0:T(8,128)S(1)}, f32[104,640]{1,0:T(8,128)S(1)}, f32[104,640]{1,0:T(...) custom-call(f32[176,640]{1,0:T(8,128)S(1)} %get-tuple-element.62.eta, ...), custom_call_target="tpu_custom_call" | custom-call | tf_op jit(solution)/shard_map/subcycles/pallas_call | solution.py:688
  78.5 21.2 %finish.1 = (f32[96,512]{1,0:T(8,128)}, f32[96,512]{1,0:T(8,128)}, f32[96,512]{1,0:T(8,128)}, f32[41,96,512]{2,1,0:T(8,128)}, f32[41,96,512]{2,1,0:T(8,128)}, /*...) custom-call(f32[12,41,8,512]{3,2,1,0:T(8,128)S(1)} %get-tuple-element.56.refs_0_, ...), custom_call_target="tpu_custom_call" | custom-call | tf_op jit(solution)/shard_map/finish/pallas_call | solution.py:793
Async XLA Ops:
  27.9 28.9 %copy-start = (f32[36,2]{0,1:T(2,128)S(1)}, f32[36,2]{0,1:T(2,128)}, u32[]{:S(2)}) copy-start(f32[36,2]{0,1:T(2,128)} %param.19) | copy-start | bytes 868
